TPU v7x, 32 devices: a whole 2x2x4 slice. The times are simulated.
32 devices in a mesh: section: 2 (over x), ctx: 2 (over y), dp: 8 (over z, core).
Axes of the slice: x: 2, y: 2, z: 4, core: 2. Of those that a mesh axis runs over, the one named last changes fastest.
Arguments:
- tokens: bfloat16 [2, 8, 256, 2048], P(None, 'dp', 'ctx'), may hold values from -6 to 6
- cotangent: bfloat16 [2, 8, 256, 2048], P(None, 'dp', 'ctx'), may hold values from -6 to 6
- segment_ids: int32 [2, 8, 256], P(None, 'dp'), may hold values from 0 to 7, never falling along the last dimension, each value on 1 to 192 neighbouring positions
- w_query: bfloat16 [2, 2048, 2048], P('section', 'dp'), may hold values from -0.125 to 0.125
- w_keyvalue: bfloat16 [2, 2048, 256], P('section', 'dp'), may hold values from -0.125 to 0.125
- w_out: bfloat16 [2, 2048, 2048], P('section', 'dp'), may hold values from -0.75 to 0.75
- w_up: bfloat16 [2, 2048, 8192], P('section', 'dp'), may hold values from -0.125 to 0.125
- w_down: bfloat16 [2, 8192, 2048], P('section', 'dp'), may hold values from -0.0625 to 0.0625
- ln_gains: bfloat16 [2, 2, 2048], P('section', None, 'dp'), may hold values from 0.25 to 1.75
- ln_biases: bfloat16 [2, 2, 2048], P('section', None, 'dp'), may hold values from -1.5 to 1.5
Outputs:
- section_outputs: bfloat16 [2, 2, 8, 256, 2048], P('section', None, 'dp', 'ctx')
- input_grads: bfloat16 [2, 2, 8, 256, 2048], P('section', None, 'dp', 'ctx')
- grad_query: float32 [2, 2048, 2048], P('section', 'dp')
- grad_keyvalue: float32 [2, 2048, 256], P('section', 'dp')
- grad_out: float32 [2, 2048, 2048], P('section', 'dp')
- grad_up: float32 [2, 2048, 8192], P('section', 'dp')
- grad_down: float32 [2, 8192, 2048], P('section', 'dp')
- grad_gains: float32 [2, 2, 2048], P('section', None, 'dp')
- grad_biases: float32 [2, 2, 2048], P('section', None, 'dp')
Inputs may be any that keep to these rules, and one draw needn't show every extreme that they name: `segment_ids`: in each sequence the ids start at 0 and never fall; 8 documents of 1 to 192 tokens, the longest exactly 192.
All inputs are finite; a program needn't handle non-finite values.
Results may differ from a plain program's by a relative error of at most 0.024.
Values may be sent and summed in bfloat16 or wider, within the bound.
A program may use at most 384 MiB of HBM per device.

v0:
```python
import jax
import jax.numpy as jnp
from jax import lax
from jax.sharding import PartitionSpec as P

HEADS = 16
HEAD = 128


epsilon = 1e-05
masked_score = -1000000000.0


def from_behind(x, axis, by):
    devices = lax.axis_size(axis)
    pairs = [(i, i + by) for i in range(devices) if 0 <= i + by < devices]
    return lax.ppermute(x, axis, pairs)


def layer_norm(values_in, gain_row, bias_row):
    mean_row = jnp.mean(values_in, axis=-1, keepdims=True)
    centered = values_in - mean_row
    variance = jnp.mean(centered * centered, axis=-1, keepdims=True)
    return centered * lax.rsqrt(variance + epsilon) * gain_row + bias_row


def dense(left, right):
    return jnp.dot(left, right, preferred_element_type=jnp.float32)


def dense_left(left, right):
    return lax.dot_general(
        left, right, (((0,), (0,)), ((), ())), preferred_element_type=jnp.float32
    )


def dense_right(left, right):
    return lax.dot_general(
        left, right, (((1,), (1,)), ((), ())), preferred_element_type=jnp.float32
    )


def select_tree(flag, first_tree, second_tree):
    return jax.tree.map(lambda left, right: jnp.where(flag, left, right), first_tree, second_tree)


def unpack(gathered):
    return (
        gathered[0][0],
        gathered[1][0],
        gathered[2][0],
        gathered[3][0],
        gathered[4][0],
        gathered[5][0].astype(jnp.float32),
        gathered[6][0].astype(jnp.float32),
    )


def allowed_keys(segments, cycle_place, cycle_size, tok_rows):
    offsets = jnp.arange(tok_rows, dtype=jnp.int32)
    query_pos = cycle_place * tok_rows + offsets
    query_seg = lax.dynamic_slice_in_dim(segments, cycle_place * tok_rows, tok_rows)
    blocks = []
    for cycle_step in range(cycle_size):
        source = cycle_place - cycle_step
        key_pos = source * tok_rows + offsets
        key_seg = lax.dynamic_slice_in_dim(segments, jnp.maximum(source, 0) * tok_rows, tok_rows)
        blocks.append(
            (source >= 0)
            & (key_pos[None, :] <= query_pos[:, None])
            & (key_seg[None, :] == query_seg[:, None])
        )
    return jnp.concatenate(blocks, axis=1)


def head_scores(query, keyvalue_all, allowed, tok_rows):
    head_rows = query.reshape(tok_rows * HEADS, HEAD)
    scores = dense_right(head_rows, keyvalue_all[:, :HEAD]) * HEAD ** (-0.5)
    scores = scores.reshape(tok_rows, HEADS, -1)
    scores = jnp.where(allowed[:, None, :], scores, masked_score)
    return (scores.reshape(tok_rows * HEADS, -1), head_rows)


def layer_forward(hidden, segments, weights, cycle_place, cycle_size):
    w_query, w_keyvalue, w_out, w_up, w_down, gains, biases = weights
    tok_rows = hidden.shape[0]
    normed = layer_norm(hidden, gains[0], biases[0]).astype(jnp.bfloat16)
    query = dense(normed, w_query).astype(jnp.bfloat16)
    keyvalue = dense(normed, w_keyvalue).astype(jnp.bfloat16)
    received = [keyvalue]
    moving = keyvalue
    moving = from_behind(moving, "ctx", 1)
    received.append(moving)
    keyvalue_all = jnp.concatenate(received, axis=0)
    allowed = allowed_keys(segments, cycle_place, cycle_size, tok_rows)
    scores, head_rows = head_scores(query, keyvalue_all, allowed, tok_rows)
    top_score = jnp.max(scores, axis=1, keepdims=True)
    log_total = top_score + jnp.log(jnp.sum(jnp.exp(scores - top_score), axis=1, keepdims=True))
    attn_probs = jnp.exp(scores - log_total).astype(jnp.bfloat16)
    mixed = (
        dense(attn_probs, keyvalue_all[:, HEAD:])
        .reshape(tok_rows, HEADS * HEAD)
        .astype(jnp.bfloat16)
    )
    after = hidden + dense(mixed, w_out)
    normed_two = layer_norm(after, gains[1], biases[1]).astype(jnp.bfloat16)
    up_rows = dense(normed_two, w_up)
    activated = jax.nn.gelu(up_rows, approximate=True).astype(jnp.bfloat16)
    result = after + dense(activated, w_down)
    kept = (
        hidden,
        normed,
        query,
        keyvalue_all,
        log_total,
        mixed,
        after,
        normed_two,
        up_rows,
        activated,
    )
    return (result, kept)


def layer_backward(grad_result, kept, segments, weights, cycle_place, cycle_size):
    w_query, w_keyvalue, w_out, w_up, w_down, gains, biases = weights
    hidden, normed, query, keyvalue_all, log_total, mixed, after, normed_two, up_rows, activated = (
        kept
    )
    tok_rows = hidden.shape[0]
    grad_low = grad_result.astype(jnp.bfloat16)
    grad_act = dense_right(grad_low, w_down)
    _, gelu_back = jax.vjp(lambda entries: jax.nn.gelu(entries, approximate=True), up_rows)
    grad_upper = gelu_back(grad_act)[0].astype(jnp.bfloat16)
    _, norm_back_two = jax.vjp(layer_norm, after, gains[1], biases[1])
    grad_after_norm, grad_gain_two, grad_bias_two = norm_back_two(dense_right(grad_upper, w_up))
    grad_after = grad_result + grad_after_norm
    grad_branch = grad_after.astype(jnp.bfloat16)
    grad_mixed = (
        dense_right(grad_branch, w_out).astype(jnp.bfloat16).reshape(tok_rows * HEADS, HEAD)
    )
    allowed = allowed_keys(segments, cycle_place, cycle_size, tok_rows)
    scores, head_rows = head_scores(query, keyvalue_all, allowed, tok_rows)
    attn_probs = jnp.exp(scores - log_total)
    grad_probs = dense_right(grad_mixed, keyvalue_all[:, HEAD:])
    grad_values = dense_left(attn_probs.astype(jnp.bfloat16), grad_mixed)
    inner = jnp.sum(attn_probs * grad_probs, axis=1, keepdims=True)
    grad_scores = (attn_probs * (grad_probs - inner)).astype(jnp.bfloat16)
    scale_factor = HEAD ** (-0.5)
    grad_queries = (
        (dense(grad_scores, keyvalue_all[:, :HEAD]) * scale_factor)
        .astype(jnp.bfloat16)
        .reshape(tok_rows, HEADS * HEAD)
    )
    grad_keys = dense_left(grad_scores, head_rows) * scale_factor
    grad_pieces = jnp.concatenate([grad_keys, grad_values], axis=1)
    carried = grad_pieces[(cycle_size - 1) * tok_rows :]
    carried = (
        from_behind(carried.astype(jnp.bfloat16), "ctx", -1).astype(carried.dtype)
        + grad_pieces[0:tok_rows]
    )
    grad_kv = carried.astype(jnp.bfloat16)
    grad_normed = dense_right(grad_queries, w_query) + dense_right(grad_kv, w_keyvalue)
    _, norm_back_one = jax.vjp(layer_norm, hidden, gains[0], biases[0])
    grad_hidden, grad_gain_one, grad_bias_one = norm_back_one(grad_normed)
    grad_input = grad_after + grad_hidden
    terms = (
        normed,
        grad_queries,
        grad_kv,
        mixed,
        grad_branch,
        normed_two,
        grad_upper,
        activated,
        grad_low,
        jnp.stack([grad_gain_one, grad_gain_two]),
        jnp.stack([grad_bias_one, grad_bias_two]),
    )
    return (grad_input, terms)


def body(
    tokens, cotangent, segment_ids, w_query, w_keyvalue, w_out, w_up, w_down, ln_gains, ln_biases
):
    section_index = lax.axis_index("section")
    cycle_place = lax.axis_index("ctx")
    cycle_size = lax.axis_size("ctx")
    micro_count = tokens.shape[0]
    tok_rows = tokens.shape[2]
    width = tokens.shape[3]
    early_section = section_index == 0
    late_section = section_index == 1
    segment_rows = segment_ids[:, 0]
    gathered = (
        lax.all_gather(w_query, "dp", axis=1, tiled=True),
        lax.all_gather(w_keyvalue, "dp", axis=1, tiled=True),
        lax.all_gather(w_out, "dp", axis=1, tiled=True),
        lax.all_gather(w_up, "dp", axis=1, tiled=True),
        lax.all_gather(w_down, "dp", axis=1, tiled=True),
        lax.all_gather(ln_gains, "dp", axis=2, tiled=True),
        lax.all_gather(ln_biases, "dp", axis=2, tiled=True),
    )
    forward_weights = unpack(gathered)
    incoming = jnp.zeros((tok_rows, width), jnp.bfloat16)
    outputs_list = []
    saved_list = []
    for clock_tick in range(micro_count + 1):
        own_rows = tokens[min(clock_tick, micro_count - 1), 0]
        entry = jnp.where(early_section, own_rows, incoming)
        segments = jnp.where(
            early_section,
            segment_rows[min(clock_tick, micro_count - 1)],
            segment_rows[max(clock_tick - 1, 0)],
        )
        result, kept = layer_forward(
            entry.astype(jnp.float32), segments, forward_weights, cycle_place, cycle_size
        )
        result_low = result.astype(jnp.bfloat16)
        outputs_list.append(result_low)
        saved_list.append(kept)
        if clock_tick < micro_count:
            incoming = from_behind(result_low, "section", 1)
    backward_weights = unpack(
        (
            lax.all_gather(w_query, "dp", axis=1, tiled=True),
            lax.all_gather(w_keyvalue, "dp", axis=1, tiled=True),
            lax.all_gather(w_out, "dp", axis=1, tiled=True),
            lax.all_gather(w_up, "dp", axis=1, tiled=True),
            lax.all_gather(w_down, "dp", axis=1, tiled=True),
            lax.all_gather(ln_gains, "dp", axis=2, tiled=True),
            lax.all_gather(ln_biases, "dp", axis=2, tiled=True),
        )
    )
    arriving = jnp.zeros((tok_rows, width), jnp.bfloat16)
    grads_list = []
    terms_list = []
    for clock_tick in range(micro_count + 1):
        own_rows = cotangent[min(clock_tick, micro_count - 1), 0]
        entry = jnp.where(late_section, own_rows, arriving)
        kept = select_tree(
            late_section,
            saved_list[min(clock_tick + 1, micro_count)],
            saved_list[max(clock_tick - 1, 0)],
        )
        segments = jnp.where(
            late_section,
            segment_rows[min(clock_tick, micro_count - 1)],
            segment_rows[max(clock_tick - 1, 0)],
        )
        grad_input, terms = layer_backward(
            entry.astype(jnp.float32), kept, segments, backward_weights, cycle_place, cycle_size
        )
        grad_input_low = grad_input.astype(jnp.bfloat16)
        grads_list.append(grad_input_low)
        terms_list.append(terms)
        if clock_tick < micro_count:
            arriving = from_behind(grad_input_low, "section", -1)
    section_rows = jnp.stack(
        [
            jnp.where(early_section, outputs_list[index_mb], outputs_list[index_mb + 1])
            for index_mb in range(micro_count)
        ]
    )
    grad_rows = jnp.stack(
        [
            jnp.where(late_section, grads_list[index_mb], grads_list[index_mb + 1])
            for index_mb in range(micro_count)
        ]
    )
    chosen = [
        select_tree(late_section, terms_list[index_mb], terms_list[index_mb + 1])
        for index_mb in range(micro_count)
    ]
    joined = [
        jnp.concatenate([item[index_term] for item in chosen], axis=0) for index_term in range(9)
    ]
    (
        normed_all,
        grad_queries_all,
        grad_kv_all,
        mixed_all,
        grad_branch_all,
        normed_two_all,
        grad_upper_all,
        activated_all,
        grad_low_all,
    ) = joined
    gain_terms = chosen[0][9]
    bias_terms = chosen[0][10]
    for item in chosen[1:]:
        gain_terms = gain_terms + item[9]
        bias_terms = bias_terms + item[10]
    attention_shards = (
        lax.psum_scatter(
            dense_left(normed_all, grad_queries_all).astype(jnp.bfloat16),
            "dp",
            scatter_dimension=0,
            tiled=True,
        ).astype(jnp.float32),
        lax.psum_scatter(
            dense_left(normed_all, grad_kv_all).astype(jnp.bfloat16),
            "dp",
            scatter_dimension=0,
            tiled=True,
        ).astype(jnp.float32),
        lax.psum_scatter(
            dense_left(mixed_all, grad_branch_all).astype(jnp.bfloat16),
            "dp",
            scatter_dimension=0,
            tiled=True,
        ).astype(jnp.float32),
        lax.psum_scatter(
            gain_terms.astype(jnp.bfloat16), "dp", scatter_dimension=1, tiled=True
        ).astype(jnp.float32),
        lax.psum_scatter(
            bias_terms.astype(jnp.bfloat16), "dp", scatter_dimension=1, tiled=True
        ).astype(jnp.float32),
    )
    up_shard = lax.psum_scatter(
        dense_left(normed_two_all, grad_upper_all).astype(jnp.bfloat16),
        "dp",
        scatter_dimension=0,
        tiled=True,
    ).astype(jnp.float32)
    down_shard = lax.psum_scatter(
        dense_left(activated_all, grad_low_all).astype(jnp.bfloat16),
        "dp",
        scatter_dimension=0,
        tiled=True,
    ).astype(jnp.float32)
    owner_shards = (
        attention_shards[0],
        attention_shards[1],
        attention_shards[2],
        attention_shards[3],
        attention_shards[4],
        up_shard,
        down_shard,
    )
    totals = (
        lax.psum(owner_shards[0].astype(jnp.bfloat16), "ctx").astype(jnp.float32),
        lax.psum(owner_shards[1].astype(jnp.bfloat16), "ctx").astype(jnp.float32),
        lax.psum(owner_shards[2].astype(jnp.bfloat16), "ctx").astype(jnp.float32),
        lax.psum(owner_shards[3].astype(jnp.bfloat16), "ctx").astype(jnp.float32),
        lax.psum(owner_shards[4].astype(jnp.bfloat16), "ctx").astype(jnp.float32),
        lax.psum(owner_shards[5].astype(jnp.bfloat16), "ctx").astype(jnp.float32),
        lax.psum(owner_shards[6].astype(jnp.bfloat16), "ctx").astype(jnp.float32),
    )
    section_outputs = section_rows[None, :, None]
    input_grads = grad_rows[None, :, None]
    return (
        section_outputs,
        input_grads,
        totals[0][None],
        totals[1][None],
        totals[2][None],
        totals[5][None],
        totals[6][None],
        totals[3][None],
        totals[4][None],
    )


def solution(mesh):
    in_specs = (
        P(None, "dp", "ctx", None),
        P(None, "dp", "ctx", None),
        P(None, "dp", None),
        P("section", "dp", None),
        P("section", "dp", None),
        P("section", "dp", None),
        P("section", "dp", None),
        P("section", "dp", None),
        P("section", None, "dp"),
        P("section", None, "dp"),
    )
    out_specs = (
        P("section", None, "dp", "ctx", None),
        P("section", None, "dp", "ctx", None),
        P("section", "dp", None),
        P("section", "dp", None),
        P("section", "dp", None),
        P("section", "dp", None),
        P("section", "dp", None),
        P("section", None, "dp"),
        P("section", None, "dp"),
    )
    return jax.shard_map(body, mesh=mesh, in_specs=in_specs, out_specs=out_specs, check_vma=False)
```

profile of v0, /device:TPU:0, one launch (start us, length us, event | category | flops | bytes accessed | tf_op | source)
XLA Modules:
  0.0 2357.7 jit_solution(9663379760722457876)
XLA Ops:
  40.2 77.7 %all-gather.6.cloned.1.call-done = bf16[1,2048,2048]{2,1,0:T(8,128)(2,1)} async-done(((bf16[1,256,2048]{2,1,0:T(8,128)(2,1)}), bf16[1,2048,2048]{2,1,0:T(8,128)(2,1)}) %all-gather.6.cloned.1.call-update) | async-done | bytes 8388624 | tf_op jit(solution)/shard_map/all_gather | solution.py:196
  125.3 74.8 %all-gather.10.cloned.1.call-done = bf16[1,2048,2048]{2,1,0:T(8,128)(2,1)} async-done(((bf16[1,256,2048]{2,1,0:T(8,128)(2,1)}), bf16[1,2048,2048]{2,1,0:T(8,128)(2,1)}) %all-gather.10.cloned.1.call-update) | async-done | bytes 8388624 | tf_op jit(solution)/shard_map/all_gather | solution.py:198
  205.1 283.5 %all-gather.12.cloned.1.call-done = bf16[1,2048,8192]{2,1,0:T(8,128)(2,1)} async-done(((bf16[1,256,8192]{2,1,0:T(8,128)(2,1)}), bf16[1,2048,8192]{2,1,0:T(8,128)(2,1)}) %all-gather.12.cloned.1.call-update) | async-done | bytes 33554448 | tf_op jit(solution)/shard_map/all_gather | solution.py:199
  488.6 19.9 fusion.22
  508.5 268.4 %all-gather.14.cloned.1.call-done = bf16[1,8192,2048]{2,1,0:T(8,128)(2,1)} async-done(((bf16[1,1024,2048]{2,1,0:T(8,128)(2,1)}), bf16[1,8192,2048]{2,1,0:T(8,128)(2,1)}) %all-gather.14.cloned.1.call-update) | async-done | bytes 33554448 | tf_op jit(solution)/shard_map/all_gather | solution.py:200
  776.9 17.1 fusion.162
  835.0 17.1 fusion.20
  852.1 19.3 fusion.54
  871.4 20.2 multiply_reduce_fusion.7
  911.5 17.8 fusion.159
  980.2 19.9 select_select_fusion.1
  1000.1 19.1 fusion.61
  1019.3 20.2 multiply_reduce_fusion.5
  1091.6 21.1 broadcast_select_fusion.2
  1112.7 19.8 multiply_reduce_fusion.3
  1184.3 16.6 convolution_convert_fusion.1
  1202.1 16.3 convolution_convert_fusion
  1228.9 50.5 %reduce-scatter.12.cloned.1.call-done = bf16[256,2048]{1,0:T(8,128)(2,1)} async-done(((bf16[2048,2048]{1,0:T(8,128)(2,1)}), bf16[256,2048]{1,0:T(8,128)(2,1)}) %reduce-scatter.12.cloned.1.call-update) | async-done | bytes 1048592 | tf_op jit(solution)/shard_map/reduce_scatter | solution.py:295
  1279.5 90.9 %reduce-scatter.16.cloned.1.call-done = bf16[256,2048]{1,0:T(8,128)(2,1)} async-done(((bf16[2048,2048]{1,0:T(8,128)(2,1)}), bf16[256,2048]{1,0:T(8,128)(2,1)}) %reduce-scatter.16.cloned.1.call-update) | async-done | bytes 1048592 | tf_op jit(solution)/shard_map/reduce_scatter | solution.py:307
  1370.4 326.3 %reduce-scatter.18.cloned.1.call-done = bf16[256,8192]{1,0:T(8,128)(2,1)} async-done(((bf16[2048,8192]{1,0:T(8,128)(2,1)}), bf16[256,8192]{1,0:T(8,128)(2,1)}) %reduce-scatter.18.cloned.1.call-update) | async-done | bytes 4194320 | tf_op jit(solution)/shard_map/reduce_scatter | solution.py:320
  1696.7 326.2 %reduce-scatter.20.cloned.1.call-done = bf16[1024,2048]{1,0:T(8,128)(2,1)} async-done(((bf16[8192,2048]{1,0:T(8,128)(2,1)}), bf16[1024,2048]{1,0:T(8,128)(2,1)}) %reduce-scatter.20.cloned.1.call-update) | async-done | bytes 4194320 | tf_op jit(solution)/shard_map/reduce_scatter | solution.py:326
  2024.2 17.0 fusion.168
  2056.4 31.4 %reduce-scatter.24.cloned.1.call-done = bf16[256,2]{1,0:T(8,128)(2,1)} async-done(((bf16[2048,2]{1,0:T(8,128)(2,1)}), bf16[256,2]{1,0:T(8,128)(2,1)}) %reduce-scatter.24.cloned.1.call-update) | async-done | bytes 1040
  2094.7 240.1 %all-reduce.4.cloned.1.call-done = (bf16[1,256,2048]{2,1,0:T(8,128)(2,1)}, bf16[1,256,256]{2,1,0:T(8,128)(2,1)}, bf16[1,256,2048]{2,1,0:T(8,128)(2,1)}, bf16[1,2...) async-done(((bf16[1,256,2048]{2,1,0:T(8,128)(2,1)}, bf16[1,256,256]{2,1,0:T(8,128)(2,1)}, bf16[1,256,2048]{2,1,0:T(8,128)(2,1)}, bf16[1,256,8192]{2,1,0:T(8,128)(2,1)}, ...) | async-done | bytes 10616848 | tf_op jit(solution)/shard_map/psum | solution.py:342
  (502 shorter events, 310.4 us)
Async XLA Ops:
  7.2 27.5 %all-gather.8.cloned.1.call-start = ((), (), s32[]{:S(2)}) async-start(), calls=%async_computation.8 | async-start | bytes 1179648 | tf_op jit(solution)/shard_map/all_gather | solution.py:197
  7.9 110.0 %all-gather.6.cloned.1.call-start = ((), (), s32[]{:S(2)}) async-start(), calls=%async_computation.7 | async-start | bytes 9437184 | tf_op jit(solution)/shard_map/all_gather | solution.py:196
  8.7 191.4 %all-gather.10.cloned.1.call-start = ((), (), s32[]{:S(2)}) async-start(), calls=%async_computation.9 | async-start | bytes 9437184 | tf_op jit(solution)/shard_map/all_gather | solution.py:198
  9.4 479.2 %all-gather.12.cloned.1.call-start = ((), (), s32[]{:S(2)}) async-start(), calls=%async_computation.10 | async-start | bytes 37748736 | tf_op jit(solution)/shard_map/all_gather | solution.py:199
  10.0 766.9 %all-gather.14.cloned.1.call-start = ((), (), s32[]{:S(2)}) async-start(), calls=%async_computation.11 | async-start | bytes 37748736 | tf_op jit(solution)/shard_map/all_gather | solution.py:200
  10.6 1218.3 %reduce-scatter.14.cloned.1.call-start = ((), (), s32[]{:S(2)}) async-start(), calls=%async_computation.13 | async-start | bytes 1179648 | tf_op jit(solution)/shard_map/reduce_scatter | solution.py:301
  34.7 798.1 %copy-start.66 = (f32[1,1,2048]{2,1,0:T(1,128)}, f32[1,1,2048]{2,1,0:T(1,128)S(1)}, u32[]{:S(2)}) copy-start(f32[1,1,2048]{2,1,0:T(1,128)S(1)} %get-tuple-element.131) | copy-start | bytes 24580
  36.4 86.7 %collective-permute-start = (bf16[128,256]{1,0:T(8,128)(2,1)S(1)}, bf16[128,256]{1,0:T(8,128)(2,1)S(1)}, u32[]{:S(2)}, u32[]{:S(2)}) collective-permute-start(bf16[128,256]{1,0:T(8,128)(2,1)S(1)} %convolution_convert_fusion.10), channel_id=1, source_target_pairs={{0,8},{1,9},{2,10},{3,11},{4,12},{5,13},{6,14},{7,15},{16,24},{17,... | collective-permute-start | bytes 196616 | tf_op jit(solution)/shard_map/ppermute | solution.py:17
  794.0 15.1 collective-permute-start.1
  810.2 13.0 collective-permute-start.2
  929.3 15.1 collective-permute-start.3
  935.8 7.9 collective-permute-start.5
  948.1 14.0 collective-permute-start.4
  960.7 16.2 collective-permute-start.6
  1063.1 7.9 collective-permute-start.7
  1075.1 14.3 collective-permute-start.8
  1151.9 6.2 collective-permute-start.9
  1159.7 119.7 %reduce-scatter.12.cloned.1.call-start = ((), (), s32[]{:S(2)}) async-start(), calls=%async_computation.12 | async-start | bytes 9437184 | tf_op jit(solution)/shard_map/reduce_scatter | solution.py:295
  1170.5 199.9 %reduce-scatter.16.cloned.1.call-start = ((), (), s32[]{:S(2)}) async-start(), calls=%async_computation.14 | async-start | bytes 9437184 | tf_op jit(solution)/shard_map/reduce_scatter | solution.py:307
  1181.0 515.6 %reduce-scatter.18.cloned.1.call-start = ((), (), s32[]{:S(2)}) async-start(), calls=%async_computation.15 | async-start | bytes 37748736 | tf_op jit(solution)/shard_map/reduce_scatter | solution.py:320
  1200.9 821.9 %reduce-scatter.20.cloned.1.call-start = ((), (), s32[]{:S(2)}) async-start(), calls=%async_computation.16 | async-start | bytes 37748736 | tf_op jit(solution)/shard_map/reduce_scatter | solution.py:326
  1218.5 837.0 %reduce-scatter.22.cloned.1.call-start = ((), (), s32[]{:S(2)}) async-start(), calls=%async_computation.17 | async-start | bytes 589824
  1227.6 860.1 %reduce-scatter.24.cloned.1.call-start = ((), (), s32[]{:S(2)}) async-start(), calls=%async_computation.18 | async-start | bytes 589824
  1228.9 1106.0 %all-reduce.4.cloned.1.call-start = ((), (), s32[]{:S(2)}) async-start(), calls=%async_computation.19 | async-start | bytes 21233664 | tf_op jit(solution)/shard_map/psum | solution.py:342
  (134 other events, 3920.5 us)
Sparse Core Ops, SparseCore 0:
  9.6 24.8 all-gather.7
  36.0 81.8 all-gather.5
  119.5 80.5 all-gather.9
  201.5 287.0 all-gather.11
  490.1 286.7 all-gather.13
  1159.8 28.9 reduce-scatter.13
  1191.7 87.6 reduce-scatter.11
  1282.3 88.0 reduce-scatter.15
  1372.7 323.8 reduce-scatter.17
  1698.9 323.9 reduce-scatter.19
  2025.7 29.7 reduce-scatter.21
  2058.1 29.5 reduce-scatter.23
  2090.6 244.2 all-reduce.3
where the time goes:
time: 2360 us
  waiting for transfers between devices  1810 us (77%)
  matrix products  377 us (16%)
  other arithmetic  56.4 us (2%)
  local copies, waits for them, and re-layouts  47.3 us (2%)
  starting transfers between devices  28.2 us (1%)
  blocking collectives  27.3 us (1%)
    reduce_scatter x1, waiting for transfers between devices, body(): lax.psum_scatter(dense_left(normed_two_all, grad_upper_all).astype(jnp.bf...  326 us
    reduce_scatter x1, waiting for transfers between devices, body(): lax.psum_scatter(dense_left(activated_all, grad_low_all).astype(jnp.bfloa...  326 us
    all_gather x1, waiting for transfers between devices, body(): lax.all_gather(w_up, 'dp', axis=1, tiled=True)  284 us
    all_gather x1, waiting for transfers between devices, body(): lax.all_gather(w_down, 'dp', axis=1, tiled=True)  268 us
    psum x1, waiting for transfers between devices, body(): lax.psum(owner_shards[0].astype(jnp.bfloat16), 'ctx').astype(jnp.float32)  240 us
    dot_general x24, matrix products, dense_right(): lax.dot_general(left, right, (((1,), (1,)), ((), ())), preferred_element_...  179 us
    dot_general x21, matrix products, dense(): return jnp.dot(left, right, preferred_element_type=jnp.float32)  146 us
    reduce_scatter x1, waiting for transfers between devices, body(): lax.psum_scatter(dense_left(mixed_all, grad_branch_all).astype(jnp.bfloat...  90.9 us
  transfers between devices with their start and end apart: 23, of which 15 were waited for; matrix products, arithmetic and copies ran while one was open for 8% of the time, Pallas kernels for 0%

commit v1 on v0

v1 whole, which is shorter than its diff:
```python
import jax
import jax.numpy as jnp
from jax import lax
from jax.sharding import PartitionSpec as P

HEADS = 16
HEAD = 128


epsilon = 1e-05
masked_score = -1000000000.0


def from_behind(x, axis, by):
    devices = lax.axis_size(axis)
    pairs = [(i, i + by) for i in range(devices) if 0 <= i + by < devices]
    return lax.ppermute(x, axis, pairs)


def layer_norm(values_in, gain_row, bias_row):
    mean_row = jnp.mean(values_in, axis=-1, keepdims=True)
    centered = values_in - mean_row
    variance = jnp.mean(centered * centered, axis=-1, keepdims=True)
    return centered * lax.rsqrt(variance + epsilon) * gain_row + bias_row


def dense(left, right):
    return jnp.dot(left, right, preferred_element_type=jnp.float32)


def dense_left(left, right):
    return lax.dot_general(
        left, right, (((0,), (0,)), ((), ())), preferred_element_type=jnp.float32
    )


def dense_right(left, right):
    return lax.dot_general(
        left, right, (((1,), (1,)), ((), ())), preferred_element_type=jnp.float32
    )


def allowed_keys(segments, cycle_place, cycle_size, tok_rows):
    offsets = jnp.arange(tok_rows, dtype=jnp.int32)
    query_pos = cycle_place * tok_rows + offsets
    query_seg = lax.dynamic_slice_in_dim(segments, cycle_place * tok_rows, tok_rows, axis=1)
    blocks = []
    for cycle_step in range(cycle_size):
        source = cycle_place - cycle_step
        key_pos = source * tok_rows + offsets
        key_seg = lax.dynamic_slice_in_dim(
            segments, jnp.maximum(source, 0) * tok_rows, tok_rows, axis=1
        )
        blocks.append(
            (source >= 0)
            & (key_pos[None, None, :] <= query_pos[None, :, None])
            & (key_seg[:, None, :] == query_seg[:, :, None])
        )
    return jnp.concatenate(blocks, axis=2)


def batched(left, right, left_dim, right_dim):
    return lax.dot_general(
        left, right, (((left_dim,), (right_dim,)), ((0,), (0,))), preferred_element_type=jnp.float32
    )


def head_scores(query, keyvalue_all, allowed):
    micro, rows, _ = allowed.shape
    head_rows = query.reshape(micro, rows * HEADS, HEAD)
    scores = batched(head_rows, keyvalue_all[:, :, :HEAD], 2, 2) * HEAD ** (-0.5)
    scores = scores.reshape(micro, rows, HEADS, -1)
    scores = jnp.where(allowed[:, :, None, :], scores, masked_score)
    return (scores.reshape(micro, rows * HEADS, -1), head_rows)


def layer_forward(hidden, segments, weights, micro, cycle_place, cycle_size):
    w_query, w_keyvalue, w_out, w_up, w_down, gains, biases = weights
    rows = hidden.shape[0] // micro
    normed = layer_norm(hidden, gains[0], biases[0]).astype(jnp.bfloat16)
    query = dense(normed, w_query).astype(jnp.bfloat16)
    keyvalue = dense(normed, w_keyvalue).astype(jnp.bfloat16)
    moving = from_behind(keyvalue, "ctx", 1)
    keyvalue_all = jnp.concatenate(
        [keyvalue.reshape(micro, rows, -1), moving.reshape(micro, rows, -1)], axis=1
    )
    allowed = allowed_keys(segments, cycle_place, cycle_size, rows)
    scores, _ = head_scores(query, keyvalue_all, allowed)
    top_score = jnp.max(scores, axis=2, keepdims=True)
    log_total = top_score + jnp.log(jnp.sum(jnp.exp(scores - top_score), axis=2, keepdims=True))
    attn_probs = jnp.exp(scores - log_total).astype(jnp.bfloat16)
    mixed = (
        batched(attn_probs, keyvalue_all[:, :, HEAD:], 2, 1)
        .reshape(micro * rows, HEADS * HEAD)
        .astype(jnp.bfloat16)
    )
    after = hidden + dense(mixed, w_out)
    normed_two = layer_norm(after, gains[1], biases[1]).astype(jnp.bfloat16)
    up_rows = dense(normed_two, w_up)
    activated = jax.nn.gelu(up_rows, approximate=True).astype(jnp.bfloat16)
    result = after + dense(activated, w_down)
    kept = (
        hidden,
        normed,
        query,
        keyvalue_all,
        log_total,
        mixed,
        after,
        normed_two,
        up_rows,
        activated,
    )
    return (result, kept)


def layer_backward(grad_result, kept, segments, weights, micro, cycle_place, cycle_size):
    w_query, w_keyvalue, w_out, w_up, w_down, gains, biases = weights
    hidden, normed, query, keyvalue_all, log_total, mixed, after, normed_two, up_rows, activated = (
        kept
    )
    rows = hidden.shape[0] // micro
    grad_low = grad_result.astype(jnp.bfloat16)
    grad_act = dense_right(grad_low, w_down)
    _, gelu_back = jax.vjp(lambda entries: jax.nn.gelu(entries, approximate=True), up_rows)
    grad_upper = gelu_back(grad_act)[0].astype(jnp.bfloat16)
    _, norm_back_two = jax.vjp(layer_norm, after, gains[1], biases[1])
    grad_after_norm, grad_gain_two, grad_bias_two = norm_back_two(dense_right(grad_upper, w_up))
    grad_after = grad_result + grad_after_norm
    grad_branch = grad_after.astype(jnp.bfloat16)
    grad_mixed = (
        dense_right(grad_branch, w_out).astype(jnp.bfloat16).reshape(micro, rows * HEADS, HEAD)
    )
    allowed = allowed_keys(segments, cycle_place, cycle_size, rows)
    scores, head_rows = head_scores(query, keyvalue_all, allowed)
    attn_probs = jnp.exp(scores - log_total)
    grad_probs = batched(grad_mixed, keyvalue_all[:, :, HEAD:], 2, 2)
    grad_values = batched(attn_probs.astype(jnp.bfloat16), grad_mixed, 1, 1)
    inner = jnp.sum(attn_probs * grad_probs, axis=2, keepdims=True)
    grad_scores = (attn_probs * (grad_probs - inner)).astype(jnp.bfloat16)
    scale_factor = HEAD ** (-0.5)
    grad_queries = (
        (batched(grad_scores, keyvalue_all[:, :, :HEAD], 2, 1) * scale_factor)
        .astype(jnp.bfloat16)
        .reshape(micro * rows, HEADS * HEAD)
    )
    grad_keys = batched(grad_scores, head_rows, 1, 1) * scale_factor
    grad_pieces = jnp.concatenate([grad_keys, grad_values], axis=2)
    carried = grad_pieces[:, (cycle_size - 1) * rows :]
    carried = (
        from_behind(carried.astype(jnp.bfloat16), "ctx", -1).astype(carried.dtype)
        + grad_pieces[:, 0:rows]
    )
    grad_kv = carried.astype(jnp.bfloat16).reshape(micro * rows, -1)
    grad_normed = dense_right(grad_queries, w_query) + dense_right(grad_kv, w_keyvalue)
    _, norm_back_one = jax.vjp(layer_norm, hidden, gains[0], biases[0])
    grad_hidden, grad_gain_one, grad_bias_one = norm_back_one(grad_normed)
    grad_input = grad_after + grad_hidden
    terms = (
        normed,
        grad_queries,
        grad_kv,
        mixed,
        grad_branch,
        normed_two,
        grad_upper,
        activated,
        grad_low,
        jnp.stack([grad_gain_one, grad_gain_two, grad_bias_one, grad_bias_two]),
    )
    return (grad_input, terms)


def body(
    tokens, cotangent, segment_ids, w_query, w_keyvalue, w_out, w_up, w_down, ln_gains, ln_biases
):
    section_index = lax.axis_index("section")
    cycle_place = lax.axis_index("ctx")
    cycle_size = lax.axis_size("ctx")
    micro = tokens.shape[0]
    width = tokens.shape[3]
    early = section_index == 0
    late = section_index == 1
    segments = segment_ids[:, 0]
    own_tokens = tokens[:, 0].reshape(-1, width)
    own_cotangent = cotangent[:, 0].reshape(-1, width)

    def spread(weight):
        half = weight.shape[1] // cycle_size
        part = lax.dynamic_slice_in_dim(weight, cycle_place * half, half, axis=1)
        return lax.all_gather(part, ("dp", "ctx"), axis=1, tiled=True)[0]

    scales = lax.all_gather(
        jnp.concatenate([ln_gains, ln_biases], axis=1), "dp", axis=2, tiled=True
    )[0].astype(jnp.float32)
    weights = (
        spread(w_query),
        lax.all_gather(w_keyvalue, "dp", axis=1, tiled=True)[0],
        spread(w_out),
        spread(w_up),
        spread(w_down),
        scales[0:2],
        scales[2:4],
    )
    result, kept_first = layer_forward(
        own_tokens.astype(jnp.float32), segments, weights, micro, cycle_place, cycle_size
    )
    first_low = result.astype(jnp.bfloat16)
    incoming = from_behind(first_low, "section", 1)
    result, kept_second = layer_forward(
        incoming.astype(jnp.float32), segments, weights, micro, cycle_place, cycle_size
    )
    second_low = result.astype(jnp.bfloat16)
    grad, terms_second = layer_backward(
        own_cotangent.astype(jnp.float32), kept_second, segments, weights, micro, cycle_place,
        cycle_size,
    )
    grad_second = grad.astype(jnp.bfloat16)
    arriving = from_behind(grad_second, "section", -1)
    grad, terms_first = layer_backward(
        arriving.astype(jnp.float32), kept_first, segments, weights, micro, cycle_place, cycle_size
    )
    grad_first = grad.astype(jnp.bfloat16)
    section_rows = jnp.where(early, first_low, second_low)
    grad_rows = jnp.where(early, grad_first, grad_second)
    (
        normed_all,
        grad_queries_all,
        grad_kv_all,
        mixed_all,
        grad_branch_all,
        normed_two_all,
        grad_upper_all,
        activated_all,
        grad_low_all,
        scale_terms,
    ) = [jnp.where(early, one, two) for one, two in zip(terms_first, terms_second)]

    def reduced(left, right):
        part = dense_left(left, right).astype(jnp.bfloat16)
        piece = lax.psum_scatter(part, ("dp", "ctx"), scatter_dimension=0, tiled=True)
        return lax.all_gather(piece, "ctx", axis=0, tiled=True).astype(jnp.float32)[None]

    grad_down = reduced(activated_all, grad_low_all)
    grad_up = reduced(normed_two_all, grad_upper_all)
    grad_out = reduced(mixed_all, grad_branch_all)
    grad_query = reduced(normed_all, grad_queries_all)
    grad_keyvalue = reduced(normed_all, grad_kv_all)
    scale_grads = lax.psum(
        lax.psum_scatter(
            scale_terms.astype(jnp.bfloat16), "dp", scatter_dimension=1, tiled=True
        ),
        "ctx",
    ).astype(jnp.float32)[None]
    local = (1, micro, 1, own_tokens.shape[0] // micro, width)
    return (
        section_rows.reshape(local),
        grad_rows.reshape(local),
        grad_query,
        grad_keyvalue,
        grad_out,
        grad_up,
        grad_down,
        scale_grads[:, 0:2],
        scale_grads[:, 2:4],
    )


def solution(mesh):
    in_specs = (
        P(None, "dp", "ctx", None),
        P(None, "dp", "ctx", None),
        P(None, "dp", None),
        P("section", "dp", None),
        P("section", "dp", None),
        P("section", "dp", None),
        P("section", "dp", None),
        P("section", "dp", None),
        P("section", None, "dp"),
        P("section", None, "dp"),
    )
    out_specs = (
        P("section", None, "dp", "ctx", None),
        P("section", None, "dp", "ctx", None),
        P("section", "dp", None),
        P("section", "dp", None),
        P("section", "dp", None),
        P("section", "dp", None),
        P("section", "dp", None),
        P("section", None, "dp"),
        P("section", None, "dp"),
    )
    return jax.shard_map(body, mesh=mesh, in_specs=in_specs, out_specs=out_specs, check_vma=False)
```

time: 2360 us -> 1940 us (0.82)
  waiting for transfers between devices: 1810 us -> 1510 us
  matrix products: 377 us -> 289 us
    psum x1 -> x0, waiting for transfers between devices: 240 us -> none  [body(): lax.psum(owner_shards[0].astype(jnp.bfloat16), 'ctx').astype(jnp.float32)]
    all_gather x5 -> x9, waiting for transfers between devices: 704 us -> 608 us  [the longest x4 465 us: spread(): return lax.all_gather(part, ('dp', 'ctx'), axis=1, tiled=True)[0]]
    dot_general x24 -> x10, matrix products: 179 us -> 110 us  [dense_right(): lax.dot_general(left, right, (((1,), (1,)), ((), ())), preferred_element_...]
    reduce_scatter x5, waiting for transfers between devices: 794 us -> 839 us  [reduced(): lax.psum_scatter(part, ('dp', 'ctx'), scatter_dimension=0, tiled=True)]
    dot_general x21 -> x10, matrix products: 146 us -> 103 us  [dense(): return jnp.dot(left, right, preferred_element_type=jnp.float32)]
    unnamed x15 -> x16, waiting for transfers between devices: 45.6 us -> 14.4 us
    ppermute x10 -> x6, waiting for transfers between devices: 21.8 us -> 47.5 us  [from_behind(): return lax.ppermute(x, axis, pairs)]
    dot_general x11 -> x5, matrix products: 51.5 us -> 53.6 us  [dense_left(): lax.dot_general(left, right, (((0,), (0,)), ((), ())), preferred_element_...]
  transfers between devices with their start and end apart: 23 -> 21, of which waited for: 15 -> 16; matrix products, arithmetic and copies ran while one was open for 8% -> 10% of each run, Pallas kernels for 0% -> 0%
where the time goes in v1:
time: 1940 us
  waiting for transfers between devices  1510 us (78%)
  matrix products  289 us (15%)
  other arithmetic  42.8 us (2%)
  local copies, waits for them, and re-layouts  38.9 us (2%)
  blocking collectives  24.6 us (1%)
    reduce_scatter x5, waiting for transfers between devices, reduced(): lax.psum_scatter(part, ('dp', 'ctx'), scatter_dimension=0, tiled=True)  839 us
    all_gather x4, waiting for transfers between devices, spread(): return lax.all_gather(part, ('dp', 'ctx'), axis=1, tiled=True)[0]  465 us
    all_gather x4, waiting for transfers between devices, reduced(): lax.all_gather(piece, 'ctx', axis=0, tiled=True).astype(jnp.float32)[None]  143 us
    dot_general x10, matrix products, dense_right(): lax.dot_general(left, right, (((1,), (1,)), ((), ())), preferred_element_...  110 us
    dot_general x10, matrix products, dense(): return jnp.dot(left, right, preferred_element_type=jnp.float32)  103 us
    dot_general x5, matrix products, dense_left(): lax.dot_general(left, right, (((0,), (0,)), ((), ())), preferred_element_...  53.6 us
    ppermute x6, waiting for transfers between devices, from_behind(): return lax.ppermute(x, axis, pairs)  47.5 us
  transfers between devices with their start and end apart: 21, of which 16 were waited for; matrix products, arithmetic and copies ran while one was open for 10% of the time, Pallas kernels for 0%

profile of v1, /device:TPU:0, one launch (start us, length us, event | category | flops | bytes accessed | tf_op | source)
XLA Modules:
  0.0 1935.3 jit_solution(17718069085464563189)
XLA Ops:
  42.3 69.2 %all-gather.10.cloned.1.call-done = bf16[1,2048,2048]{2,1,0:T(8,128)(2,1)} async-done(((bf16[1,128,2048]{2,1,0:T(8,128)(2,1)}), bf16[1,2048,2048]{2,1,0:T(8,128)(2,1)}) %all-gather.10.cloned.1.call-update) | async-done | bytes 8388624 | tf_op jit(solution)/shard_map/all_gather | solution.py:191
  125.1 62.1 %all-gather.14.cloned.1.call-done = bf16[1,2048,2048]{2,1,0:T(8,128)(2,1)} async-done(((bf16[1,128,2048]{2,1,0:T(8,128)(2,1)}), bf16[1,2048,2048]{2,1,0:T(8,128)(2,1)}) %all-gather.14.cloned.1.call-update) | async-done | bytes 8388624 | tf_op jit(solution)/shard_map/all_gather | solution.py:191
  193.8 171.9 %all-gather.16.cloned.1.call-done = bf16[1,2048,8192]{2,1,0:T(8,128)(2,1)} async-done(((bf16[1,128,8192]{2,1,0:T(8,128)(2,1)}), bf16[1,2048,8192]{2,1,0:T(8,128)(2,1)}) %all-gather.16.cloned.1.call-update) | async-done | bytes 33554448 | tf_op jit(solution)/shard_map/all_gather | solution.py:191
  365.7 17.9 fusion.14
  383.6 161.9 %all-gather.18.cloned.1.call-done = bf16[1,8192,2048]{2,1,0:T(8,128)(2,1)} async-done(((bf16[1,512,2048]{2,1,0:T(8,128)(2,1)}), bf16[1,8192,2048]{2,1,0:T(8,128)(2,1)}) %all-gather.18.cloned.1.call-update) | async-done | bytes 33554448 | tf_op jit(solution)/shard_map/all_gather | solution.py:191
  545.5 19.7 %fusion.77 = bf16[256,2048]{1,0:T(8,128)(2,1)} fusion(f32[256,2048]{1,0:T(8,128)S(1)} %get-tuple-element.74, bf16[1,8192,2048]{2,1,0:T(8,128)(2,1)} %all-gather.18.cloned.1.call-done, f32[256,8192]{1,0:T(8,128)} %fusion.14), kind=kOutput, calls=%fused_computation.94 | convolution fusion | flops 8609857536 | bytes 45088768 | tf_op jit(solution)/shard_map/dot_general | solution.py:28
  568.8 23.1 %collective-permute-done.1 = bf16[256,2048]{1,0:T(8,128)(2,1)S(1)} collective-permute-done((bf16[256,2048]{1,0:T(8,128)(2,1)}, bf16[256,2048]{1,0:T(8,128)(2,1)S(1)}, u32[]{:S(2)}, u32[]{:S(2)}) %collective-permute-start.1) | collective-permute-done | bytes 1048608 | tf_op jit(solution)/shard_map/ppermute | solution.py:17
  617.6 17.5 fusion.12
  635.1 21.8 %fusion.32 = bf16[256,8192]{1,0:T(8,128)(2,1)} fusion(f32[256,8192]{1,0:T(8,128)} %fusion.12, bf16[256,2048]{1,0:T(8,128)(2,1)} %bitcast.197, bf16[1,8192,2048]{2,1,0:T(8,128)(2,1)} %all-gather.18.cloned.1.call-done), kind=kOutput, calls=%fused_computation.36 | convolution fusion | flops 8631877632 | bytes 47185920 | tf_op jit(solution)/shard_map/dot_general | solution.py:38
  656.9 18.4 multiply_reduce_fusion.2
  714.0 24.4 %collective-permute-done.4 = bf16[256,2048]{1,0:T(8,128)(2,1)} collective-permute-done((bf16[256,2048]{1,0:T(8,128)(2,1)}, bf16[256,2048]{1,0:T(8,128)(2,1)}, u32[]{:S(2)}, u32[]{:S(2)}) %collective-permute-start.4) | collective-permute-done | bytes 1048608 | tf_op jit(solution)/shard_map/ppermute | solution.py:17
  738.4 20.8 %fusion.25 = bf16[256,8192]{1,0:T(8,128)(2,1)} fusion(f32[256,8192]{1,0:T(8,128)} %fusion.14, bf16[256,2048]{1,0:T(8,128)(2,1)} %collective-permute-done.4, bf16[1,8192,2048]{2,1,0:T(8,128)(2,1)} %all-gather.18.cloned.1.call-done), kind=kOutput, calls=%fused_computation.29 | convolution fusion | flops 8631877632 | bytes 47185920 | tf_op jit(solution)/shard_map/dot_general | solution.py:38
  759.2 18.2 multiply_reduce_fusion.3
  836.4 22.7 %convolution_convert_fusion = bf16[8192,2048]{1,0:T(8,128)(2,1)} fusion(pred[]{:T(512)S(6)} %eq.18, bf16[256,2048]{1,0:T(8,128)(2,1)} %collective-permute-done.4, bf16[256,2048]{1,0:T(8,128)(2,1)S(1)} %bitcast.198, f32[256,8192]{1,0:T(8,128)} %fusion.14, f32[256,8192]{1,0:T(8,128)} %fusion.12), kind=kOutput, calls=%fused_computation.16 | convolution fusion | flops 8647081984 | bytes 52428800 | tf_op jit(solution)/shard_map/dot_general | solution.py:32
  860.8 18.1 convolution_convert_fusion.1
  892.2 107.1 %reduce-scatter.9.cloned.1.call-done = bf16[128,2048]{1,0:T(8,128)(2,1)} async-done(((bf16[2048,2048]{1,0:T(8,128)(2,1)}), bf16[128,2048]{1,0:T(8,128)(2,1)}) %reduce-scatter.9.cloned.1.call-update) | async-done | bytes 524304 | tf_op jit(solution)/shard_map/reduce_scatter | solution.py:241
  999.4 334.4 %reduce-scatter.17.cloned.1.call-done = bf16[512,2048]{1,0:T(8,128)(2,1)} async-done(((bf16[8192,2048]{1,0:T(8,128)(2,1)}), bf16[512,2048]{1,0:T(8,128)(2,1)}) %reduce-scatter.17.cloned.1.call-update) | async-done | bytes 2097168 | tf_op jit(solution)/shard_map/reduce_scatter | solution.py:241
  1333.9 333.8 %reduce-scatter.15.cloned.1.call-done = bf16[128,8192]{1,0:T(8,128)(2,1)} async-done(((bf16[2048,8192]{1,0:T(8,128)(2,1)}), bf16[128,8192]{1,0:T(8,128)(2,1)}) %reduce-scatter.15.cloned.1.call-update) | async-done | bytes 2097168 | tf_op jit(solution)/shard_map/reduce_scatter | solution.py:241
  1667.7 19.6 %fusion.96 = bf16[256,2048]{1,0:T(8,128)(2,1)} fusion(bf16[256,2048]{1,0:T(8,128)(2,1)S(1)} %copy-done.95, f32[256,2048]{1,0:T(8,128)S(1)} %copy-done.9, bf16[1,8192,2048]{2,1,0:T(8,128)(2,1)} %all-gather.18.cloned.1.call-done, pred[]{:T(512)S(6)} %eq.18, f32[256,8192]{1,0:T(8,128)} %fusion.12), kind=kOutput, calls=%fused_computation.106 | convolution fusion | flops 8610381824 | bytes 46137344 | tf_op jit(solution)/shard_map/dot_general | solution.py:28
  1707.2 53.7 %reduce-scatter.11.cloned.1.call-done = bf16[128,256]{1,0:T(8,128)(2,1)} async-done(((bf16[2048,256]{1,0:T(8,128)(2,1)}), bf16[128,256]{1,0:T(8,128)(2,1)}) %reduce-scatter.11.cloned.1.call-update) | async-done | bytes 65552 | tf_op jit(solution)/shard_map/reduce_scatter | solution.py:241
  1766.8 15.9 all-gather.22.cloned.1.call-done
  1785.5 20.1 %all-gather.20.cloned.1.call-done = bf16[256,2048]{1,0:T(8,128)(2,1)} async-done(((bf16[128,2048]{1,0:T(8,128)(2,1)}), bf16[256,2048]{1,0:T(8,128)(2,1)}) %all-gather.20.cloned.1.call-update) | async-done | bytes 1048592 | tf_op jit(solution)/shard_map/all_gather | solution.py:242
  1808.3 55.4 %all-gather.26.cloned.1.call-done = bf16[1024,2048]{1,0:T(8,128)(2,1)} async-done(((bf16[512,2048]{1,0:T(8,128)(2,1)}), bf16[1024,2048]{1,0:T(8,128)(2,1)}) %all-gather.26.cloned.1.call-update) | async-done | bytes 4194320 | tf_op jit(solution)/shard_map/all_gather | solution.py:242
  1870.3 51.5 %all-gather.24.cloned.1.call-done = bf16[256,8192]{1,0:T(8,128)(2,1)} async-done(((bf16[128,8192]{1,0:T(8,128)(2,1)}), bf16[256,8192]{1,0:T(8,128)(2,1)}) %all-gather.24.cloned.1.call-update) | async-done | bytes 4194320 | tf_op jit(solution)/shard_map/all_gather | solution.py:242
  (340 shorter events, 240.5 us)
Async XLA Ops:
  7.2 29.8 %all-gather.12.cloned.1.call-start = ((), (), s32[]{:S(2)}) async-start(), calls=%async_computation.7 | async-start | bytes 1179648 | tf_op jit(solution)/shard_map/all_gather | solution.py:198
  7.9 103.6 %all-gather.10.cloned.1.call-start = ((), (), s32[]{:S(2)}) async-start(), calls=%async_computation.6 | async-start | bytes 8912896 | tf_op jit(solution)/shard_map/all_gather | solution.py:191
  9.3 178.0 %all-gather.14.cloned.1.call-start = ((), (), s32[]{:S(2)}) async-start(), calls=%async_computation.8 | async-start | bytes 8912896 | tf_op jit(solution)/shard_map/all_gather | solution.py:191
  11.2 354.5 %all-gather.16.cloned.1.call-start = ((), (), s32[]{:S(2)}) async-start(), calls=%async_computation.9 | async-start | bytes 35651584 | tf_op jit(solution)/shard_map/all_gather | solution.py:191
  14.4 531.1 %all-gather.18.cloned.1.call-start = ((), (), s32[]{:S(2)}) async-start(), calls=%async_computation.10 | async-start | bytes 35651584 | tf_op jit(solution)/shard_map/all_gather | solution.py:191
  17.7 874.5 %reduce-scatter.13.cloned.1.call-start = ((), (), s32[]{:S(2)}) async-start(), calls=%async_computation.14 | async-start | bytes 8912896 | tf_op jit(solution)/shard_map/reduce_scatter | solution.py:241
  36.5 581.1 %copy-start.48 = (f32[1,1,2048]{2,1,0:T(1,128)}, f32[1,1,2048]{2,1,0:T(1,128)S(1)}, u32[]{:S(2)}) copy-start(f32[1,1,2048]{2,1,0:T(1,128)S(1)} %get-tuple-element.55) | copy-start | bytes 24580
  38.7 81.1 %collective-permute-start = (bf16[256,256]{1,0:T(8,128)(2,1)S(1)}, bf16[256,256]{1,0:T(8,128)(2,1)S(1)}, u32[]{:S(2)}, u32[]{:S(2)}) collective-permute-start(bf16[256,256]{1,0:T(8,128)(2,1)S(1)} %convolution_convert_fusion.8), channel_id=1, source_target_pairs={{0,8},{1,9},{2,10},{3,11},{4,12},{5,13},{6,14},{7,15},{16,24},{17,... | collective-permute-start | bytes 393224 | tf_op jit(solution)/shard_map/ppermute | solution.py:17
  193.4 352.1 %copy-start.10 = (f32[256,2048]{1,0:T(8,128)}, f32[256,2048]{1,0:T(8,128)S(1)}, u32[]{:S(2)}) copy-start(f32[256,2048]{1,0:T(8,128)S(1)} %get-tuple-element.74) | copy-start | bytes 6291460
  565.2 26.7 %collective-permute-start.1 = (bf16[256,2048]{1,0:T(8,128)(2,1)}, bf16[256,2048]{1,0:T(8,128)(2,1)S(1)}, u32[]{:S(2)}, u32[]{:S(2)}) collective-permute-start(bf16[256,2048]{1,0:T(8,128)(2,1)} %fusion.77), channel_id=1, source_target_pairs={{0,16},{1,17},{2,18},{3,19},{4,20},{5,21},{6,22},{7,23},{8,24},{9,... | collective-permute-start | bytes 3145736 | tf_op jit(solution)/shard_map/ppermute | solution.py:17
  593.3 11.5 collective-permute-start.2
  696.2 8.5 collective-permute-start.3
  711.0 27.4 %collective-permute-start.4 = (bf16[256,2048]{1,0:T(8,128)(2,1)}, bf16[256,2048]{1,0:T(8,128)(2,1)}, u32[]{:S(2)}, u32[]{:S(2)}) collective-permute-start(bf16[256,2048]{1,0:T(8,128)(2,1)} %add_convert_fusion.2), channel_id=1, source_target_pairs={{16,0},{17,1},{18,2},{19,3},{20,4},{21,5},{22,6},{23,7},{24,8},{25... | collective-permute-start | bytes 3145736 | tf_op jit(solution)/shard_map/ppermute | solution.py:17
  788.6 210.8 %reduce-scatter.9.cloned.1.call-start = ((), (), s32[]{:S(2)}) async-start(), calls=%async_computation.11 | async-start | bytes 8912896 | tf_op jit(solution)/shard_map/reduce_scatter | solution.py:241
  811.5 8.7 collective-permute-start.5
  835.2 498.6 %reduce-scatter.17.cloned.1.call-start = ((), (), s32[]{:S(2)}) async-start(), calls=%async_computation.18 | async-start | bytes 35651584 | tf_op jit(solution)/shard_map/reduce_scatter | solution.py:241
  859.2 808.4 %reduce-scatter.15.cloned.1.call-start = ((), (), s32[]{:S(2)}) async-start(), calls=%async_computation.16 | async-start | bytes 35651584 | tf_op jit(solution)/shard_map/reduce_scatter | solution.py:241
  879.0 821.8 %reduce-scatter.19.cloned.1.call-start = ((), (), s32[]{:S(2)}) async-start(), calls=%async_computation.20 | async-start | bytes 589824
  880.8 880.1 %reduce-scatter.11.cloned.1.call-start = ((), (), s32[]{:S(2)}) async-start(), calls=%async_computation.13 | async-start | bytes 1114112 | tf_op jit(solution)/shard_map/reduce_scatter | solution.py:241
  882.4 900.3 %all-gather.22.cloned.1.call-start = ((), (), s32[]{:S(2)}) async-start(), calls=%async_computation.15 | async-start | bytes 1572864 | tf_op jit(solution)/shard_map/all_gather | solution.py:242
  892.2 913.3 %all-gather.20.cloned.1.call-start = ((), (), s32[]{:S(2)}) async-start(), calls=%async_computation.12 | async-start | bytes 1572864 | tf_op jit(solution)/shard_map/all_gather | solution.py:242
  999.4 864.3 %all-gather.26.cloned.1.call-start = ((), (), s32[]{:S(2)}) async-start(), calls=%async_computation.19 | async-start | bytes 6291456 | tf_op jit(solution)/shard_map/all_gather | solution.py:242
  1333.8 333.9 %copy-start.95 = (bf16[256,2048]{1,0:T(8,128)(2,1)S(1)}, bf16[256,2048]{1,0:T(8,128)(2,1)}, u32[]{:S(2)}) copy-start(bf16[256,2048]{1,0:T(8,128)(2,1)} %fusion.77) | copy-start | bytes 3145732
  1333.8 588.0 %all-gather.24.cloned.1.call-start = ((), (), s32[]{:S(2)}) async-start(), calls=%async_computation.17 | async-start | bytes 6291456 | tf_op jit(solution)/shard_map/all_gather | solution.py:242
  (93 other events, 1521.6 us)
Sparse Core Ops, SparseCore 0:
  9.6 24.9 all-gather.11
  37.4 74.1 all-gather.9
  114.3 72.8 all-gather.13
  189.2 176.4 all-gather.15
  367.7 177.7 all-gather.17
  788.7 103.4 reduce-scatter.12
  896.2 103.0 reduce-scatter.8
  1003.6 330.1 reduce-scatter.16
  1338.1 329.5 reduce-scatter.14
  1670.3 30.4 reduce-scatter.18
  1705.0 55.8 reduce-scatter.10
  1762.3 20.2 all-gather.21
  1784.2 21.2 all-gather.19
  1806.9 56.7 all-gather.25
  1865.1 56.7 all-gather.23

commit v2 on v1

--- a/solution.py
+++ b/solution.py
@@ -1,6 +1,11 @@
+import functools
+import math
+
 import jax
 import jax.numpy as jnp
 from jax import lax
+from jax.experimental import pallas as pl
+from jax.experimental.pallas import tpu as pltpu
 from jax.sharding import PartitionSpec as P
 
 HEADS = 16
@@ -9,12 +14,6 @@
 
 epsilon = 1e-05
 masked_score = -1000000000.0
-
-
-def from_behind(x, axis, by):
-    devices = lax.axis_size(axis)
-    pairs = [(i, i + by) for i in range(devices) if 0 <= i + by < devices]
-    return lax.ppermute(x, axis, pairs)
 
 
 def layer_norm(values_in, gain_row, bias_row):
@@ -38,6 +37,606 @@
     return lax.dot_general(
         left, right, (((1,), (1,)), ((), ())), preferred_element_type=jnp.float32
     )
+
+
+MESH = pl.DeviceIdType.MESH
+PARTS = 2
+
+
+def gelu(v):
+    inner = math.sqrt(2.0 / math.pi) * (v + 0.044715 * v * v * v)
+    return 0.5 * v * (1.0 + jnp.tanh(inner))
+
+
+def gelu_slope(v):
+    scale = math.sqrt(2.0 / math.pi)
+    tanh = jnp.tanh(scale * (v + 0.044715 * v * v * v))
+    return 0.5 * (1.0 + tanh) + 0.5 * v * (1.0 - tanh * tanh) * scale * (1.0 + 0.134145 * v * v)
+
+
+def tile_at(step, size):
+    return pl.ds(pl.multiple_of(step * size, size), size)
+
+
+def flat(block):
+    return block.reshape(block.shape[0] * block.shape[1], block.shape[2])
+
+
+def store_part(part, columns, values):
+    rows = part.shape[1]
+    part[0, :, columns] = values[:rows]
+    part[1, :, columns] = values[rows:]
+
+
+def masked_probs(query, key, mask):
+    scores = dense_right(query, key) * HEAD ** (-0.5)
+    scores = jnp.where(mask, scores, masked_score)
+    scores = jnp.exp(scores - jnp.max(scores, axis=1, keepdims=True))
+    return scores / jnp.sum(scores, axis=1, keepdims=True)
+
+
+def mask_of(seg_col, seg_row, at):
+    length = seg_row.shape[2]
+    place = lax.broadcasted_iota(jnp.int32, (length, length), 0)
+    source = lax.broadcasted_iota(jnp.int32, (length, length), 1)
+    return (source <= place) & (seg_col[at] == seg_row[at])
+
+
+def ffn_forward_at(at, gath, part, weights, ins, outs):
+    w_up, w_down = weights
+    up_out, act_out = outs
+    size = 256
+
+    def up_tile(step, carry):
+        columns = tile_at(step, size)
+        up_rows = dense(flat(gath[at]), w_up[:, columns])
+        up_out[at, :, columns] = up_rows.astype(jnp.bfloat16)
+        act_out[at, :, columns] = gelu(up_rows).astype(jnp.bfloat16)
+        return carry
+
+    lax.fori_loop(0, w_up.shape[1] // size, up_tile, 0)
+
+    def down_tile(step, carry):
+        columns = tile_at(step, size)
+        store_part(part, columns, dense(act_out[at], w_down[:, columns]))
+        return carry
+
+    lax.fori_loop(0, w_down.shape[1] // size, down_tile, 0)
+
+
+def ffn_backward_at(at, gath, part, weights, ins, outs):
+    w_up, w_down = weights
+    (up_in,) = ins
+    (upper_out,) = outs
+    size = 256
+
+    def act_tile(step, carry):
+        columns = tile_at(step, size)
+        grad_act = dense_right(flat(gath[at]), w_down[columns, :])
+        slope = gelu_slope(up_in[at, :, columns].astype(jnp.float32))
+        upper_out[at, :, columns] = (grad_act * slope).astype(jnp.bfloat16)
+        return carry
+
+    lax.fori_loop(0, w_down.shape[0] // size, act_tile, 0)
+
+    def back_tile(step, carry):
+        columns = tile_at(step, size)
+        store_part(part, columns, dense_right(upper_out[at], w_up[columns, :]))
+        return carry
+
+    lax.fori_loop(0, w_up.shape[0] // size, back_tile, 0)
+
+
+def attention_forward_at(at, gath, part, weights, ins, outs):
+    w_query, w_keyvalue, w_out = weights
+    seg_col, seg_row = ins
+    query_out, keyvalue_out, mixed_out = outs
+    size = 256
+    rows = flat(gath[at])
+    query_out[at] = dense(rows, w_query[...]).astype(jnp.bfloat16)
+    keyvalue_out[at] = dense(rows, w_keyvalue[...]).astype(jnp.bfloat16)
+    mask = mask_of(seg_col, seg_row, at)
+    for head in range(w_query.shape[1] // HEAD):
+        own = slice(head * HEAD, (head + 1) * HEAD)
+        probs = masked_probs(query_out[at, :, own], keyvalue_out[at, :, :HEAD], mask)
+        mixed = dense(probs.astype(jnp.bfloat16), keyvalue_out[at, :, HEAD:])
+        mixed_out[at, :, own] = mixed.astype(jnp.bfloat16)
+
+    def out_tile(step, carry):
+        columns = tile_at(step, size)
+        store_part(part, columns, dense(mixed_out[at], w_out[:, columns]))
+        return carry
+
+    lax.fori_loop(0, w_out.shape[1] // size, out_tile, 0)
+
+
+def attention_backward_at(at, gath, part, weights, ins, outs):
+    w_query, w_keyvalue, w_out = weights
+    seg_col, seg_row, query_in, keyvalue_in = ins
+    query_out, keyvalue_out = outs
+    size = 256
+    scale = HEAD ** (-0.5)
+    grad_mixed = dense_right(flat(gath[at]), w_out[...]).astype(jnp.bfloat16)
+    key = keyvalue_in[at, :, :HEAD]
+    value = keyvalue_in[at, :, HEAD:]
+    mask = mask_of(seg_col, seg_row, at)
+    grad_key = jnp.zeros(key.shape, jnp.float32)
+    grad_value = jnp.zeros(value.shape, jnp.float32)
+    for head in range(w_query.shape[1] // HEAD):
+        own = slice(head * HEAD, (head + 1) * HEAD)
+        query = query_in[at, :, own]
+        branch = grad_mixed[:, own]
+        probs = masked_probs(query, key, mask)
+        grad_probs = dense_right(branch, value)
+        inner = jnp.sum(probs * grad_probs, axis=1, keepdims=True)
+        grad_scores = (probs * (grad_probs - inner)).astype(jnp.bfloat16)
+        query_out[at, :, own] = (dense(grad_scores, key) * scale).astype(jnp.bfloat16)
+        grad_key = grad_key + dense_left(grad_scores, query)
+        grad_value = grad_value + dense_left(probs.astype(jnp.bfloat16), branch)
+    keyvalue_out[at, :, :HEAD] = (grad_key * scale).astype(jnp.bfloat16)
+    keyvalue_out[at, :, HEAD:] = grad_value.astype(jnp.bfloat16)
+
+    def back_tile(step, carry):
+        columns = tile_at(step, size)
+        store_part(
+            part,
+            columns,
+            dense_right(query_out[at], w_query[columns, :])
+            + dense_right(keyvalue_out[at], w_keyvalue[columns, :]),
+        )
+        return carry
+
+    lax.fori_loop(0, w_query.shape[0] // size, back_tile, 0)
+
+
+def pass_kernel(compute, n_weights, n_ins, n_outs, places, *refs):
+    refs = list(refs)
+    take = lambda count: [refs.pop(0) for _ in range(count)]
+    (x_ref,) = take(1)
+    early_weights = take(n_weights)
+    late_weights = take(n_weights)
+    ins = take(n_ins)
+    y_ref, gath = take(2)
+    outs = take(n_outs)
+    weights = take(n_weights)
+    part, partner_out, partner_in, total, line_out, from_left, from_right = take(7)
+    (
+        weight_sem, gather_right, gather_left, gather_partner, gather_line_in, gather_partner_in,
+        partner_send, partner_recv, right_send, right_recv, left_send, left_recv,
+    ) = take(12)
+
+    section = lax.axis_index("section")
+    me = lax.axis_index("dp")
+    z = me // 2
+    k = me % 2
+    last = places - 1
+    rows = x_ref.shape[0]
+    size = rows // PARTS
+    right = {"dp": me + 2}
+    left = {"dp": me - 2}
+    partner = {"dp": 2 * z + 1 - k}
+    has_left = z > 0
+    has_right = z < last
+
+    barrier = pltpu.get_barrier_semaphore()
+    pl.semaphore_signal(barrier, inc=1, device_id=partner, device_id_type=MESH)
+
+    @pl.when(has_left)
+    def _():
+        pl.semaphore_signal(barrier, inc=1, device_id=left, device_id_type=MESH)
+
+    @pl.when(has_right)
+    def _():
+        pl.semaphore_signal(barrier, inc=1, device_id=right, device_id_type=MESH)
+
+    for index in range(n_weights):
+
+        @pl.when(section == 0)
+        def _():
+            pltpu.make_async_copy(early_weights[index], weights[index], weight_sem.at[index]).start()
+
+        @pl.when(section != 0)
+        def _():
+            pltpu.make_async_copy(late_weights[index], weights[index], weight_sem.at[index]).start()
+
+    peers = 1 + jnp.where(has_left, 1, 0) + jnp.where(has_right, 1, 0)
+    pl.semaphore_wait(barrier, peers)
+
+    def cut(index):
+        return pl.ds(index * size, size)
+
+    def to_right(block, index, source):
+        return pltpu.make_async_remote_copy(
+            source, gath.at[block, k, cut(index)], gather_right.at[block, index],
+            gather_line_in.at[block, index], device_id=right, device_id_type=MESH,
+        )
+
+    def to_left(block, index, source):
+        return pltpu.make_async_remote_copy(
+            source, gath.at[block, k, cut(index)], gather_left.at[block, index],
+            gather_line_in.at[block, index], device_id=left, device_id_type=MESH,
+        )
+
+    def to_partner(block, source):
+        return pltpu.make_async_remote_copy(
+            source, gath.at[block, k], gather_partner.at[block],
+            gather_partner_in.at[block], device_id=partner, device_id_type=MESH,
+        )
+
+    def sum_to_partner(block):
+        return pltpu.make_async_remote_copy(
+            partner_out.at[block], partner_in.at[block], partner_send.at[block],
+            partner_recv.at[block], device_id=partner, device_id_type=MESH,
+        )
+
+    def sum_to_right(block, index):
+        return pltpu.make_async_remote_copy(
+            line_out.at[block, cut(index)], from_left.at[block, cut(index)],
+            right_send.at[block, index], right_recv.at[block, index],
+            device_id=right, device_id_type=MESH,
+        )
+
+    def sum_to_left(block, index):
+        return pltpu.make_async_remote_copy(
+            line_out.at[block, cut(index)], from_right.at[block, cut(index)],
+            left_send.at[block, index], left_recv.at[block, index],
+            device_id=left, device_id_type=MESH,
+        )
+
+    for index in range(PARTS):
+
+        @pl.when(has_right)
+        def _():
+            to_right(z, index, x_ref.at[cut(index)]).start()
+
+        @pl.when(has_left)
+        def _():
+            to_left(z, index, x_ref.at[cut(index)]).start()
+
+    to_partner(z, x_ref).start()
+    gath[z, k] = x_ref[...]
+
+    at_end = (z == 0) | (z == last)
+    low_half = z < places // 2
+
+    def step(i, carry):
+        inner_block = jnp.where(i == 0, 1, jnp.where(i == 1, 0, i))
+        low_block = jnp.where(z == 0, i, inner_block)
+        high_block = last - jnp.where(z == last, i, inner_block)
+        block = jnp.where(low_half, low_block, high_block)
+        wave = jnp.where(at_end, i, jnp.where(i == 1, 1, jnp.where(i == 3, 2, 0)))
+        from_low = z - wave
+        from_high = z + wave
+
+        @pl.when((wave > 0) & (from_low >= 0))
+        def _():
+            for index in range(PARTS):
+                to_right(from_low, index, gath.at[from_low, k, cut(index)]).wait_recv()
+
+                @pl.when(has_right)
+                def _():
+                    to_right(from_low, index, gath.at[from_low, k, cut(index)]).start()
+
+            to_partner(from_low, gath.at[from_low, k]).start()
+
+        @pl.when((wave > 0) & (from_high <= last))
+        def _():
+            for index in range(PARTS):
+                to_left(from_high, index, gath.at[from_high, k, cut(index)]).wait_recv()
+
+                @pl.when(has_left)
+                def _():
+                    to_left(from_high, index, gath.at[from_high, k, cut(index)]).start()
+
+            to_partner(from_high, gath.at[from_high, k]).start()
+
+        pltpu.make_async_remote_copy(
+            gath.at[block, 1 - k], gath.at[block, 1 - k], gather_partner.at[block],
+            gather_partner_in.at[block], device_id=partner, device_id_type=MESH,
+        ).wait_recv()
+
+        @pl.when(i == 0)
+        def _():
+            for index in range(n_weights):
+                pltpu.make_async_copy(
+                    early_weights[index], weights[index], weight_sem.at[index]
+                ).wait()
+
+        compute(block, gath, part, weights, ins, outs)
+        partner_out[block] = part[1 - k].astype(jnp.bfloat16)
+        sum_to_partner(block).start()
+        sum_to_partner(block).wait_recv()
+        total[block] = part[k] + partner_in[block].astype(jnp.float32)
+
+        @pl.when((z == 0) & (block > 0))
+        def _():
+            line_out[block] = total[block].astype(jnp.bfloat16)
+            for index in range(PARTS):
+                sum_to_right(block, index).start()
+
+        @pl.when((z == last) & (block < last))
+        def _():
+            line_out[block] = total[block].astype(jnp.bfloat16)
+            for index in range(PARTS):
+                sum_to_left(block, index).start()
+
+        return carry
+
+    lax.fori_loop(0, places, step, 0)
+
+    n_left = jnp.where(has_left, places - z, 0)
+    n_right = jnp.where(has_right, z + 1, 0)
+    n_first = jnp.where(low_half, n_left, n_right)
+
+    def finish(i, carry):
+        in_first = i < n_first
+        turn = jnp.where(in_first, i, i - n_first)
+        is_left = in_first == low_half
+        block = jnp.where(is_left, z + turn, z - turn)
+
+        @pl.when(is_left)
+        def _():
+            for index in range(PARTS):
+                sum_to_right(block, index).wait_recv()
+                total[block, cut(index)] += from_left[block, cut(index)].astype(jnp.float32)
+
+                @pl.when(block > z)
+                def _():
+                    line_out[block, cut(index)] = total[block, cut(index)].astype(jnp.bfloat16)
+                    sum_to_right(block, index).start()
+
+        @pl.when(jnp.logical_not(is_left))
+        def _():
+            for index in range(PARTS):
+                sum_to_left(block, index).wait_recv()
+                total[block, cut(index)] += from_right[block, cut(index)].astype(jnp.float32)
+
+                @pl.when(block < z)
+                def _():
+                    line_out[block, cut(index)] = total[block, cut(index)].astype(jnp.bfloat16)
+                    sum_to_left(block, index).start()
+
+        return carry
+
+    lax.fori_loop(0, n_left + n_right, finish, 0)
+    y_ref[...] = total[z]
+
+    def drain(block, carry):
+        to_partner(block, gath.at[block, k]).wait_send()
+        sum_to_partner(block).wait_send()
+        for index in range(PARTS):
+
+            @pl.when((block <= z) & has_right)
+            def _():
+                to_right(block, index, gath.at[block, k, cut(index)]).wait_send()
+
+            @pl.when((block >= z) & has_left)
+            def _():
+                to_left(block, index, gath.at[block, k, cut(index)]).wait_send()
+
+            @pl.when(block > z)
+            def _():
+                sum_to_right(block, index).wait_send()
+
+            @pl.when(block < z)
+            def _():
+                sum_to_left(block, index).wait_send()
+
+        return carry
+
+    lax.fori_loop(0, places, drain, 0)
+
+
+def tensor_pass(compute, name, ident, x, early_weights, late_weights, ins, out_widths):
+    rows, width = x.shape
+    places = lax.axis_size("dp") // 2
+    vmem = pl.BlockSpec(memory_space=pltpu.VMEM)
+    hbm = pl.BlockSpec(memory_space=pl.ANY)
+    count = len(early_weights)
+    dma = pltpu.SemaphoreType.DMA
+    kernel = functools.partial(pass_kernel, compute, count, len(ins), len(out_widths), places)
+    return pl.pallas_call(
+        kernel,
+        name=name,
+        out_shape=[
+            jax.ShapeDtypeStruct((rows, width), jnp.float32),
+            jax.ShapeDtypeStruct((places, 2, rows, width), jnp.bfloat16),
+        ]
+        + [jax.ShapeDtypeStruct((places, 2 * rows, out), jnp.bfloat16) for out in out_widths],
+        in_specs=[vmem] + [hbm] * (2 * count) + [vmem] * len(ins),
+        out_specs=[vmem] * (2 + len(out_widths)),
+        scratch_shapes=[pltpu.VMEM(weight.shape, weight.dtype) for weight in early_weights]
+        + [
+            pltpu.VMEM((2, rows, width), jnp.float32),
+            pltpu.VMEM((places, rows, width), jnp.bfloat16),
+            pltpu.VMEM((places, rows, width), jnp.bfloat16),
+            pltpu.VMEM((places, rows, width), jnp.float32),
+            pltpu.VMEM((places, rows, width), jnp.bfloat16),
+            pltpu.VMEM((places, rows, width), jnp.bfloat16),
+            pltpu.VMEM((places, rows, width), jnp.bfloat16),
+            dma((count,)),
+            dma((places, PARTS)),
+            dma((places, PARTS)),
+            dma((places,)),
+            dma((places, PARTS)),
+            dma((places,)),
+            dma((places,)),
+            dma((places,)),
+            dma((places, PARTS)),
+            dma((places, PARTS)),
+            dma((places, PARTS)),
+            dma((places, PARTS)),
+        ],
+        compiler_params=pltpu.CompilerParams(
+            collective_id=ident, has_side_effects=True, vmem_limit_bytes=60 * 1024 * 1024
+        ),
+    )(x, *early_weights, *late_weights, *ins)
+
+
+def swapped(size, places):
+    pairs = []
+    for ctx in range(2):
+        for at in range(size):
+            z, k = at // 2, at % 2
+            pairs.append((ctx * size + at, k * size + 2 * z + ctx))
+    return pairs
+
+
+def regroup(x):
+    size = lax.axis_size("dp")
+    return lax.ppermute(x, ("ctx", "dp"), swapped(size, size // 2))
+
+
+def regroup_across(x):
+    size = lax.axis_size("dp")
+    half = 2 * size
+    pairs = swapped(size, size // 2)
+    across = [(a, b + half) for a, b in pairs] + [(a + half, b) for a, b in pairs]
+    return lax.ppermute(x, ("section", "ctx", "dp"), across)
+
+
+def exchange(x):
+    return lax.ppermute(x, "section", [(0, 1), (1, 0)])
+
+
+def spread_body(
+    tokens, cotangent, segment_ids, w_query, w_keyvalue, w_out, w_up, w_down, ln_gains, ln_biases
+):
+    section = lax.axis_index("section")
+    ctx = lax.axis_index("ctx")
+    size = lax.axis_size("dp")
+    places = size // 2
+    early = section == 0
+    width = tokens.shape[3]
+    length = segment_ids.shape[2]
+    tall = (places * tokens.shape[2] * 2, -1)
+
+    def own_micro(x):
+        return lax.dynamic_index_in_dim(x, section, 0, keepdims=False)[0]
+
+    hidden = regroup(own_micro(tokens)).astype(jnp.float32)
+    segments = lax.all_gather(own_micro(segment_ids), "dp").reshape(places, 2, length)
+    segments = lax.dynamic_index_in_dim(segments, ctx, 1, keepdims=False)
+    segs = [segments[:, :, None], segments[:, None, :]]
+    scales = lax.all_gather(
+        jnp.concatenate([ln_gains[0], ln_biases[0]], axis=0), ("section", "dp")
+    ).reshape(2, size, 4, -1)
+    scales = scales.transpose(0, 2, 1, 3).reshape(2, 4, width).astype(jnp.float32)
+    keyvalue = lax.all_gather(w_keyvalue[0], ("section", "dp"), axis=0, tiled=True)
+    keyvalue = keyvalue.reshape(2, width, -1)
+    query = lax.all_to_all(w_query[0], "dp", 1, 0, tiled=True)
+    out = w_out[0]
+    up = lax.all_to_all(w_up[0], "dp", 1, 0, tiled=True)
+    down = w_down[0]
+    query_far, out_far = exchange(query), exchange(out)
+    up_far, down_far = exchange(up), exchange(down)
+    attention_weights = [
+        ([query, keyvalue[0], out], [query_far, keyvalue[0], out_far]),
+        ([query_far, keyvalue[1], out_far], [query, keyvalue[1], out]),
+    ]
+    ffn_weights = [([up, down], [up_far, down_far]), ([up_far, down_far], [up, down])]
+    head_width = query.shape[1]
+    unit_width = up.shape[1]
+
+    def forward(layer, hidden):
+        normed = layer_norm(hidden, scales[layer, 0], scales[layer, 2]).astype(jnp.bfloat16)
+        y, normed_all, q, kv, mixed = tensor_pass(
+            attention_forward_at, "attention_forward", 0, normed, *attention_weights[layer], segs,
+            [head_width, keyvalue.shape[2], head_width],
+        )
+        after = hidden + y
+        normed_two = layer_norm(after, scales[layer, 1], scales[layer, 3]).astype(jnp.bfloat16)
+        y, normed_two_all, up_rows, activated = tensor_pass(
+            ffn_forward_at, "ffn_forward", 1, normed_two, *ffn_weights[layer], [],
+            [unit_width, unit_width],
+        )
+        result = (after + y).astype(jnp.bfloat16)
+        return result, (hidden, normed_all, q, kv, mixed, after, normed_two_all, up_rows, activated)
+
+    def backward(layer, grad_low, kept):
+        hidden, normed_all, q, kv, mixed, after, normed_two_all, up_rows, activated = kept
+        y, grad_low_all, grad_upper = tensor_pass(
+            ffn_backward_at, "ffn_backward", 2, grad_low, *ffn_weights[layer], [up_rows],
+            [unit_width],
+        )
+        _, norm_back = jax.vjp(layer_norm, after, scales[layer, 1], scales[layer, 3])
+        grad_norm, gain_two, bias_two = norm_back(y)
+        grad_after = grad_low.astype(jnp.float32) + grad_norm
+        y, grad_branch_all, grad_query, grad_kv = tensor_pass(
+            attention_backward_at, "attention_backward", 3, grad_after.astype(jnp.bfloat16),
+            *attention_weights[layer], segs + [q, kv], [head_width, keyvalue.shape[2]],
+        )
+        _, norm_back = jax.vjp(layer_norm, hidden, scales[layer, 0], scales[layer, 2])
+        grad_norm, gain_one, bias_one = norm_back(y)
+        grad_input = (grad_after + grad_norm).astype(jnp.bfloat16)
+
+        def product(left, right):
+            return dense_left(left.reshape(tall), right.reshape(tall)).astype(jnp.bfloat16)
+
+        weight_grads = (
+            product(activated, grad_low_all),
+            product(normed_two_all, grad_upper),
+            product(mixed, grad_branch_all),
+            product(normed_all, grad_query),
+            product(normed_all, grad_kv),
+        )
+        return grad_input, weight_grads, jnp.stack([gain_one, gain_two, bias_one, bias_two])
+
+    first, kept_first = forward(0, hidden)
+    second, kept_second = forward(1, first.astype(jnp.float32))
+    grad_low = regroup(own_micro(cotangent))
+    grad_second, weights_second, scales_second = backward(1, grad_low, kept_second)
+    grad_first, weights_first, scales_first = backward(0, grad_second, kept_first)
+
+    def both_rows(one, two):
+        near = regroup(jnp.where(early, one, two))
+        far = regroup_across(jnp.where(early, two, one))
+        return jnp.stack([jnp.where(early, near, far), jnp.where(early, far, near)])[None, :, None]
+
+    def total(grad):
+        return lax.psum(grad, ("section", "ctx"))
+
+    def own(one, two):
+        return jnp.where(early, one, two)
+
+    def summed(index):
+        return own(total(weights_first[index]), total(weights_second[index]))
+
+    down_grad, up_grad, out_grad, query_grad = [summed(index) for index in range(4)]
+    up_grad = lax.all_to_all(up_grad, "dp", 0, 1, tiled=True)
+    query_grad = lax.all_to_all(query_grad, "dp", 0, 1, tiled=True)
+    keyvalue_grad = own(
+        *[
+            total(lax.psum_scatter(pair[4], "dp", scatter_dimension=0, tiled=True))
+            for pair in (weights_first, weights_second)
+        ]
+    )
+    scale_grads = lax.psum(jnp.stack([scales_first, scales_second]), ("section", "ctx", "dp"))
+    scale_grads = lax.dynamic_index_in_dim(scale_grads, section, 0, keepdims=True)
+    scale_grads = lax.dynamic_slice_in_dim(
+        scale_grads, lax.axis_index("dp") * ln_gains.shape[2], ln_gains.shape[2], axis=2
+    )
+
+    def given(grad):
+        return grad.astype(jnp.float32)[None]
+
+    return (
+        both_rows(first, second),
+        both_rows(grad_first, grad_second),
+        given(query_grad),
+        given(keyvalue_grad),
+        given(out_grad),
+        given(up_grad),
+        given(down_grad),
+        scale_grads[:, 0:2],
+        scale_grads[:, 2:4],
+    )
+
+
+def from_behind(x, axis, by):
+    devices = lax.axis_size(axis)
+    pairs = [(i, i + by) for i in range(devices) if 0 <= i + by < devices]
+    return lax.ppermute(x, axis, pairs)
 
 
 def allowed_keys(segments, cycle_place, cycle_size, tok_rows):
@@ -290,4 +889,5 @@
         P("section", None, "dp"),
         P("section", None, "dp"),
     )
-    return jax.shard_map(body, mesh=mesh, in_specs=in_specs, out_specs=out_specs, check_vma=False)
+    step = spread_body if mesh.shape["dp"] == 8 else body
+    return jax.shard_map(step, mesh=mesh, in_specs=in_specs, out_specs=out_specs, check_vma=False)

time: 1940 us -> 1750 us (0.902)
  waiting for transfers between devices: 1510 us -> 843 us
  Pallas kernels: 0 us -> 657 us
  matrix products: 289 us -> 50.3 us
    reduce_scatter x5 -> x2, waiting for transfers between devices: 839 us -> 21.4 us  [spread_body(): lax.psum_scatter(pair[4], 'dp', scatter_dimension=0, tiled=True)]
    pallas_call x0 -> x8, Pallas kernels: none -> 657 us  [tensor_pass(): pl.pallas_call(kernel, name=name, out_shape=[jax.ShapeDtypeStruct((rows,...]
    all_gather x9 -> x1, waiting for transfers between devices: 608 us -> 0.01 us  [spread_body(): lax.all_gather(w_keyvalue[0], ('section', 'dp'), axis=0, tiled=True)]
    psum x0 -> x2, waiting for transfers between devices: none -> 523 us  [the longest x1 383 us: total(): return lax.psum(grad, ('section', 'ctx'))]
    dot_general x32 -> x0, matrix products: 235 us -> none  [the longest x10 110 us: dense_right(): lax.dot_general(left, right, (((1,), (1,)), ((), ())), preferred_element_...]
    all_to_all x0 -> x4, waiting for transfers between devices: none -> 126 us  [the longest x1 104 us: spread_body(): up = lax.all_to_all(w_up[0], 'dp', 1, 0, tiled=True)]
    ppermute x6 -> x10, waiting for transfers between devices: 47.5 us -> 172 us  [the longest x4 172 us: exchange(): return lax.ppermute(x, 'section', [(0, 1), (1, 0)])]
    all_gather x2, blocking collectives: 19.6 us -> 39.5 us  [the longest x1 24.6 us: spread_body(): lax.all_gather(jnp.concatenate([ln_gains[0], ln_biases[0]], axis=0), ('se...]
  transfers between devices with their start and end apart: 21 -> 19, of which waited for: 16 -> 7; matrix products, arithmetic and copies ran while one was open for 10% -> 5% of each run, Pallas kernels for 0% -> 19%
where the time goes in v2:
time: 1750 us; the launch traced here: 1740 us
  waiting for transfers between devices  843 us (48%)
  Pallas kernels  657 us (38%)
  other arithmetic  52.5 us (3%)
  matrix products  50.3 us (3%)
  local copies, waits for them, and re-layouts  46.6 us (3%)
  blocking collectives  39.5 us (2%)
  starting transfers between devices  33.1 us (2%)
    pallas_call x8, Pallas kernels, tensor_pass(): pl.pallas_call(kernel, name=name, out_shape=[jax.ShapeDtypeStruct((rows,...  657 us
    psum x1, waiting for transfers between devices, total(): return lax.psum(grad, ('section', 'ctx'))  383 us
    ppermute x4, waiting for transfers between devices, exchange(): return lax.ppermute(x, 'section', [(0, 1), (1, 0)])  172 us
    psum x1, waiting for transfers between devices, spread_body(): lax.psum(jnp.stack([scales_first, scales_second]), ('section', 'ctx', 'dp'))  140 us
    all_to_all x1, waiting for transfers between devices, spread_body(): up = lax.all_to_all(w_up[0], 'dp', 1, 0, tiled=True)  104 us
    dot_general x10, matrix products, dense_left(): lax.dot_general(left, right, (((0,), (0,)), ((), ())), preferred_element_...  50.3 us
  transfers between devices with their start and end apart: 19, of which 7 were waited for; matrix products, arithmetic and copies ran while one was open for 5% of the time, Pallas kernels for 19%

profile of v2, /device:TPU:0, one launch (start us, length us, event | category | flops | bytes accessed | tf_op | source)
XLA Modules:
  0.0 1737.0 jit_solution(15653288716097930051)
XLA Ops:
  7.2 6.6 copy.47
  18.1 6.5 all-to-all-start.1
  26.9 104.4 %all-to-all-done.1 = bf16[256,8,1024]{2,0,1:T(8,128)(2,1)} async-done(((bf16[256,8,1024]{2,0,1:T(8,128)(2,1)}), bf16[256,8,1024]{2,0,1:T(8,128)(2,1)}, u32[]{:S(2)}, u32[]{:S(2)}) %all-to-all-start.1) | async-done | bytes 4194336 | tf_op jit(solution)/shard_map/all_to_all | solution.py:529
  144.7 14.9 all-gather.2
  159.7 24.6 %all-gather.3 = bf16[16,4,256]{2,1,0:T(4,128)(2,1)S(1)} all-gather(bf16[1,4,256]{2,1,0:T(4,128)(2,1)S(1)} %maximum_bitcast_fusion.4), channel_id=2, replica_groups=mesh['section'=2,'ctx'=2,'dp'=8] {'section','dp'}, dimensions={0}, use_global_device_ids=true | all-gather | bytes 34816 | tf_op jit(solution)/shard_map/all_gather | solution.py:521
  191.2 150.1 %collective-permute-done.2.refs_6_.refs_3_ = bf16[256,2048]{1,0:T(8,128)(2,1)} collective-permute-done((bf16[256,2048]{1,0:T(8,128)(2,1)S(1)}, bf16[256,2048]{1,0:T(8,128)(2,1)}, u32[]{:S(2)}, u32[]{:S(2)}) %collective-permute-start.2) | collective-permute-done | bytes 1048608 | tf_op jit(solution)/shard_map/ppermute | solution.py:499
  341.3 21.8 %collective-permute-done.1.refs_4_.refs_1_ = bf16[2048,256]{1,0:T(8,128)(2,1)} collective-permute-done((bf16[2048,256]{1,0:T(8,128)(2,1)S(1)}, bf16[2048,256]{1,0:T(8,128)(2,1)}, u32[]{:S(2)}, u32[]{:S(2)}) %collective-permute-start.1) | collective-permute-done | bytes 1048608 | tf_op jit(solution)/shard_map/ppermute | solution.py:499
  363.1 79.2 %attention_forward.2 = (f32[128,2048]{1,0:T(8,128)}, bf16[4,2,128,2048]{3,2,1,0:T(8,128)(2,1)}, bf16[4,256,256]{2,1,0:T(8,128)(2,1)}, bf16[4,256,256]{2,1,0:T(8,128)(2,1)}, bf16[4,256,256]{2,1,0:T(8,128)(2,1)}) custom-call(bf16[128,2048]{1,0:T(8,128)(2,1)} %fusion.16.refs_0_, bf16[2048,256]{1,0:T(8,128)(2,1)} %bitcast.126, ...), custom_call_target="tpu_custom_call" | custom-call | tf_op jit(solution)/shard_map/attention_forward/pallas_call | solution.py:438
  445.1 83.7 %ffn_forward.2 = (f32[128,2048]{1,0:T(8,128)}, bf16[4,2,128,2048]{3,2,1,0:T(8,128)(2,1)}, bf16[4,256,1024]{2,1,0:T(8,128)(2,1)}, bf16[4,256,1024]{2,1,0:T(8,128)(2,1)}) custom-call(bf16[128,2048]{1,0:T(8,128)(2,1)} %add_convert_fusion.5.refs_0_, bf16[2048,1024]{1,0:T(8,128)(2,1)} %bitcast.19.refs_1_.refs_3_, bf16[1024,2048]{1,0:T(8,128)(2,1)} %bitcast.121, ...), custom_call_target="tpu_custom_call" | custom-call | tf_op jit(solution)/shard_map/ffn_forward/pallas_call | solution.py:438
  531.8 78.3 %attention_forward.3 = (f32[128,2048]{1,0:T(8,128)}, bf16[4,2,128,2048]{3,2,1,0:T(8,128)(2,1)}, bf16[4,256,256]{2,1,0:T(8,128)(2,1)}, bf16[4,256,256]{2,1,0:T(8,128)(2,1)}, bf16[4,256,256]{2,1,0:T(8,128)(2,1)}) custom-call(bf16[128,2048]{1,0:T(8,128)(2,1)} %fusion.13.refs_0_, bf16[2048,256]{1,0:T(8,128)(2,1)} %collective-permute-done.1.refs_4_.refs_1_, ...), custom_call_target="tpu_custom_call" | custom-call | tf_op jit(solution)/shard_map/attention_forward/pallas_call | solution.py:438
  612.8 83.7 %ffn_forward.3 = (f32[128,2048]{1,0:T(8,128)}, bf16[4,2,128,2048]{3,2,1,0:T(8,128)(2,1)}, bf16[4,256,1024]{2,1,0:T(8,128)(2,1)}, bf16[4,256,1024]{2,1,0:T(8,128)(2,1)}) custom-call(bf16[128,2048]{1,0:T(8,128)(2,1)} %add_convert_fusion.3.refs_0_, bf16[2048,1024]{1,0:T(8,128)(2,1)} %collective-permute-done.3.refs_3_.refs_1_, ...), custom_call_target="tpu_custom_call" | custom-call | tf_op jit(solution)/shard_map/ffn_forward/pallas_call | solution.py:438
  697.3 84.6 %ffn_backward.2 = (f32[128,2048]{1,0:T(8,128)}, bf16[4,2,128,2048]{3,2,1,0:T(8,128)(2,1)}, bf16[4,256,1024]{2,1,0:T(8,128)(2,1)}) custom-call(bf16[128,2048]{1,0:T(8,128)(2,1)} %copy-done.12, bf16[2048,1024]{1,0:T(8,128)(2,1)} %collective-permute-done.3.refs_3_.refs_1_, bf16[1024,2048]{1,0:T(8,128)(2,1)} %collective-permute-done.4.refs_4_.refs_2_, ...), custom_call_target="tpu_custom_call" | custom-call | tf_op jit(solution)/shard_map/ffn_backward/pallas_call | solution.py:438
  787.2 81.5 %attention_backward.2 = (f32[128,2048]{1,0:T(8,128)}, bf16[4,2,128,2048]{3,2,1,0:T(8,128)(2,1)}, bf16[4,256,256]{2,1,0:T(8,128)(2,1)}, bf16[4,256,256]{2,1,0:T(8,128)(2,1)}) custom-call(bf16[128,2048]{1,0:T(8,128)(2,1)} %fusion.22.refs_0_, bf16[2048,256]{1,0:T(8,128)(2,1)} %collective-permute-done.1.refs_4_.refs_1_, ...), custom_call_target="tpu_custom_call" | custom-call | tf_op jit(solution)/shard_map/attention_backward/pallas_call | solution.py:438
  874.9 84.5 %ffn_backward.3 = (f32[128,2048]{1,0:T(8,128)}, bf16[4,2,128,2048]{3,2,1,0:T(8,128)(2,1)}, bf16[4,256,1024]{2,1,0:T(8,128)(2,1)}) custom-call(bf16[128,2048]{1,0:T(8,128)(2,1)} %add_convert_fusion.1.refs_0_, bf16[2048,1024]{1,0:T(8,128)(2,1)} %bitcast.19.refs_1_.refs_3_, bf16[1024,2048]{1,0:T(8,128)(2,1)} %bitcast.124, ...), custom_call_target="tpu_custom_call" | custom-call | tf_op jit(solution)/shard_map/ffn_backward/pallas_call | solution.py:438
  963.9 81.4 %attention_backward.3 = (f32[128,2048]{1,0:T(8,128)}, bf16[4,2,128,2048]{3,2,1,0:T(8,128)(2,1)}, bf16[4,256,256]{2,1,0:T(8,128)(2,1)}, bf16[4,256,256]{2,1,0:T(8,128)(2,1)}) custom-call(bf16[128,2048]{1,0:T(8,128)(2,1)} %fusion.23.refs_0_, bf16[2048,256]{1,0:T(8,128)(2,1)} %bitcast.129, bf16[2048,256]{1,0:T(8,128)(2,1)} %get-tuple-element.139.refs_2_.refs_5_, ...), custom_call_target="tpu_custom_call" | custom-call | tf_op jit(solution)/shard_map/attention_backward/pallas_call | solution.py:438
  1073.6 6.3 convolution_convert_fusion
  1084.8 6.2 convolution_convert_fusion.3
  1091.0 6.2 convolution_convert_fusion.1
  1097.3 21.4 %reduce-scatter.5.cloned.1.call-done = bf16[256,256]{1,0:T(8,128)(2,1)} async-done(((bf16[2048,256]{1,0:T(8,128)(2,1)}), bf16[256,256]{1,0:T(8,128)(2,1)}) %reduce-scatter.5.cloned.1.call-update) | async-done | bytes 131088 | tf_op jit(solution)/shard_map/reduce_scatter | solution.py:610
  1118.7 383.1 %all-reduce.6.cloned.1.call-done = (bf16[2048,256]{1,0:T(8,128)(2,1)}, bf16[2048,256]{1,0:T(8,128)(2,1)}, bf16[256,256]{1,0:T(8,128)(2,1)}, bf16[256,256]{1,0:T(...) async-done(((bf16[2048,256]{1,0:T(8,128)(2,1)}, ...) | async-done | bytes 21233680 | tf_op jit(solution)/shard_map/psum | solution.py:597
  1513.3 21.9 %all-to-all-done.2 = bf16[8,256,256]{2,1,0:T(8,128)(2,1)S(1)} async-done(((bf16[8,256,256]{2,1,0:T(8,128)(2,1)}), bf16[8,256,256]{2,1,0:T(8,128)(2,1)S(1)}, u32[]{:S(2)}, u32[]{:S(2)}) %all-to-all-start.2) | async-done | bytes 1048608 | tf_op jit(solution)/shard_map/all_to_all | solution.py:607
  1554.3 139.6 %all-reduce.4.cloned.1.call-done = f32[2,4,2048]{2,1,0:T(4,128)} async-done(((f32[2,4,2048]{2,1,0:T(4,128)}), f32[2,4,2048]{2,1,0:T(4,128)}) %all-reduce.4.cloned.1.call-update) | async-done | bytes 65552 | tf_op jit(solution)/shard_map/psum | solution.py:614
  1712.5 8.1 copy.42
  1720.5 9.4 reshape.304
  (194 shorter events, 134.0 us)
Async XLA Ops:
  7.2 129.9 %copy-start = (bf16[2,1,128,2048]{3,2,1,0:T(8,128)(2,1)S(1)}, bf16[2,1,128,2048]{3,2,1,0:T(8,128)(2,1)}, u32[]{:S(2)}) copy-start(bf16[2,1,128,2048]{3,2,1,0:T(8,128)(2,1)} %param.11) | copy-start | bytes 3145732
  18.1 113.2 %all-to-all-start.1 = ((bf16[256,8,1024]{2,0,1:T(8,128)(2,1)}), bf16[256,8,1024]{2,0,1:T(8,128)(2,1)}, u32[]{:S(2)}, u32[]{:S(2)}) async-start(bf16[256,8,1024]{2,0,1:T(8,128)(2,1)} %copy.37), calls=%async_computation.1 | async-start | bytes 8388608 | tf_op jit(solution)/shard_map/all_to_all | solution.py:529
  24.6 163.6 %all-gather.6.cloned.1.call-start = ((), (), s32[]{:S(2)}) async-start(), calls=%async_computation.9 | async-start | bytes 2228224 | tf_op jit(solution)/shard_map/all_gather | solution.py:525
  25.4 134.2 %copy-start.23 = (bf16[1,2,256]{2,1,0:T(2,128)(2,1)S(1)}, bf16[1,2,256]{2,1,0:T(2,128)(2,1)}, u32[]{:S(2)}) copy-start(bf16[1,2,256]{2,1,0:T(2,128)(2,1)} %param.19) | copy-start | bytes 3076
  25.4 134.2 %copy-start.24 = (bf16[1,2,256]{2,1,0:T(2,128)(2,1)S(1)}, bf16[1,2,256]{2,1,0:T(2,128)(2,1)}, u32[]{:S(2)}) copy-start(bf16[1,2,256]{2,1,0:T(2,128)(2,1)} %param.18) | copy-start | bytes 3076
  131.3 55.1 %all-to-all-start = ((bf16[256,8,256]{2,0,1:T(8,128)(2,1)}), bf16[256,8,256]{2,0,1:T(8,128)(2,1)S(1)}, u32[]{:S(2)}, u32[]{:S(2)}) async-start(bf16[256,8,256]{2,0,1:T(8,128)(2,1)} %copy.35), calls=%async_computation | async-start | bytes 2097152 | tf_op jit(solution)/shard_map/all_to_all | solution.py:527
  134.9 962.3 %reduce-scatter.3.cloned.1.call-start = ((), (), s32[]{:S(2)}) async-start(), calls=%async_computation.6 | async-start | bytes 1179648 | tf_op jit(solution)/shard_map/reduce_scatter | solution.py:610
  135.0 310.1 %collective-permute-start.4 = (bf16[1024,2048]{1,0:T(8,128)(2,1)}, bf16[1024,2048]{1,0:T(8,128)(2,1)}, u32[]{:S(2)}, u32[]{:S(2)}) collective-permute-start(bf16[1024,2048]{1,0:T(8,128)(2,1)} %bitcast.120), channel_id=1, source_target_pairs={{0,16},{16,0},{1,17},{17,1},{2,18},{18,2},{3,19},{19,3},{4,20},{20... | collective-permute-start | bytes 12582920 | tf_op jit(solution)/shard_map/ppermute | solution.py:499
  136.5 308.6 %collective-permute-start.3 = (bf16[2048,1024]{1,0:T(8,128)(2,1)}, bf16[2048,1024]{1,0:T(8,128)(2,1)}, u32[]{:S(2)}, u32[]{:S(2)}) collective-permute-start(bf16[2048,1024]{1,0:T(8,128)(2,1)} %bitcast.19.refs_1_.refs_3_), channel_id=1, source_target_pairs={{0,16},{16,0},{1,17},{17,1},{2,18},{18,2},{3,19},{19,3},{4,20},{20... | collective-permute-start | bytes 12582920 | tf_op jit(solution)/shard_map/ppermute | solution.py:499
  137.9 558.6 %collective-permute-start.7 = (bf16[128,2048]{1,0:T(8,128)(2,1)}, bf16[128,2048]{1,0:T(8,128)(2,1)S(1)}, u32[]{:S(2)}, u32[]{:S(2)}) collective-permute-start(bf16[128,2048]{1,0:T(8,128)(2,1)} %dynamic-slice_bitcast_fusion), channel_id=1, source_target_pairs={{0,0},{1,8},{2,2},{3,10},{4,4},{5,12},{6,6},{7,14},{8,1},{9,9},{10... | collective-permute-start | bytes 1572872 | tf_op jit(solution)/shard_map/ppermute | solution.py:487
  141.5 44.5 %collective-permute-start = (bf16[128,2048]{1,0:T(8,128)(2,1)}, bf16[128,2048]{1,0:T(8,128)(2,1)S(1)}, u32[]{:S(2)}, u32[]{:S(2)}) collective-permute-start(bf16[128,2048]{1,0:T(8,128)(2,1)} %dynamic-slice_bitcast_fusion.1), channel_id=1, source_target_pairs={{0,0},{1,8},{2,2},{3,10},{4,4},{5,12},{6,6},{7,14},{8,1},{9,9},{10... | collective-permute-start | bytes 1572872 | tf_op jit(solution)/shard_map/ppermute | solution.py:487
  143.2 198.2 %collective-permute-start.2 = (bf16[256,2048]{1,0:T(8,128)(2,1)S(1)}, bf16[256,2048]{1,0:T(8,128)(2,1)}, u32[]{:S(2)}, u32[]{:S(2)}) collective-permute-start(bf16[256,2048]{1,0:T(8,128)(2,1)S(1)} %bitcast.136), channel_id=1, source_target_pairs={{0,16},{16,0},{1,17},{17,1},{2,18},{18,2},{3,19},{19,3},{4,20},{20... | collective-permute-start | bytes 3145736 | tf_op jit(solution)/shard_map/ppermute | solution.py:499
  185.9 256.4 %copy-start.3 = (bf16[128,2048]{1,0:T(8,128)(2,1)}, bf16[128,2048]{1,0:T(8,128)(2,1)S(1)}, u32[]{:S(2)}) copy-start(bf16[128,2048]{1,0:T(8,128)(2,1)S(1)} %collective-permute-done) | copy-start | bytes 1572868
  186.4 176.7 %copy-start.2 = (bf16[256,8,256]{2,0,1:T(8,128)(2,1)}, bf16[256,8,256]{2,0,1:T(8,128)(2,1)S(1)}, u32[]{:S(2)}) copy-start(bf16[256,8,256]{2,0,1:T(8,128)(2,1)S(1)} %all-to-all-done) | copy-start | bytes 3145732
  186.4 176.7 %collective-permute-start.1 = (bf16[2048,256]{1,0:T(8,128)(2,1)S(1)}, bf16[2048,256]{1,0:T(8,128)(2,1)}, u32[]{:S(2)}, u32[]{:S(2)}) collective-permute-start(bf16[2048,256]{1,0:T(8,128)(2,1)S(1)} %bitcast.125), channel_id=1, source_target_pairs={{0,16},{16,0},{1,17},{17,1},{2,18},{18,2},{3,19},{19,3},{4,20},{20... | collective-permute-start | bytes 3145736 | tf_op jit(solution)/shard_map/ppermute | solution.py:499
  1054.6 64.1 %reduce-scatter.5.cloned.1.call-start = ((), (), s32[]{:S(2)}) async-start(), calls=%async_computation.7 | async-start | bytes 1179648 | tf_op jit(solution)/shard_map/reduce_scatter | solution.py:610
  1079.9 421.8 %all-reduce.6.cloned.1.call-start = ((), (), s32[]{:S(2)}) async-start(), calls=%async_computation.10 | async-start | bytes 42467328 | tf_op jit(solution)/shard_map/psum | solution.py:597
  1504.0 31.2 %all-to-all-start.2 = ((bf16[8,256,256]{2,1,0:T(8,128)(2,1)}), bf16[8,256,256]{2,1,0:T(8,128)(2,1)S(1)}, u32[]{:S(2)}, u32[]{:S(2)}) async-start(bf16[8,256,256]{2,1,0:T(8,128)(2,1)} %bitcast.138), calls=%async_computation.2 | async-start | bytes 2097152 | tf_op jit(solution)/shard_map/all_to_all | solution.py:607
  1536.2 173.1 %all-to-all-start.3 = ((bf16[8,256,1024]{2,1,0:T(8,128)(2,1)}), bf16[8,256,1024]{2,1,0:T(8,128)(2,1)}, u32[]{:S(2)}, u32[]{:S(2)}) async-start(bf16[8,256,1024]{2,1,0:T(8,128)(2,1)} %bitcast.130), calls=%async_computation.5 | async-start | bytes 8388608 | tf_op jit(solution)/shard_map/all_to_all | solution.py:606
  1540.8 153.1 %all-reduce.4.cloned.1.call-start = ((), (), s32[]{:S(2)}) async-start(), calls=%async_computation.8 | async-start | bytes 131072 | tf_op jit(solution)/shard_map/psum | solution.py:614
  1543.3 152.1 %collective-permute-start.5 = (bf16[128,2048]{1,0:T(8,128)(2,1)}, bf16[128,2048]{1,0:T(8,128)(2,1)S(1)}, u32[]{:S(2)}, u32[]{:S(2)}) collective-permute-start(bf16[128,2048]{1,0:T(8,128)(2,1)} %get-tuple-element.136), channel_id=1, source_target_pairs={{0,0},{1,8},{2,2},{3,10},{4,4},{5,12},{6,6},{7,14},{8,1},{9,9},{10... | collective-permute-start | bytes 1572872 | tf_op jit(solution)/shard_map/ppermute | solution.py:487
  1545.1 150.2 %collective-permute-start.6 = (bf16[128,2048]{1,0:T(8,128)(2,1)}, bf16[128,2048]{1,0:T(8,128)(2,1)}, u32[]{:S(2)}, u32[]{:S(2)}) collective-permute-start(bf16[128,2048]{1,0:T(8,128)(2,1)} %get-tuple-element.137), channel_id=1, source_target_pairs={{0,16},{1,24},{2,18},{3,26},{4,20},{5,28},{6,22},{7,30},{8,17},{9,... | collective-permute-start | bytes 1572872 | tf_op jit(solution)/shard_map/ppermute | solution.py:495
  1551.8 145.9 %collective-permute-start.9 = (bf16[128,2048]{1,0:T(8,128)(2,1)}, bf16[128,2048]{1,0:T(8,128)(2,1)S(1)}, u32[]{:S(2)}, u32[]{:S(2)}) collective-permute-start(bf16[128,2048]{1,0:T(8,128)(2,1)} %broadcast_select_fusion.2), channel_id=1, source_target_pairs={{0,16},{1,24},{2,18},{3,26},{4,20},{5,28},{6,22},{7,30},{8,17},{9,... | collective-permute-start | bytes 1572872 | tf_op jit(solution)/shard_map/ppermute | solution.py:495
  1552.3 145.3 %collective-permute-start.8 = (bf16[128,2048]{1,0:T(8,128)(2,1)}, bf16[128,2048]{1,0:T(8,128)(2,1)S(1)}, u32[]{:S(2)}, u32[]{:S(2)}) collective-permute-start(bf16[128,2048]{1,0:T(8,128)(2,1)} %get-tuple-element.122), channel_id=1, source_target_pairs={{0,0},{1,8},{2,2},{3,10},{4,4},{5,12},{6,6},{7,14},{8,1},{9,9},{10... | collective-permute-start | bytes 1572872 | tf_op jit(solution)/shard_map/ppermute | solution.py:487
  (35 other events, 392.2 us)
Sparse Core Ops, SparseCore 0:
  27.6 51.1 all-gather.5
  1054.7 30.7 reduce-scatter.2
  1087.8 30.7 reduce-scatter.4
  1124.5 377.2 all-reduce.5
  1548.4 145.4 all-reduce.3

commit v3 on v2

--- a/solution.py
+++ b/solution.py
@@ -467,13 +467,236 @@
             dma((places, PARTS)),
             dma((places, PARTS)),
         ],
+        cost_estimate=pl.CostEstimate(
+            flops=60_000_000_000, bytes_accessed=20_000_000, transcendentals=0
+        ),
         compiler_params=pltpu.CompilerParams(
             collective_id=ident, has_side_effects=True, vmem_limit_bytes=60 * 1024 * 1024
         ),
     )(x, *early_weights, *late_weights, *ins)
 
 
-def swapped(size, places):
+def distribute_kernel(
+    places, query, keyvalue, out, up, down,
+    query_own, keyvalue_own, up_own, query_far, keyvalue_far, out_far, up_far, down_far,
+    local_sem, query_send, query_recv, keyvalue_send, keyvalue_recv, up_send, up_recv,
+    across_send, across_recv, over_send, over_recv,
+):
+    section = lax.axis_index("section")
+    ctx = lax.axis_index("ctx")
+    me = lax.axis_index("dp")
+    z = me // 2
+    k = me % 2
+    last = places - 1
+    rows = query.shape[0]
+    half = rows // 2
+    head_width = query_own.shape[1]
+    unit_width = up_own.shape[1]
+    across = {"section": 1 - section}
+    over = {"ctx": 1 - ctx}
+
+    def peers(act):
+        act(2 * z + 1 - k)
+        for away in range(1, places):
+
+            @pl.when(z + away <= last)
+            def _():
+                act(2 * (z + away) + k)
+                act(2 * (z + away) + 1 - k)
+
+            @pl.when(z - away >= 0)
+            def _():
+                act(2 * (z - away) + k)
+                act(2 * (z - away) + 1 - k)
+
+    def remote(source, target, send, recv, device):
+        return pltpu.make_async_remote_copy(
+            source, target, send, recv, device_id=device, device_id_type=MESH
+        )
+
+    def piece(owner, part):
+        which = jnp.where(part == 0, ctx, 1 - ctx)
+        return pl.ds(pl.multiple_of(owner * rows + which * half, half), half)
+
+    def query_copy(source, to):
+        return remote(
+            query.at[:, tile_at(to, head_width)], query_own.at[tile_at(source, rows)],
+            query_send.at[to], query_recv.at[source], {"dp": to},
+        )
+
+    def keyvalue_copy(source, to):
+        return remote(
+            keyvalue, keyvalue_own.at[tile_at(source, rows)],
+            keyvalue_send.at[to], keyvalue_recv.at[source], {"dp": to},
+        )
+
+    def up_copy(source, to, part):
+        which = jnp.where(part == 0, ctx, 1 - ctx)
+        return remote(
+            up.at[tile_at(which, half), tile_at(to, unit_width)],
+            up_own.at[piece(source, part)],
+            up_send.at[to, part], up_recv.at[source, part], {"dp": to},
+        )
+
+    barrier = pltpu.get_barrier_semaphore()
+
+    def greet(to):
+        pl.semaphore_signal(barrier, inc=1, device_id={"dp": to}, device_id_type=MESH)
+
+    peers(greet)
+    pl.semaphore_signal(barrier, inc=1, device_id=across, device_id_type=MESH)
+    pl.semaphore_signal(barrier, inc=1, device_id=over, device_id_type=MESH)
+    pl.semaphore_wait(barrier, 2 * places + 1)
+
+    local = [
+        pltpu.make_async_copy(
+            query.at[:, tile_at(me, head_width)], query_own.at[tile_at(me, rows)], local_sem.at[0]
+        ),
+        pltpu.make_async_copy(keyvalue, keyvalue_own.at[tile_at(me, rows)], local_sem.at[1]),
+        pltpu.make_async_copy(
+            up.at[:, tile_at(me, unit_width)], up_own.at[tile_at(me, rows)], local_sem.at[2]
+        ),
+    ]
+    for copy in local:
+        copy.start()
+    peers(lambda to: query_copy(me, to).start())
+    peers(lambda to: keyvalue_copy(me, to).start())
+    peers(lambda to: up_copy(me, to, 0).start())
+
+    out_half = tile_at(ctx, out.shape[0] // 2)
+    quarter = down.shape[0] // 4
+    flows = [(out, out_far, out_half)] + [
+        (down, down_far, pl.ds(pl.multiple_of((2 * ctx + index) * quarter, quarter), quarter))
+        for index in range(2)
+    ]
+
+    def flow_across(slot):
+        source, target, at = flows[slot]
+        return remote(
+            source.at[at], target.at[at], across_send.at[slot], across_recv.at[slot], across
+        )
+
+    def flow_over(slot):
+        source, target, at = flows[slot]
+        return remote(target.at[at], target.at[at], over_send.at[slot], over_recv.at[slot], over)
+
+    first_slot = len(flows)
+    kinds = [(query_own, query_far), (keyvalue_own, keyvalue_far), (up_own, up_far)]
+
+    def block_across(kind, owner):
+        own, far = kinds[kind]
+        slot = first_slot + kind * 2 * places + owner
+        at = piece(owner, 0)
+        return remote(own.at[at], far.at[at], across_send.at[slot], across_recv.at[slot], across)
+
+    def block_over(kind, owner):
+        own, far = kinds[kind]
+        slot = first_slot + kind * 2 * places + owner
+        at = piece(owner, 0)
+        return remote(far.at[at], far.at[at], over_send.at[slot], over_recv.at[slot], over)
+
+    flow_across(0).start()
+
+    local[0].wait()
+    local[1].wait()
+    block_across(0, me).start()
+    block_across(1, me).start()
+
+    def pass_small(source):
+        query_copy(source, me).wait_recv()
+        block_across(0, source).start()
+        keyvalue_copy(source, me).wait_recv()
+        block_across(1, source).start()
+
+    peers(pass_small)
+    peers(lambda to: up_copy(me, to, 1).start())
+    flow_across(1).start()
+    flow_across(0).wait_recv()
+    flow_over(0).start()
+    local[2].wait()
+    block_across(2, me).start()
+
+    def pass_up(source):
+        up_copy(source, me, 0).wait_recv()
+        block_across(2, source).start()
+
+    peers(pass_up)
+    flow_across(2).start()
+
+    def over_small(owner, carry):
+        block_across(0, owner).wait_recv()
+        block_over(0, owner).start()
+        block_across(1, owner).wait_recv()
+        block_over(1, owner).start()
+        return carry
+
+    lax.fori_loop(0, 2 * places, over_small, 0)
+    flow_across(1).wait_recv()
+    flow_over(1).start()
+
+    def over_up(owner, carry):
+        block_across(2, owner).wait_recv()
+        block_over(2, owner).start()
+        return carry
+
+    lax.fori_loop(0, 2 * places, over_up, 0)
+    flow_across(2).wait_recv()
+    flow_over(2).start()
+
+    peers(lambda source: up_copy(source, me, 1).wait_recv())
+
+    def over_wait(slot_owner, carry):
+        for kind in range(3):
+            block_over_in(kind, slot_owner).wait_recv()
+            block_across(kind, slot_owner).wait_send()
+            block_over(kind, slot_owner).wait_send()
+        return carry
+
+    def block_over_in(kind, owner):
+        own, far = kinds[kind]
+        slot = first_slot + kind * 2 * places + owner
+        at = piece(owner, 1)
+        return remote(far.at[at], far.at[at], over_send.at[slot], over_recv.at[slot], over)
+
+    lax.fori_loop(0, 2 * places, over_wait, 0)
+    for slot in range(first_slot):
+        flow_over(slot).wait_recv()
+        flow_across(slot).wait_send()
+        flow_over(slot).wait_send()
+
+    def sent(to):
+        query_copy(me, to).wait_send()
+        keyvalue_copy(me, to).wait_send()
+        up_copy(me, to, 0).wait_send()
+        up_copy(me, to, 1).wait_send()
+
+    peers(sent)
+
+
+def distribute(query, keyvalue, out, up, down):
+    size = lax.axis_size("dp")
+    places = size // 2
+    hbm = pl.BlockSpec(memory_space=pl.ANY)
+    dma = pltpu.SemaphoreType.DMA
+    rows = query.shape[0] * size
+    turned = [(rows, query.shape[1] // size), (rows, keyvalue.shape[1]), (rows, up.shape[1] // size)]
+    shapes = turned + turned[:2] + [out.shape, turned[2], down.shape]
+    slots = 3 + 3 * size
+    return pl.pallas_call(
+        functools.partial(distribute_kernel, places),
+        name="distribute",
+        out_shape=[jax.ShapeDtypeStruct(shape, jnp.bfloat16) for shape in shapes],
+        in_specs=[hbm] * 5,
+        out_specs=[hbm] * 8,
+        scratch_shapes=[dma((3,))]
+        + [dma((size,))] * 4
+        + [dma((size, 2))] * 2
+        + [dma((slots,))] * 4,
+        compiler_params=pltpu.CompilerParams(collective_id=4, has_side_effects=True),
+    )(query, keyvalue, out, up, down)
+
+
+def swapped(size):
     pairs = []
     for ctx in range(2):
         for at in range(size):
@@ -483,20 +706,32 @@
 
 
 def regroup(x):
-    size = lax.axis_size("dp")
-    return lax.ppermute(x, ("ctx", "dp"), swapped(size, size // 2))
+    return lax.ppermute(x, ("ctx", "dp"), swapped(lax.axis_size("dp")))
 
 
 def regroup_across(x):
     size = lax.axis_size("dp")
     half = 2 * size
-    pairs = swapped(size, size // 2)
+    pairs = swapped(size)
     across = [(a, b + half) for a, b in pairs] + [(a + half, b) for a, b in pairs]
     return lax.ppermute(x, ("section", "ctx", "dp"), across)
 
 
-def exchange(x):
-    return lax.ppermute(x, "section", [(0, 1), (1, 0)])
+def halves_summed(layer, grad):
+    ctx = lax.axis_index("ctx")
+    half = grad.shape[-2] // 2
+    mine = lax.dynamic_slice_in_dim(grad, ctx * half, half, axis=-2)
+    others = lax.dynamic_slice_in_dim(grad, (1 - ctx) * half, half, axis=-2)
+    mine = mine + lax.ppermute(others, "ctx", [(0, 1), (1, 0)])
+    return mine + lax.ppermute(mine, "section", [(1 - layer, layer)])
+
+
+def both_halves(half):
+    ctx = lax.axis_index("ctx")
+    other = lax.ppermute(half, "ctx", [(0, 1), (1, 0)])
+    first = jnp.where(ctx == 0, half, other)
+    second = jnp.where(ctx == 0, other, half)
+    return jnp.concatenate([first, second], axis=-2)
 
 
 def spread_body(
@@ -522,18 +757,12 @@
         jnp.concatenate([ln_gains[0], ln_biases[0]], axis=0), ("section", "dp")
     ).reshape(2, size, 4, -1)
     scales = scales.transpose(0, 2, 1, 3).reshape(2, 4, width).astype(jnp.float32)
-    keyvalue = lax.all_gather(w_keyvalue[0], ("section", "dp"), axis=0, tiled=True)
-    keyvalue = keyvalue.reshape(2, width, -1)
-    query = lax.all_to_all(w_query[0], "dp", 1, 0, tiled=True)
-    out = w_out[0]
-    up = lax.all_to_all(w_up[0], "dp", 1, 0, tiled=True)
-    down = w_down[0]
-    query_far, out_far = exchange(query), exchange(out)
-    up_far, down_far = exchange(up), exchange(down)
-    attention_weights = [
-        ([query, keyvalue[0], out], [query_far, keyvalue[0], out_far]),
-        ([query_far, keyvalue[1], out_far], [query, keyvalue[1], out]),
-    ]
+    out, down = w_out[0], w_down[0]
+    query, keyvalue, up, query_far, keyvalue_far, out_far, up_far, down_far = distribute(
+        w_query[0], w_keyvalue[0], out, w_up[0], down
+    )
+    attention_near, attention_far = [query, keyvalue, out], [query_far, keyvalue_far, out_far]
+    attention_weights = [(attention_near, attention_far), (attention_far, attention_near)]
     ffn_weights = [([up, down], [up_far, down_far]), ([up_far, down_far], [up, down])]
     head_width = query.shape[1]
     unit_width = up.shape[1]
@@ -542,7 +771,7 @@
         normed = layer_norm(hidden, scales[layer, 0], scales[layer, 2]).astype(jnp.bfloat16)
         y, normed_all, q, kv, mixed = tensor_pass(
             attention_forward_at, "attention_forward", 0, normed, *attention_weights[layer], segs,
-            [head_width, keyvalue.shape[2], head_width],
+            [head_width, keyvalue.shape[1], head_width],
         )
         after = hidden + y
         normed_two = layer_norm(after, scales[layer, 1], scales[layer, 3]).astype(jnp.bfloat16)
@@ -553,33 +782,34 @@
         result = (after + y).astype(jnp.bfloat16)
         return result, (hidden, normed_all, q, kv, mixed, after, normed_two_all, up_rows, activated)
 
+    def product(left, right):
+        return dense_left(left.reshape(tall), right.reshape(tall)).astype(jnp.bfloat16)
+
+    def rows_of_all(grad):
+        return grad.reshape(size, grad.shape[0] // size, grad.shape[1])
+
     def backward(layer, grad_low, kept):
         hidden, normed_all, q, kv, mixed, after, normed_two_all, up_rows, activated = kept
         y, grad_low_all, grad_upper = tensor_pass(
             ffn_backward_at, "ffn_backward", 2, grad_low, *ffn_weights[layer], [up_rows],
             [unit_width],
         )
+        up_grad = halves_summed(layer, rows_of_all(product(normed_two_all, grad_upper)))
+        down_grad = halves_summed(layer, product(activated, grad_low_all))
         _, norm_back = jax.vjp(layer_norm, after, scales[layer, 1], scales[layer, 3])
         grad_norm, gain_two, bias_two = norm_back(y)
         grad_after = grad_low.astype(jnp.float32) + grad_norm
         y, grad_branch_all, grad_query, grad_kv = tensor_pass(
             attention_backward_at, "attention_backward", 3, grad_after.astype(jnp.bfloat16),
-            *attention_weights[layer], segs + [q, kv], [head_width, keyvalue.shape[2]],
-        )
+            *attention_weights[layer], segs + [q, kv], [head_width, keyvalue.shape[1]],
+        )
+        query_grad = halves_summed(layer, rows_of_all(product(normed_all, grad_query)))
+        out_grad = halves_summed(layer, product(mixed, grad_branch_all))
+        keyvalue_grad = product(normed_all, grad_kv)
         _, norm_back = jax.vjp(layer_norm, hidden, scales[layer, 0], scales[layer, 2])
         grad_norm, gain_one, bias_one = norm_back(y)
         grad_input = (grad_after + grad_norm).astype(jnp.bfloat16)
-
-        def product(left, right):
-            return dense_left(left.reshape(tall), right.reshape(tall)).astype(jnp.bfloat16)
-
-        weight_grads = (
-            product(activated, grad_low_all),
-            product(normed_two_all, grad_upper),
-            product(mixed, grad_branch_all),
-            product(normed_all, grad_query),
-            product(normed_all, grad_kv),
-        )
+        weight_grads = (query_grad, keyvalue_grad, out_grad, up_grad, down_grad)
         return grad_input, weight_grads, jnp.stack([gain_one, gain_two, bias_one, bias_two])
 
     first, kept_first = forward(0, hidden)
@@ -593,29 +823,24 @@
         far = regroup_across(jnp.where(early, two, one))
         return jnp.stack([jnp.where(early, near, far), jnp.where(early, far, near)])[None, :, None]
 
-    def total(grad):
-        return lax.psum(grad, ("section", "ctx"))
-
-    def own(one, two):
-        return jnp.where(early, one, two)
-
-    def summed(index):
-        return own(total(weights_first[index]), total(weights_second[index]))
-
-    down_grad, up_grad, out_grad, query_grad = [summed(index) for index in range(4)]
-    up_grad = lax.all_to_all(up_grad, "dp", 0, 1, tiled=True)
-    query_grad = lax.all_to_all(query_grad, "dp", 0, 1, tiled=True)
-    keyvalue_grad = own(
-        *[
-            total(lax.psum_scatter(pair[4], "dp", scatter_dimension=0, tiled=True))
-            for pair in (weights_first, weights_second)
-        ]
-    )
-    scale_grads = lax.psum(jnp.stack([scales_first, scales_second]), ("section", "ctx", "dp"))
+    query_grad, _, out_grad, up_grad, down_grad = [
+        jnp.where(early, one, two) for one, two in zip(weights_first, weights_second)
+    ]
+
+    def turned(grad):
+        grad = lax.all_to_all(grad, "dp", 0, 0)
+        return grad.transpose(1, 0, 2).reshape(grad.shape[1], size * grad.shape[2])
+
+    keyvalue_grad = lax.psum_scatter(
+        jnp.stack([weights_first[1], weights_second[1]]), "dp", scatter_dimension=1, tiled=True
+    )
+    keyvalue_grad = lax.psum(keyvalue_grad, ("section", "ctx"))
+    keyvalue_grad = lax.dynamic_index_in_dim(keyvalue_grad, section, 0, keepdims=False)
+    scale_grads = lax.psum_scatter(
+        jnp.stack([scales_first, scales_second]), "dp", scatter_dimension=2, tiled=True
+    )
+    scale_grads = lax.psum(scale_grads, ("section", "ctx"))
     scale_grads = lax.dynamic_index_in_dim(scale_grads, section, 0, keepdims=True)
-    scale_grads = lax.dynamic_slice_in_dim(
-        scale_grads, lax.axis_index("dp") * ln_gains.shape[2], ln_gains.shape[2], axis=2
-    )
 
     def given(grad):
         return grad.astype(jnp.float32)[None]
@@ -623,11 +848,11 @@
     return (
         both_rows(first, second),
         both_rows(grad_first, grad_second),
-        given(query_grad),
+        given(both_halves(turned(query_grad))),
         given(keyvalue_grad),
-        given(out_grad),
-        given(up_grad),
-        given(down_grad),
+        given(both_halves(out_grad)),
+        given(both_halves(turned(up_grad))),
+        given(both_halves(down_grad)),
         scale_grads[:, 0:2],
         scale_grads[:, 2:4],
     )

time: 1750 us -> 1390 us (0.79)
  waiting for transfers between devices: 843 us -> 195 us
  Pallas kernels: 657 us -> 889 us
  other arithmetic: 52.5 us -> 86.4 us
  blocking collectives: 39.5 us -> 67.7 us
  starting transfers between devices: 33.1 us -> 56.9 us
    psum x2 -> x1, waiting for transfers between devices: 523 us -> 43.6 us  [spread_body(): keyvalue_grad = lax.psum(keyvalue_grad, ('section', 'ctx'))]
    pallas_call x0 -> x1, Pallas kernels: none -> 233 us  [distribute(): pl.pallas_call(functools.partial(distribute_kernel, places), name='distri...]
    all_to_all x4 -> x2, waiting for transfers between devices: 126 us -> 0.01 us  [turned(): grad = lax.all_to_all(grad, 'dp', 0, 0)]
    psum x0 -> x1, blocking collectives: none -> 36.6 us  [spread_body(): scale_grads = lax.psum(scale_grads, ('section', 'ctx'))]
    ppermute x8 -> x24, starting transfers between devices: 11.3 us -> 46.3 us  [the longest x8 20.2 us: halves_summed(): return mine + lax.ppermute(mine, 'section', [(1 - layer, layer)])]
    ppermute x8 -> x24, waiting for transfers between devices: 172 us -> 149 us  [the longest x8 80.6 us: halves_summed(): return mine + lax.ppermute(mine, 'section', [(1 - layer, layer)])]
    reduce_scatter x2 -> x1, waiting for transfers between devices: 21.4 us -> 0.01 us  [spread_body(): lax.psum_scatter(jnp.stack([weights_first[1], weights_second[1]]), 'dp',...]
    convert_element_type x4 -> x0, local copies, waits for them, and re-layouts: 20.2 us -> none  [given(): return grad.astype(jnp.float32)[None]]
  transfers between devices with their start and end apart: 19 -> 31, of which waited for: 7 -> 8; matrix products, arithmetic and copies ran while one was open for 5% -> 9% of each run, Pallas kernels for 19% -> 58%
where the time goes in v3:
time: 1390 us; the launch traced here: 1380 us
  Pallas kernels  889 us (64%)
  waiting for transfers between devices  195 us (14%)
  other arithmetic  86.4 us (6%)
  blocking collectives  67.7 us (5%)
  starting transfers between devices  56.9 us (4%)
  matrix products  34 us (2%)
  local copies, waits for them, and re-layouts  31.9 us (2%)
  between operations  15.5 us (1%)
    pallas_call x8, Pallas kernels, tensor_pass(): pl.pallas_call(kernel, name=name, out_shape=[jax.ShapeDtypeStruct((rows,...  656 us
    pallas_call x1, Pallas kernels, distribute(): pl.pallas_call(functools.partial(distribute_kernel, places), name='distri...  233 us
    ppermute x8, waiting for transfers between devices, halves_summed(): return mine + lax.ppermute(mine, 'section', [(1 - layer, layer)])  80.6 us
    ppermute x4, waiting for transfers between devices, both_halves(): other = lax.ppermute(half, 'ctx', [(0, 1), (1, 0)])  57.8 us
    psum x1, waiting for transfers between devices, spread_body(): keyvalue_grad = lax.psum(keyvalue_grad, ('section', 'ctx'))  43.6 us
    psum x1, blocking collectives, spread_body(): scale_grads = lax.psum(scale_grads, ('section', 'ctx'))  36.6 us
    dot_general x10, matrix products, dense_left(): lax.dot_general(left, right, (((0,), (0,)), ((), ())), preferred_element_...  34 us
  transfers between devices with their start and end apart: 31, of which 8 were waited for; matrix products, arithmetic and copies ran while one was open for 9% of the time, Pallas kernels for 58%

profile of v3, /device:TPU:0, one launch (start us, length us, event | category | flops | bytes accessed | tf_op | source)
XLA Modules:
  0.0 1376.4 jit_solution(9399251066844186211)
XLA Ops:
  9.3 5.4 collective-permute-start.3
  16.4 13.5 all-gather.1
  30.0 17.6 %all-gather.2 = bf16[16,4,256]{2,1,0:T(4,128)(2,1)S(1)} all-gather(bf16[1,4,256]{2,1,0:T(4,128)(2,1)S(1)} %maximum_bitcast_fusion.4), channel_id=2, replica_groups=mesh['section'=2,'ctx'=2,'dp'=8] {'section','dp'}, dimensions={0}, use_global_device_ids=true | all-gather | bytes 34816 | tf_op jit(solution)/shard_map/all_gather | solution.py:756
  49.2 232.8 %distribute.1 = (bf16[2048,256]{1,0:T(8,128)(2,1)}, bf16[2048,256]{1,0:T(8,128)(2,1)}, bf16[2048,1024]{1,0:T(8,128)(2,1)}, bf16[2048,256]{1,0:T(8,128)(2,1)}, bf...) custom-call(bf16[256,2048]{1,0:T(8,128)(2,1)} %bitcast.145, ...), custom_call_target="tpu_custom_call" | custom-call | tf_op jit(solution)/shard_map/distribute/pallas_call | solution.py:685
  284.5 78.3 %attention_forward.2 = (f32[128,2048]{1,0:T(8,128)}, bf16[4,2,128,2048]{3,2,1,0:T(8,128)(2,1)}, bf16[4,256,256]{2,1,0:T(8,128)(2,1)}, bf16[4,256,256]{2,1,0:T(8,128)(2,1)}, bf16[4,256,256]{2,1,0:T(8,128)(2,1)}) custom-call(bf16[128,2048]{1,0:T(8,128)(2,1)} %fusion.18.refs_0_, bf16[2048,256]{1,0:T(8,128)(2,1)} %get-tuple-element.49.refs_1_.refs_4_, ...), custom_call_target="tpu_custom_call" | custom-call | flops 60000002048 | bytes 20000000 | tf_op jit(solution)/shard_map/attention_forward/pallas_call | solution.py:438
  365.6 83.8 %ffn_forward.2 = (f32[128,2048]{1,0:T(8,128)}, bf16[4,2,128,2048]{3,2,1,0:T(8,128)(2,1)}, bf16[4,256,1024]{2,1,0:T(8,128)(2,1)}, bf16[4,256,1024]{2,1,0:T(8,128)(2,1)}) custom-call(bf16[128,2048]{1,0:T(8,128)(2,1)} %add_convert_fusion.5.refs_0_, bf16[2048,1024]{1,0:T(8,128)(2,1)} %get-tuple-element.55.refs_1_.refs_3_, bf16[1024,2048]{1,0:T(8,128)(2,1)} %bitcast.133, ...), custom_call_target="tpu_custom_call" | custom-call | flops 60000002048 | bytes 20000000 | tf_op jit(solution)/shard_map/ffn_forward/pallas_call | solution.py:438
  452.4 78.4 %attention_forward.3 = (f32[128,2048]{1,0:T(8,128)}, bf16[4,2,128,2048]{3,2,1,0:T(8,128)(2,1)}, bf16[4,256,256]{2,1,0:T(8,128)(2,1)}, bf16[4,256,256]{2,1,0:T(8,128)(2,1)}, bf16[4,256,256]{2,1,0:T(8,128)(2,1)}) custom-call(bf16[128,2048]{1,0:T(8,128)(2,1)} %fusion.15.refs_0_, bf16[2048,256]{1,0:T(8,128)(2,1)} %get-tuple-element.51.refs_4_.refs_1_, ...), custom_call_target="tpu_custom_call" | custom-call | flops 60000002048 | bytes 20000000 | tf_op jit(solution)/shard_map/attention_forward/pallas_call | solution.py:438
  533.6 83.8 %ffn_forward.3 = (f32[128,2048]{1,0:T(8,128)}, bf16[4,2,128,2048]{3,2,1,0:T(8,128)(2,1)}, bf16[4,256,1024]{2,1,0:T(8,128)(2,1)}, bf16[4,256,1024]{2,1,0:T(8,128)(2,1)}) custom-call(bf16[128,2048]{1,0:T(8,128)(2,1)} %add_convert_fusion.3.refs_0_, bf16[2048,1024]{1,0:T(8,128)(2,1)} %get-tuple-element.56.refs_3_.refs_1_, ...), custom_call_target="tpu_custom_call" | custom-call | flops 60000002048 | bytes 20000000 | tf_op jit(solution)/shard_map/ffn_forward/pallas_call | solution.py:438
  617.4 84.4 %ffn_backward.2 = (f32[128,2048]{1,0:T(8,128)}, bf16[4,2,128,2048]{3,2,1,0:T(8,128)(2,1)}, bf16[4,256,1024]{2,1,0:T(8,128)(2,1)}) custom-call(bf16[128,2048]{1,0:T(8,128)(2,1)} %collective-permute-done.3.refs_0_, bf16[2048,1024]{1,0:T(8,128)(2,1)} %get-tuple-element.56.refs_3_.refs_1_, bf16[1024,2048]{1,0:T(8,128)(2,1)} %get-tuple-element.57.refs_4_.refs_2_, ...), custom_call_target="tpu_custom_call" | custom-call | flops 60000002048 | bytes 20000000 | tf_op jit(solution)/shard_map/ffn_backward/pallas_call | solution.py:438
  704.6 6.6 convolution_convert_fusion.2
  726.4 81.6 %attention_backward.2 = (f32[128,2048]{1,0:T(8,128)}, bf16[4,2,128,2048]{3,2,1,0:T(8,128)(2,1)}, bf16[4,256,256]{2,1,0:T(8,128)(2,1)}, bf16[4,256,256]{2,1,0:T(8,128)(2,1)}) custom-call(bf16[128,2048]{1,0:T(8,128)(2,1)} %fusion.24.refs_0_, bf16[2048,256]{1,0:T(8,128)(2,1)} %get-tuple-element.51.refs_4_.refs_1_, ...), custom_call_target="tpu_custom_call" | custom-call | flops 60000002048 | bytes 20000000 | tf_op jit(solution)/shard_map/attention_backward/pallas_call | solution.py:438
  812.6 84.5 %ffn_backward.3 = (f32[128,2048]{1,0:T(8,128)}, bf16[4,2,128,2048]{3,2,1,0:T(8,128)(2,1)}, bf16[4,256,1024]{2,1,0:T(8,128)(2,1)}) custom-call(bf16[128,2048]{1,0:T(8,128)(2,1)} %add_convert_fusion.1.refs_0_, bf16[2048,1024]{1,0:T(8,128)(2,1)} %get-tuple-element.55.refs_1_.refs_3_, bf16[1024,2048]{1,0:T(8,128)(2,1)} %bitcast.136, ...), custom_call_target="tpu_custom_call" | custom-call | flops 60000002048 | bytes 20000000 | tf_op jit(solution)/shard_map/ffn_backward/pallas_call | solution.py:438
  901.0 81.6 %attention_backward.3 = (f32[128,2048]{1,0:T(8,128)}, bf16[4,2,128,2048]{3,2,1,0:T(8,128)(2,1)}, bf16[4,256,256]{2,1,0:T(8,128)(2,1)}, bf16[4,256,256]{2,1,0:T(8,128)(2,1)}) custom-call(bf16[128,2048]{1,0:T(8,128)(2,1)} %fusion.25.refs_0_, bf16[2048,256]{1,0:T(8,128)(2,1)} %get-tuple-element.49.refs_1_.refs_4_, ...), custom_call_target="tpu_custom_call" | custom-call | flops 60000002048 | bytes 20000000 | tf_op jit(solution)/shard_map/attention_backward/pallas_call | solution.py:438
  1002.6 7.6 convolution_convert_fusion.3
  1034.0 36.6 %psum.15 = f32[2,4,256]{2,1,0:T(4,128)S(1)} all-reduce(f32[2,4,256]{2,1,0:T(4,128)S(1)} %copy.46), channel_id=1, replica_groups=mesh['section'=2,'ctx'=2,'dp'=8] {'section','ctx'}, use_global_device_ids=true, to_apply=%region_27.28 | all-reduce | flops 2048 | bytes 16384 | tf_op jit(solution)/shard_map/psum | solution.py:842
  1096.6 48.2 %collective-permute-done.7 = bf16[8,128,256]{2,1,0:T(8,128)(2,1)S(1)} collective-permute-done((bf16[8,128,256]{2,1,0:T(8,128)(2,1)S(1)}, bf16[8,128,256]{2,1,0:T(8,128)(2,1)S(1)}, u32[]{:S(2)}, u32[]{:S(2)}) %collective-permute-start.7) | collective-permute-done | bytes 524320 | tf_op jit(solution)/shard_map/ppermute | solution.py:726
  1144.8 5.3 collective-permute-start.1
  1169.6 5.2 add_select_fusion.1
  1174.8 10.8 collective-permute-done.13
  1186.4 5.4 collective-permute-start.4
  1206.5 27.8 %collective-permute-done.12 = bf16[128,2048]{1,0:T(8,128)(2,1)S(1)} collective-permute-done((bf16[128,2048]{1,0:T(8,128)(2,1)}, bf16[128,2048]{1,0:T(8,128)(2,1)S(1)}, u32[]{:S(2)}, u32[]{:S(2)}) %collective-permute-start.12) | collective-permute-done | bytes 524320 | tf_op jit(solution)/shard_map/ppermute | solution.py:726
  1244.4 5.9 collective-permute-done.15
  1254.8 51.9 %collective-permute-done.10 = bf16[128,2048]{1,0:T(8,128)(2,1)} collective-permute-done((bf16[128,2048]{1,0:T(8,128)(2,1)S(1)}, bf16[128,2048]{1,0:T(8,128)(2,1)}, u32[]{:S(2)}, u32[]{:S(2)}) %collective-permute-start.10) | collective-permute-done | bytes 524320 | tf_op jit(solution)/shard_map/ppermute | solution.py:731
  1311.2 43.6 %all-reduce.2.cloned.1.call-done = bf16[2,256,256]{2,1,0:T(8,128)(2,1)} async-done(((bf16[2,256,256]{2,1,0:T(8,128)(2,1)}), bf16[2,256,256]{2,1,0:T(8,128)(2,1)}) %all-reduce.2.cloned.1.call-update) | async-done | bytes 262160 | tf_op jit(solution)/shard_map/psum | solution.py:837
  (322 shorter events, 180.4 us)
Async XLA Ops:
  7.2 1025.6 %reduce-scatter.7.cloned.1.call-start = ((), (), s32[]{:S(2)}) async-start(), calls=%async_computation.6 | async-start | bytes 1179648
  9.3 608.1 %collective-permute-start.3 = (bf16[128,2048]{1,0:T(8,128)(2,1)}, bf16[128,2048]{1,0:T(8,128)(2,1)}, u32[]{:S(2)}, u32[]{:S(2)}) collective-permute-start(bf16[128,2048]{1,0:T(8,128)(2,1)} %dynamic-slice_bitcast_fusion), channel_id=1, source_target_pairs={{0,0},{1,8},{2,2},{3,10},{4,4},{5,12},{6,6},{7,14},{8,1},{9,9},{10... | collective-permute-start | bytes 1572872 | tf_op jit(solution)/shard_map/ppermute | solution.py:709
  15.7 267.0 %collective-permute-start = (bf16[128,2048]{1,0:T(8,128)(2,1)S(1)}, bf16[128,2048]{1,0:T(8,128)(2,1)S(1)}, u32[]{:S(2)}, u32[]{:S(2)}) collective-permute-start(bf16[128,2048]{1,0:T(8,128)(2,1)S(1)} %dynamic-slice_bitcast_fusion.1), channel_id=1, source_target_pairs={{0,0},{1,8},{2,2},{3,10},{4,4},{5,12},{6,6},{7,14},{8,1},{9,9},{10... | collective-permute-start | bytes 1572872 | tf_op jit(solution)/shard_map/ppermute | solution.py:709
  714.4 357.7 %collective-permute-start.18 = (bf16[8,128,1024]{2,1,0:T(8,128)(2,1)}, bf16[8,128,1024]{2,1,0:T(8,128)(2,1)}, u32[]{:S(2)}, u32[]{:S(2)}) collective-permute-start(bf16[8,128,1024]{2,1,0:T(8,128)(2,1)} %constant_dynamic-slice_fusion.4), channel_id=1, source_target_pairs={{0,8},{8,0},{1,9},{9,1},{2,10},{10,2},{3,11},{11,3},{4,12},{12,4},... | collective-permute-start | bytes 6291464 | tf_op jit(solution)/shard_map/ppermute | solution.py:725
  723.4 431.2 %collective-permute-start.23 = (bf16[512,2048]{1,0:T(8,128)(2,1)}, bf16[512,2048]{1,0:T(8,128)(2,1)}, u32[]{:S(2)}, u32[]{:S(2)}) collective-permute-start(bf16[512,2048]{1,0:T(8,128)(2,1)} %constant_dynamic-slice_fusion.2), channel_id=1, source_target_pairs={{0,8},{8,0},{1,9},{9,1},{2,10},{10,2},{3,11},{11,3},{4,12},{12,4},... | collective-permute-start | bytes 6291464 | tf_op jit(solution)/shard_map/ppermute | solution.py:725
  996.9 73.7 %collective-permute-start.8 = (bf16[8,128,256]{2,1,0:T(8,128)(2,1)}, bf16[8,128,256]{2,1,0:T(8,128)(2,1)}, u32[]{:S(2)}, u32[]{:S(2)}) collective-permute-start(bf16[8,128,256]{2,1,0:T(8,128)(2,1)} %constant_dynamic-slice_fusion.8), channel_id=1, source_target_pairs={{0,8},{8,0},{1,9},{9,1},{2,10},{10,2},{3,11},{11,3},{4,12},{12,4},... | collective-permute-start | bytes 1572872 | tf_op jit(solution)/shard_map/ppermute | solution.py:725
  997.9 86.2 %collective-permute-start.6 = (bf16[8,128,256]{2,1,0:T(8,128)(2,1)}, bf16[8,128,256]{2,1,0:T(8,128)(2,1)}, u32[]{:S(2)}, u32[]{:S(2)}) collective-permute-start(bf16[8,128,256]{2,1,0:T(8,128)(2,1)} %constant_dynamic-slice_fusion.9), channel_id=1, source_target_pairs={{0,8},{8,0},{1,9},{9,1},{2,10},{10,2},{3,11},{11,3},{4,12},{12,4},... | collective-permute-start | bytes 1572872 | tf_op jit(solution)/shard_map/ppermute | solution.py:725
  1002.3 306.2 %reduce-scatter.5.cloned.1.call-start = ((), (), s32[]{:S(2)}) async-start(), calls=%async_computation.4 | async-start | bytes 2359296 | tf_op jit(solution)/shard_map/reduce_scatter | solution.py:834
  1013.3 65.4 %collective-permute-start.16 = (bf16[8,128,1024]{2,1,0:T(8,128)(2,1)}, bf16[8,128,1024]{2,1,0:T(8,128)(2,1)S(1)}, u32[]{:S(2)}, u32[]{:S(2)}) collective-permute-start(bf16[8,128,1024]{2,1,0:T(8,128)(2,1)} %constant_dynamic-slice_fusion.5), channel_id=1, source_target_pairs={{0,8},{8,0},{1,9},{9,1},{2,10},{10,2},{3,11},{11,3},{4,12},{12,4},... | collective-permute-start | bytes 6291464 | tf_op jit(solution)/shard_map/ppermute | solution.py:725
  1072.2 85.7 %collective-permute-start.21 = (bf16[512,2048]{1,0:T(8,128)(2,1)}, bf16[512,2048]{1,0:T(8,128)(2,1)}, u32[]{:S(2)}, u32[]{:S(2)}) collective-permute-start(bf16[512,2048]{1,0:T(8,128)(2,1)} %constant_dynamic-slice_fusion.3), channel_id=1, source_target_pairs={{0,8},{8,0},{1,9},{9,1},{2,10},{10,2},{3,11},{11,3},{4,12},{12,4},... | collective-permute-start | bytes 6291464 | tf_op jit(solution)/shard_map/ppermute | solution.py:725
  1084.2 79.3 %collective-permute-start.19 = (bf16[8,128,1024]{2,1,0:T(8,128)(2,1)}, bf16[8,128,1024]{2,1,0:T(8,128)(2,1)}, u32[]{:S(2)}, u32[]{:S(2)}) collective-permute-start(bf16[8,128,1024]{2,1,0:T(8,128)(2,1)} %dynamic-slice_add_fusion.2), channel_id=1, source_target_pairs={{0,16},{1,17},{2,18},{3,19},{4,20},{5,21},{6,22},{7,23},{8,24},{9,... | collective-permute-start | bytes 6291464 | tf_op jit(solution)/shard_map/ppermute | solution.py:726
  1086.8 81.6 %collective-permute-start.17 = (bf16[8,128,1024]{2,1,0:T(8,128)(2,1)}, bf16[8,128,1024]{2,1,0:T(8,128)(2,1)}, u32[]{:S(2)}, u32[]{:S(2)}) collective-permute-start(bf16[8,128,1024]{2,1,0:T(8,128)(2,1)} %dynamic-slice_add_fusion.3), channel_id=1, source_target_pairs={{16,0},{17,1},{18,2},{19,3},{20,4},{21,5},{22,6},{23,7},{24,8},{25... | collective-permute-start | bytes 6291464 | tf_op jit(solution)/shard_map/ppermute | solution.py:726
  1093.8 51.0 %collective-permute-start.7 = (bf16[8,128,256]{2,1,0:T(8,128)(2,1)S(1)}, bf16[8,128,256]{2,1,0:T(8,128)(2,1)S(1)}, u32[]{:S(2)}, u32[]{:S(2)}) collective-permute-start(bf16[8,128,256]{2,1,0:T(8,128)(2,1)S(1)} %dynamic-slice_add_fusion.7), channel_id=1, source_target_pairs={{16,0},{17,1},{18,2},{19,3},{20,4},{21,5},{22,6},{23,7},{24,8},{25... | collective-permute-start | bytes 1572872 | tf_op jit(solution)/shard_map/ppermute | solution.py:726
  1151.1 40.7 %all-to-all-start = ((bf16[8,128,256]{2,1,0:T(8,128)(2,1)}), bf16[8,128,256]{2,1,0:T(8,128)(2,1)S(1)}, u32[]{:S(2)}, u32[]{:S(2)}) async-start(bf16[8,128,256]{2,1,0:T(8,128)(2,1)} %add_select_fusion.3), calls=%async_computation | async-start | bytes 1048576 | tf_op jit(solution)/shard_map/all_to_all | solution.py:831
  1154.6 43.4 %collective-permute-start.2 = (bf16[128,2048]{1,0:T(8,128)(2,1)}, bf16[128,2048]{1,0:T(8,128)(2,1)S(1)}, u32[]{:S(2)}, u32[]{:S(2)}) collective-permute-start(bf16[128,2048]{1,0:T(8,128)(2,1)} %get-tuple-element.147), channel_id=1, source_target_pairs={{0,16},{1,24},{2,18},{3,26},{4,20},{5,28},{6,22},{7,30},{8,17},{9,... | collective-permute-start | bytes 1572872 | tf_op jit(solution)/shard_map/ppermute | solution.py:717
  1157.9 41.4 %collective-permute-start.5 = (bf16[128,2048]{1,0:T(8,128)(2,1)}, bf16[128,2048]{1,0:T(8,128)(2,1)}, u32[]{:S(2)}, u32[]{:S(2)}) collective-permute-start(bf16[128,2048]{1,0:T(8,128)(2,1)} %broadcast_select_fusion), channel_id=1, source_target_pairs={{0,16},{1,24},{2,18},{3,26},{4,20},{5,28},{6,22},{7,30},{8,17},{9,... | collective-permute-start | bytes 1572872 | tf_op jit(solution)/shard_map/ppermute | solution.py:717
  1163.5 72.0 %collective-permute-start.24 = (bf16[512,2048]{1,0:T(8,128)(2,1)S(1)}, bf16[512,2048]{1,0:T(8,128)(2,1)}, u32[]{:S(2)}, u32[]{:S(2)}) collective-permute-start(bf16[512,2048]{1,0:T(8,128)(2,1)S(1)} %dynamic-slice_add_fusion), channel_id=1, source_target_pairs={{0,16},{1,17},{2,18},{3,19},{4,20},{5,21},{6,22},{7,23},{8,24},{9,... | collective-permute-start | bytes 6291464 | tf_op jit(solution)/shard_map/ppermute | solution.py:726
  1168.4 67.2 %collective-permute-start.22 = (bf16[512,2048]{1,0:T(8,128)(2,1)}, bf16[512,2048]{1,0:T(8,128)(2,1)}, u32[]{:S(2)}, u32[]{:S(2)}) collective-permute-start(bf16[512,2048]{1,0:T(8,128)(2,1)} %dynamic-slice_add_fusion.1), channel_id=1, source_target_pairs={{16,0},{17,1},{18,2},{19,3},{20,4},{21,5},{22,6},{23,7},{24,8},{25... | collective-permute-start | bytes 6291464 | tf_op jit(solution)/shard_map/ppermute | solution.py:726
  1191.8 59.4 %all-to-all-start.1 = ((bf16[8,128,1024]{2,1,0:T(8,128)(2,1)}), bf16[8,128,1024]{2,1,0:T(8,128)(2,1)}, u32[]{:S(2)}, u32[]{:S(2)}) async-start(bf16[8,128,1024]{2,1,0:T(8,128)(2,1)} %add_select_fusion.1), calls=%async_computation.2 | async-start | bytes 4194304 | tf_op jit(solution)/shard_map/all_to_all | solution.py:831
  1196.6 158.2 %all-reduce.2.cloned.1.call-start = ((), (), s32[]{:S(2)}) async-start(), calls=%async_computation.5 | async-start | bytes 524288 | tf_op jit(solution)/shard_map/psum | solution.py:837
  1198.0 36.3 %collective-permute-start.12 = (bf16[128,2048]{1,0:T(8,128)(2,1)}, bf16[128,2048]{1,0:T(8,128)(2,1)S(1)}, u32[]{:S(2)}, u32[]{:S(2)}) collective-permute-start(bf16[128,2048]{1,0:T(8,128)(2,1)} %dynamic-slice_add_fusion.5), channel_id=1, source_target_pairs={{16,0},{17,1},{18,2},{19,3},{20,4},{21,5},{22,6},{23,7},{24,8},{25... | collective-permute-start | bytes 1572872 | tf_op jit(solution)/shard_map/ppermute | solution.py:726
  1240.2 116.3 %collective-permute-start.25 = (bf16[512,2048]{1,0:T(8,128)(2,1)}, bf16[512,2048]{1,0:T(8,128)(2,1)}, u32[]{:S(2)}, u32[]{:S(2)}) collective-permute-start(bf16[512,2048]{1,0:T(8,128)(2,1)} %add_select_fusion), channel_id=1, source_target_pairs={{0,8},{8,0},{1,9},{9,1},{2,10},{10,2},{3,11},{11,3},{4,12},{12,4},... | collective-permute-start | bytes 6291464 | tf_op jit(solution)/shard_map/ppermute | solution.py:731
  1244.3 62.3 %collective-permute-start.10 = (bf16[128,2048]{1,0:T(8,128)(2,1)S(1)}, bf16[128,2048]{1,0:T(8,128)(2,1)}, u32[]{:S(2)}, u32[]{:S(2)}) collective-permute-start(bf16[128,2048]{1,0:T(8,128)(2,1)S(1)} %bitcast.137), channel_id=1, source_target_pairs={{0,8},{8,0},{1,9},{9,1},{2,10},{10,2},{3,11},{11,3},{4,12},{12,4},... | collective-permute-start | bytes 1572872 | tf_op jit(solution)/shard_map/ppermute | solution.py:731
  1253.1 110.1 %collective-permute-start.20 = (bf16[128,8192]{1,0:T(8,128)(2,1)S(1)}, bf16[128,8192]{1,0:T(8,128)(2,1)}, u32[]{:S(2)}, u32[]{:S(2)}) collective-permute-start(bf16[128,8192]{1,0:T(8,128)(2,1)S(1)} %bitcast.125), channel_id=1, source_target_pairs={{0,8},{8,0},{1,9},{9,1},{2,10},{10,2},{3,11},{11,3},{4,12},{12,4},... | collective-permute-start | bytes 6291464 | tf_op jit(solution)/shard_map/ppermute | solution.py:731
  (89 other events, 2910.2 us)
Sparse Core Ops, SparseCore 0:
  1002.5 30.3 reduce-scatter.6
  1035.7 34.4 reduce-scatter.4
  1308.7 46.0 all-reduce.1

commit v4 on v3

--- a/solution.py
+++ b/solution.py
@@ -189,21 +189,34 @@
     lax.fori_loop(0, w_query.shape[0] // size, back_tile, 0)
 
 
-def pass_kernel(compute, n_weights, n_ins, n_outs, places, *refs):
+def half_of(ref, which):
+    half = ref.shape[-2] // 2
+    at = pl.ds(pl.multiple_of(which * half, half), half)
+    return ref.at[at] if len(ref.shape) == 2 else ref.at[:, at]
+
+
+def half_shape(shape):
+    return shape[:-2] + (shape[-2] // 2, shape[-1])
+
+
+def pass_kernel(compute, n_weights, n_ins, n_outs, places, side_axes, *refs):
     refs = list(refs)
     take = lambda count: [refs.pop(0) for _ in range(count)]
     (x_ref,) = take(1)
     early_weights = take(n_weights)
     late_weights = take(n_weights)
     ins = take(n_ins)
+    side_from = take(len(side_axes))
     y_ref, gath = take(2)
     outs = take(n_outs)
+    side_to = take(len(side_axes))
     weights = take(n_weights)
     part, partner_out, partner_in, total, line_out, from_left, from_right = take(7)
     (
         weight_sem, gather_right, gather_left, gather_partner, gather_line_in, gather_partner_in,
         partner_send, partner_recv, right_send, right_recv, left_send, left_recv,
-    ) = take(12)
+        side_send, side_recv,
+    ) = take(14)
 
     section = lax.axis_index("section")
     me = lax.axis_index("dp")
@@ -239,8 +252,23 @@
         def _():
             pltpu.make_async_copy(late_weights[index], weights[index], weight_sem.at[index]).start()
 
-    peers = 1 + jnp.where(has_left, 1, 0) + jnp.where(has_right, 1, 0)
+    far = {"ctx": 1 - lax.axis_index("ctx"), "section": 1 - section}
+    for axis in sorted(set(side_axes)):
+        pl.semaphore_signal(barrier, inc=1, device_id={axis: far[axis]}, device_id_type=MESH)
+    peers = 1 + len(set(side_axes)) + jnp.where(has_left, 1, 0) + jnp.where(has_right, 1, 0)
     pl.semaphore_wait(barrier, peers)
+
+    sides = []
+    for index, axis in enumerate(side_axes):
+        source, target = side_from[index], side_to[index]
+        if axis == "ctx":
+            source = half_of(source, far["ctx"])
+        sides.append(
+            pltpu.make_async_remote_copy(
+                source, target, side_send.at[index], side_recv.at[index],
+                device_id={axis: far[axis]}, device_id_type=MESH,
+            )
+        )
 
     def cut(index):
         return pl.ds(index * size, size)
@@ -294,6 +322,8 @@
             to_left(z, index, x_ref.at[cut(index)]).start()
 
     to_partner(z, x_ref).start()
+    for copy in sides:
+        copy.start()
     gath[z, k] = x_ref[...]
 
     at_end = (z == 0) | (z == last)
@@ -425,26 +455,34 @@
         return carry
 
     lax.fori_loop(0, places, drain, 0)
-
-
-def tensor_pass(compute, name, ident, x, early_weights, late_weights, ins, out_widths):
+    for copy in sides:
+        copy.wait()
+
+
+def tensor_pass(compute, ident, x, early_weights, late_weights, ins, out_widths, sides=()):
     rows, width = x.shape
     places = lax.axis_size("dp") // 2
     vmem = pl.BlockSpec(memory_space=pltpu.VMEM)
     hbm = pl.BlockSpec(memory_space=pl.ANY)
     count = len(early_weights)
     dma = pltpu.SemaphoreType.DMA
-    kernel = functools.partial(pass_kernel, compute, count, len(ins), len(out_widths), places)
-    return pl.pallas_call(
+    axes = [axis for axis, _ in sides]
+    moved = [
+        half_shape(array.shape) if axis == "ctx" else array.shape for axis, array in sides
+    ]
+    kernel = functools.partial(
+        pass_kernel, compute, count, len(ins), len(out_widths), places, axes
+    )
+    call = pl.pallas_call(
         kernel,
-        name=name,
         out_shape=[
             jax.ShapeDtypeStruct((rows, width), jnp.float32),
             jax.ShapeDtypeStruct((places, 2, rows, width), jnp.bfloat16),
         ]
-        + [jax.ShapeDtypeStruct((places, 2 * rows, out), jnp.bfloat16) for out in out_widths],
-        in_specs=[vmem] + [hbm] * (2 * count) + [vmem] * len(ins),
-        out_specs=[vmem] * (2 + len(out_widths)),
+        + [jax.ShapeDtypeStruct((places, 2 * rows, out), jnp.bfloat16) for out in out_widths]
+        + [jax.ShapeDtypeStruct(shape, jnp.bfloat16) for shape in moved],
+        in_specs=[vmem] + [hbm] * (2 * count) + [vmem] * len(ins) + [hbm] * len(axes),
+        out_specs=[vmem] * (2 + len(out_widths)) + [hbm] * len(axes),
         scratch_shapes=[pltpu.VMEM(weight.shape, weight.dtype) for weight in early_weights]
         + [
             pltpu.VMEM((2, rows, width), jnp.float32),
@@ -466,6 +504,8 @@
             dma((places, PARTS)),
             dma((places, PARTS)),
             dma((places, PARTS)),
+            dma((max(len(axes), 1),)),
+            dma((max(len(axes), 1),)),
         ],
         cost_estimate=pl.CostEstimate(
             flops=60_000_000_000, bytes_accessed=20_000_000, transcendentals=0
@@ -473,13 +513,18 @@
         compiler_params=pltpu.CompilerParams(
             collective_id=ident, has_side_effects=True, vmem_limit_bytes=60 * 1024 * 1024
         ),
-    )(x, *early_weights, *late_weights, *ins)
+    )
+    return call(
+        x, *early_weights, *late_weights, *ins, *[array for _, array in sides]
+    )
 
 
 def distribute_kernel(
-    places, query, keyvalue, out, up, down,
-    query_own, keyvalue_own, up_own, query_far, keyvalue_far, out_far, up_far, down_far,
-    local_sem, query_send, query_recv, keyvalue_send, keyvalue_recv, up_send, up_recv,
+    places, query, keyvalue, notes, out, up, down,
+    query_own, keyvalue_own, notes_own, up_own,
+    query_far, keyvalue_far, notes_far, out_far, up_far, down_far,
+    local_sem, query_send, query_recv, keyvalue_send, keyvalue_recv, notes_send, notes_recv,
+    up_send, up_recv,
     across_send, across_recv, over_send, over_recv,
 ):
     section = lax.axis_index("section")
@@ -514,9 +559,9 @@
             source, target, send, recv, device_id=device, device_id_type=MESH
         )
 
-    def piece(owner, part):
+    def piece(owner, part, count):
         which = jnp.where(part == 0, ctx, 1 - ctx)
-        return pl.ds(pl.multiple_of(owner * rows + which * half, half), half)
+        return tile_at(2 * owner + which, count // 2)
 
     def query_copy(source, to):
         return remote(
@@ -530,11 +575,17 @@
             keyvalue_send.at[to], keyvalue_recv.at[source], {"dp": to},
         )
 
+    def notes_copy(source, to):
+        return remote(
+            notes, notes_own.at[tile_at(source, notes.shape[0])],
+            notes_send.at[to], notes_recv.at[source], {"dp": to},
+        )
+
     def up_copy(source, to, part):
         which = jnp.where(part == 0, ctx, 1 - ctx)
         return remote(
             up.at[tile_at(which, half), tile_at(to, unit_width)],
-            up_own.at[piece(source, part)],
+            up_own.at[piece(source, part, rows)],
             up_send.at[to, part], up_recv.at[source, part], {"dp": to},
         )
 
@@ -553,21 +604,23 @@
             query.at[:, tile_at(me, head_width)], query_own.at[tile_at(me, rows)], local_sem.at[0]
         ),
         pltpu.make_async_copy(keyvalue, keyvalue_own.at[tile_at(me, rows)], local_sem.at[1]),
+        pltpu.make_async_copy(notes, notes_own.at[tile_at(me, notes.shape[0])], local_sem.at[2]),
         pltpu.make_async_copy(
-            up.at[:, tile_at(me, unit_width)], up_own.at[tile_at(me, rows)], local_sem.at[2]
+            up.at[:, tile_at(me, unit_width)], up_own.at[tile_at(me, rows)], local_sem.at[3]
         ),
     ]
     for copy in local:
         copy.start()
+    peers(lambda to: notes_copy(me, to).start())
     peers(lambda to: query_copy(me, to).start())
     peers(lambda to: keyvalue_copy(me, to).start())
     peers(lambda to: up_copy(me, to, 0).start())
 
+    pieces = 2 * places
     out_half = tile_at(ctx, out.shape[0] // 2)
-    quarter = down.shape[0] // 4
+    short = down.shape[0] // 2 // pieces
     flows = [(out, out_far, out_half)] + [
-        (down, down_far, pl.ds(pl.multiple_of((2 * ctx + index) * quarter, quarter), quarter))
-        for index in range(2)
+        (down, down_far, tile_at(pieces * ctx + index, short)) for index in range(pieces)
     ]
 
     def flow_across(slot):
@@ -577,85 +630,93 @@
         )
 
     def flow_over(slot):
-        source, target, at = flows[slot]
+        _, target, at = flows[slot]
         return remote(target.at[at], target.at[at], over_send.at[slot], over_recv.at[slot], over)
 
     first_slot = len(flows)
-    kinds = [(query_own, query_far), (keyvalue_own, keyvalue_far), (up_own, up_far)]
+    kinds = [
+        (notes_own, notes_far, notes.shape[0]),
+        (query_own, query_far, rows),
+        (keyvalue_own, keyvalue_far, rows),
+        (up_own, up_far, rows),
+    ]
 
     def block_across(kind, owner):
-        own, far = kinds[kind]
+        own, far, count = kinds[kind]
         slot = first_slot + kind * 2 * places + owner
-        at = piece(owner, 0)
+        at = piece(owner, 0, count)
         return remote(own.at[at], far.at[at], across_send.at[slot], across_recv.at[slot], across)
 
     def block_over(kind, owner):
-        own, far = kinds[kind]
+        _, far, count = kinds[kind]
         slot = first_slot + kind * 2 * places + owner
-        at = piece(owner, 0)
+        at = piece(owner, 0, count)
         return remote(far.at[at], far.at[at], over_send.at[slot], over_recv.at[slot], over)
 
-    flow_across(0).start()
-
-    local[0].wait()
-    local[1].wait()
+    for slot in range(first_slot):
+        flow_across(slot).start()
+    peers(lambda to: up_copy(me, to, 1).start())
+
+    def hand_over(slot):
+        flow_across(slot).wait_recv()
+        flow_over(slot).start()
+
+    for index in range(3):
+        local[index].wait()
     block_across(0, me).start()
     block_across(1, me).start()
-
-    def pass_small(source):
+    block_across(2, me).start()
+    hand_over(0)
+
+    def pass_query(source):
+        notes_copy(source, me).wait_recv()
+        block_across(0, source).start()
         query_copy(source, me).wait_recv()
-        block_across(0, source).start()
+        block_across(1, source).start()
+
+    def pass_keyvalue(source):
         keyvalue_copy(source, me).wait_recv()
-        block_across(1, source).start()
-
-    peers(pass_small)
-    peers(lambda to: up_copy(me, to, 1).start())
-    flow_across(1).start()
-    flow_across(0).wait_recv()
-    flow_over(0).start()
-    local[2].wait()
-    block_across(2, me).start()
+        block_across(2, source).start()
+
+    peers(pass_query)
+    for slot in range(1, 1 + pieces // 2):
+        hand_over(slot)
+    peers(pass_keyvalue)
+    for slot in range(1 + pieces // 2, first_slot):
+        hand_over(slot)
+    local[3].wait()
+    block_across(3, me).start()
 
     def pass_up(source):
         up_copy(source, me, 0).wait_recv()
-        block_across(2, source).start()
+        block_across(3, source).start()
 
     peers(pass_up)
-    flow_across(2).start()
-
-    def over_small(owner, carry):
-        block_across(0, owner).wait_recv()
-        block_over(0, owner).start()
-        block_across(1, owner).wait_recv()
-        block_over(1, owner).start()
-        return carry
-
-    lax.fori_loop(0, 2 * places, over_small, 0)
-    flow_across(1).wait_recv()
-    flow_over(1).start()
-
-    def over_up(owner, carry):
-        block_across(2, owner).wait_recv()
-        block_over(2, owner).start()
-        return carry
-
-    lax.fori_loop(0, 2 * places, over_up, 0)
-    flow_across(2).wait_recv()
-    flow_over(2).start()
+
+    def over_block(kind):
+        def move(owner, carry):
+            block_across(kind, owner).wait_recv()
+            block_over(kind, owner).start()
+            return carry
+
+        lax.fori_loop(0, 2 * places, move, 0)
+
+    for kind in range(len(kinds)):
+        over_block(kind)
 
     peers(lambda source: up_copy(source, me, 1).wait_recv())
 
     def over_wait(slot_owner, carry):
-        for kind in range(3):
+        for kind in range(len(kinds)):
             block_over_in(kind, slot_owner).wait_recv()
             block_across(kind, slot_owner).wait_send()
             block_over(kind, slot_owner).wait_send()
         return carry
 
     def block_over_in(kind, owner):
-        own, far = kinds[kind]
+        _, far, count = kinds[kind]
         slot = first_slot + kind * 2 * places + owner
-        at = piece(owner, 1)
+        at = piece(owner, 1, count)
         return remote(far.at[at], far.at[at], over_send.at[slot], over_recv.at[slot], over)
 
     lax.fori_loop(0, 2 * places, over_wait, 0)
@@ -665,6 +726,7 @@
         flow_over(slot).wait_send()
 
     def sent(to):
+        notes_copy(me, to).wait_send()
         query_copy(me, to).wait_send()
         keyvalue_copy(me, to).wait_send()
         up_copy(me, to, 0).wait_send()
@@ -673,27 +735,385 @@
     peers(sent)
 
 
-def distribute(query, keyvalue, out, up, down):
+def distribute(query, keyvalue, notes, out, up, down):
     size = lax.axis_size("dp")
     places = size // 2
     hbm = pl.BlockSpec(memory_space=pl.ANY)
     dma = pltpu.SemaphoreType.DMA
     rows = query.shape[0] * size
-    turned = [(rows, query.shape[1] // size), (rows, keyvalue.shape[1]), (rows, up.shape[1] // size)]
-    shapes = turned + turned[:2] + [out.shape, turned[2], down.shape]
-    slots = 3 + 3 * size
+    small = [
+        (rows, query.shape[1] // size),
+        (rows, keyvalue.shape[1]),
+        (notes.shape[0] * size, notes.shape[1]),
+    ]
+    turned = (rows, up.shape[1] // size)
+    shapes = small + [turned] + small + [out.shape, turned, down.shape]
+    slots = 1 + 5 * size
     return pl.pallas_call(
         functools.partial(distribute_kernel, places),
         name="distribute",
         out_shape=[jax.ShapeDtypeStruct(shape, jnp.bfloat16) for shape in shapes],
-        in_specs=[hbm] * 5,
-        out_specs=[hbm] * 8,
-        scratch_shapes=[dma((3,))]
-        + [dma((size,))] * 4
+        in_specs=[hbm] * 6,
+        out_specs=[hbm] * len(shapes),
+        scratch_shapes=[dma((4,))]
+        + [dma((size,))] * 6
         + [dma((size, 2))] * 2
         + [dma((slots,))] * 4,
+        cost_estimate=pl.CostEstimate(
+            flops=150_000_000_000, bytes_accessed=20_000_000, transcendentals=0
+        ),
         compiler_params=pltpu.CompilerParams(collective_id=4, has_side_effects=True),
-    )(query, keyvalue, out, up, down)
+    )(query, keyvalue, notes, out, up, down)
+
+
+def collect_kernel(
+    places, up_full, down_full, query_full, out_full, up_moved, down_moved,
+    up_late, down_late, query_late, out_late, up_far, down_far, query_far, out_far, small,
+    up_out, down_out, query_out, out_out, small_out,
+    small_in, small_sum, small_far, small_total, small_side,
+    up, up_in, up_part, up_side, down, down_in, down_part, down_side,
+    query, query_in, query_part, query_side, out, out_in, out_part, out_side,
+    local_sem, side_send, side_recv, across_send, across_recv,
+    turn_send, turn_recv, over_send, over_recv, small_send, small_recv,
+):
+    section = lax.axis_index("section")
+    ctx = lax.axis_index("ctx")
+    me = lax.axis_index("dp")
+    z = me // 2
+    k = me % 2
+    last = places - 1
+    size = 2 * places
+    early = section == 0
+    late = section != 0
+    across = {"section": 1 - section}
+    over = {"ctx": 1 - ctx}
+    chunks = 4
+    short = down.shape[0] // chunks
+    turned = [(up, up_out), (query, query_out)]
+    half = up.shape[1]
+
+    def peers(act):
+        act(2 * z + 1 - k)
+        for away in range(1, places):
+
+            @pl.when(z + away <= last)
+            def _():
+                act(2 * (z + away) + k)
+                act(2 * (z + away) + 1 - k)
+
+            @pl.when(z - away >= 0)
+            def _():
+                act(2 * (z - away) + k)
+                act(2 * (z - away) + 1 - k)
+
+    def remote(source, target, send, recv, device):
+        return pltpu.make_async_remote_copy(
+            source, target, send, recv, device_id=device, device_id_type=MESH
+        )
+
+    barrier = pltpu.get_barrier_semaphore()
+
+    def greet(to):
+        pl.semaphore_signal(barrier, inc=1, device_id={"dp": to}, device_id_type=MESH)
+
+    peers(greet)
+    pl.semaphore_signal(barrier, inc=1, device_id=across, device_id_type=MESH)
+    pl.semaphore_signal(barrier, inc=1, device_id=over, device_id_type=MESH)
+    pl.semaphore_wait(barrier, size + 1)
+
+    side = [
+        remote(half_of(query_full, 1 - ctx), query_side, side_send.at[0], side_recv.at[0], over),
+        remote(half_of(out_full, 1 - ctx), out_side, side_send.at[1], side_recv.at[1], over),
+    ]
+    for copy in side:
+        copy.start()
+
+    def small_turn(source, to, layer):
+        return remote(
+            small.at[layer, to], small_in.at[layer, source],
+            small_send.at[layer, to], small_recv.at[layer, source], {"dp": to},
+        )
+
+    own_small = [
+        pltpu.make_async_copy(
+            small.at[layer, me], small_in.at[layer, me], local_sem.at[13 + layer]
+        )
+        for layer in range(2)
+    ]
+    for layer in range(2):
+        own_small[layer].start()
+
+    def small_start(to):
+        for layer in range(2):
+            small_turn(me, to, layer).start()
+
+    def small_wait(source):
+        for layer in range(2):
+            small_turn(source, me, layer).wait_recv()
+
+    def small_sent(to):
+        for layer in range(2):
+            small_turn(me, to, layer).wait_send()
+
+    small_across = remote(
+        small_sum.at[1 - section], small_far, across_send.at[size + 6], across_recv.at[size + 6],
+        across,
+    )
+    small_over = remote(small_total, small_side, side_send.at[2], side_recv.at[2], over)
+
+    def up_across(owner):
+        return remote(
+            up_part.at[owner], up_in.at[owner], across_send.at[owner], across_recv.at[owner], across
+        )
+
+    def down_across(index):
+        slot = size + index
+        at = pl.ds(index * short, short)
+        return remote(
+            down_part.at[at], down_in.at[at], across_send.at[slot], across_recv.at[slot], across
+        )
+
+    query_across = remote(
+        query_part, query_in, across_send.at[size + chunks], across_recv.at[size + chunks], across
+    )
+    out_across = remote(
+        out_part, out_in, across_send.at[size + chunks + 1], across_recv.at[size + chunks + 1],
+        across,
+    )
+
+    def load(index, source, target):
+        copy = pltpu.make_async_copy(source, target, local_sem.at[index])
+        copy.start()
+        return copy
+
+    loads = [
+        load(0, half_of(up_full, ctx), up_part),
+        load(1, up_moved, up_side),
+        load(2, half_of(query_full, ctx), query_part),
+        load(3, half_of(out_full, ctx), out_part),
+        load(4, half_of(down_full, ctx), down_part),
+        load(5, down_moved, down_side),
+    ]
+    owned = [
+        (up_late, up), (up_far, up_in), (query_late, query), (query_far, query_in),
+        (out_late, out), (out_far, out_in), (down_late, down), (down_far, down_in),
+    ]
+
+    @pl.when(late)
+    def _():
+        for index, (source, target) in enumerate(owned):
+            load(15 + index, source, target)
+
+    loads[0].wait()
+    loads[1].wait()
+
+    def send_up(owner):
+        up_part[owner] = up_part[owner] + up_side[owner]
+
+        @pl.when(late)
+        def _():
+            up_across(owner).start()
+
+    peers(send_up)
+    send_up(me)
+    loads[2].wait()
+    loads[3].wait()
+    for copy in side:
+        copy.wait_recv()
+    query_part[...] = query_part[...] + query_side[...]
+    out_part[...] = out_part[...] + out_side[...]
+    loads[4].wait()
+    loads[5].wait()
+    down_part[...] = down_part[...] + down_side[...]
+
+    @pl.when(late)
+    def _():
+        query_across.start()
+        out_across.start()
+        for index in range(chunks):
+            down_across(index).start()
+        for index, (source, target) in enumerate(owned):
+            pltpu.make_async_copy(source, target, local_sem.at[15 + index]).wait()
+
+    def turn(kind, source, to):
+        block, target = turned[kind]
+        width = block.shape[2]
+        at = kind * size
+        return remote(
+            block.at[to], target.at[tile_at(ctx, half), tile_at(source, width)],
+            turn_send.at[at + to], turn_recv.at[at + source], {"dp": to},
+        )
+
+    def own_block(kind):
+        block, target = turned[kind]
+        return pltpu.make_async_copy(
+            block.at[me], target.at[tile_at(ctx, half), tile_at(me, block.shape[2])],
+            local_sem.at[6 + kind],
+        )
+
+    def hand_over(kind, source, side_of):
+        block, target = turned[kind]
+        at = kind * size + source
+        region = target.at[tile_at(side_of, half), tile_at(source, block.shape[2])]
+        return remote(region, region, over_send.at[at], over_recv.at[at], over)
+
+    def sum_up(owner):
+        @pl.when(early)
+        def _():
+            up_across(owner).wait_recv()
+            up[owner] = up_part[owner] + up_in[owner]
+
+        @pl.when(late)
+        def _():
+            up[owner] = up[owner] + up_in[owner]
+
+    def up_block(owner):
+        sum_up(owner)
+        turn(0, me, owner).start()
+
+    def arrived(kind):
+        def act(source):
+            turn(kind, source, me).wait_recv()
+            hand_over(kind, source, ctx).start()
+
+        return act
+
+    peers(up_block)
+    sum_up(me)
+    peers(small_start)
+    own_block(0).start()
+    peers(arrived(0))
+    own_block(0).wait()
+    hand_over(0, me, ctx).start()
+
+    @pl.when(early)
+    def _():
+        query_across.wait_recv()
+        query[...] = query_part[...] + query_in[...]
+        out_across.wait_recv()
+        out[...] = out_part[...] + out_in[...]
+
+    @pl.when(late)
+    def _():
+        query[...] = query[...] + query_in[...]
+        out[...] = out[...] + out_in[...]
+
+    peers(lambda owner: turn(1, me, owner).start())
+    own_block(1).start()
+
+    def flat_over(index, side_of):
+        slot = 2 * size + index
+        if index == 0:
+            source, target, at = out, out_out, tile_at(side_of, out.shape[0])
+            return remote(source, target.at[at], over_send.at[slot], over_recv.at[slot], over), (
+                pltpu.make_async_copy(source, target.at[at], local_sem.at[8])
+            )
+        source = down.at[pl.ds((index - 1) * short, short)]
+        target = down_out.at[tile_at(side_of * chunks + index - 1, short)]
+        return remote(source, target, over_send.at[slot], over_recv.at[slot], over), (
+            pltpu.make_async_copy(source, target, local_sem.at[8 + index])
+        )
+
+    for copy in flat_over(0, ctx):
+        copy.start()
+    for index in range(chunks):
+
+        @pl.when(early)
+        def _():
+            at = pl.ds(index * short, short)
+            down_across(index).wait_recv()
+            down[at] = down_part[at] + down_in[at]
+
+        @pl.when(late)
+        def _():
+            at = pl.ds(index * short, short)
+            down[at] = down[at] + down_in[at]
+
+        for copy in flat_over(1 + index, ctx):
+            copy.start()
+    peers(arrived(1))
+    own_block(1).wait()
+    hand_over(1, me, ctx).start()
+    for layer in range(2):
+        own_small[layer].wait()
+    peers(small_wait)
+    for layer in range(2):
+        total = small_in[layer, 0].astype(jnp.float32)
+        for source in range(1, size):
+            total = total + small_in[layer, source].astype(jnp.float32)
+        small_sum[layer] = total.astype(jnp.bfloat16)
+    small_across.start()
+
+
+    small_across.wait_recv()
+    small_total[...] = small_sum[section] + small_far[...]
+    small_over.start()
+    small_over.wait_recv()
+    small_out[...] = (small_total[...] + small_side[...]).astype(jnp.float32)
+
+    peers(small_sent)
+    small_across.wait_send()
+    small_over.wait_send()
+    for copy in side:
+        copy.wait_send()
+
+    @pl.when(late)
+    def _():
+        peers(lambda owner: up_across(owner).wait_send())
+        up_across(me).wait_send()
+        query_across.wait_send()
+        out_across.wait_send()
+        for index in range(chunks):
+            down_across(index).wait_send()
+
+    for kind in range(2):
+        peers(lambda owner: turn(kind, me, owner).wait_send())
+
+        def finish(source, carry):
+            hand_over(kind, source, ctx).wait_send()
+            hand_over(kind, source, 1 - ctx).wait_recv()
+            return carry
+
+        lax.fori_loop(0, size, finish, 0)
+    for index in range(1 + chunks):
+        moved, kept = flat_over(index, ctx)
+        kept.wait()
+        moved.wait_send()
+        flat_over(index, 1 - ctx)[0].wait_recv()
+
+
+def collect(fulls, moved, late, far, small):
+    size = lax.axis_size("dp")
+    hbm = pl.BlockSpec(memory_space=pl.ANY)
+    dma = pltpu.SemaphoreType.DMA
+    vmem = lambda x: pltpu.VMEM(x.shape, x.dtype)
+    up, down, query, out = fulls
+    shapes = [
+        (up.shape[1], size * up.shape[2]),
+        down.shape,
+        (query.shape[1], size * query.shape[2]),
+        out.shape,
+    ]
+    return pl.pallas_call(
+        functools.partial(collect_kernel, size // 2),
+        name="collect",
+        out_shape=[jax.ShapeDtypeStruct(shape, jnp.bfloat16) for shape in shapes]
+        + [jax.ShapeDtypeStruct(small.shape[2:], jnp.float32)],
+        in_specs=[hbm] * 15,
+        out_specs=[hbm] * 4 + [pl.BlockSpec(memory_space=pltpu.VMEM)],
+        scratch_shapes=[vmem(small), vmem(small[:, 0])]
+        + [vmem(small[0, 0])] * 3
+        + [vmem(x) for x in late for _ in range(4)]
+        + [dma((23,)), dma((3,)), dma((3,))]
+        + [dma((size + 7,))] * 2
+        + [dma((2 * size,))] * 2
+        + [dma((2 * size + 5,))] * 2
+        + [dma((2, size))] * 2,
+        cost_estimate=pl.CostEstimate(
+            flops=120_000_000_000, bytes_accessed=20_000_000, transcendentals=0
+        ),
+        compiler_params=pltpu.CompilerParams(collective_id=5, has_side_effects=True),
+    )(*fulls, *moved, *late, *far, small)
 
 
 def swapped(size):
@@ -717,24 +1137,16 @@
     return lax.ppermute(x, ("section", "ctx", "dp"), across)
 
 
-def halves_summed(layer, grad):
-    ctx = lax.axis_index("ctx")
+def own_half(grad):
     half = grad.shape[-2] // 2
-    mine = lax.dynamic_slice_in_dim(grad, ctx * half, half, axis=-2)
-    others = lax.dynamic_slice_in_dim(grad, (1 - ctx) * half, half, axis=-2)
-    mine = mine + lax.ppermute(others, "ctx", [(0, 1), (1, 0)])
-    return mine + lax.ppermute(mine, "section", [(1 - layer, layer)])
-
-
-def both_halves(half):
-    ctx = lax.axis_index("ctx")
-    other = lax.ppermute(half, "ctx", [(0, 1), (1, 0)])
-    first = jnp.where(ctx == 0, half, other)
-    second = jnp.where(ctx == 0, other, half)
-    return jnp.concatenate([first, second], axis=-2)
-
-
-def spread_body(
+    return lax.dynamic_slice_in_dim(grad, lax.axis_index("ctx") * half, half, axis=-2)
+
+
+def spread_body(*args):
+    return spread_step(*args)
+
+
+def spread_step(
     tokens, cotangent, segment_ids, w_query, w_keyvalue, w_out, w_up, w_down, ln_gains, ln_biases
 ):
     section = lax.axis_index("section")
@@ -750,17 +1162,23 @@
         return lax.dynamic_index_in_dim(x, section, 0, keepdims=False)[0]
 
     hidden = regroup(own_micro(tokens)).astype(jnp.float32)
-    segments = lax.all_gather(own_micro(segment_ids), "dp").reshape(places, 2, length)
+    out, down = w_out[0], w_down[0]
+    columns = ln_gains.shape[2]
+    notes = jnp.concatenate(
+        [ln_gains[0], ln_biases[0], own_micro(segment_ids).astype(jnp.bfloat16)[None]], axis=0
+    )
+    notes = jnp.pad(notes, ((0, 32 - notes.shape[0]), (0, 0)))
+    query, keyvalue, notes, up, query_far, keyvalue_far, notes_far, out_far, up_far, down_far = (
+        distribute(w_query[0], w_keyvalue[0], notes, out, w_up[0], down)
+    )
+    notes = notes.reshape(size, 32, columns).transpose(1, 0, 2)
+    near = notes[:4].reshape(4, width).astype(jnp.float32)
+    far = notes_far.reshape(size, 32, columns).transpose(1, 0, 2)[:4].reshape(4, width)
+    far = far.astype(jnp.float32)
+    scales = [jnp.where(early, near, far), jnp.where(early, far, near)]
+    segments = notes[4].astype(jnp.int32).reshape(places, 2, length)
     segments = lax.dynamic_index_in_dim(segments, ctx, 1, keepdims=False)
     segs = [segments[:, :, None], segments[:, None, :]]
-    scales = lax.all_gather(
-        jnp.concatenate([ln_gains[0], ln_biases[0]], axis=0), ("section", "dp")
-    ).reshape(2, size, 4, -1)
-    scales = scales.transpose(0, 2, 1, 3).reshape(2, 4, width).astype(jnp.float32)
-    out, down = w_out[0], w_down[0]
-    query, keyvalue, up, query_far, keyvalue_far, out_far, up_far, down_far = distribute(
-        w_query[0], w_keyvalue[0], out, w_up[0], down
-    )
     attention_near, attention_far = [query, keyvalue, out], [query_far, keyvalue_far, out_far]
     attention_weights = [(attention_near, attention_far), (attention_far, attention_near)]
     ffn_weights = [([up, down], [up_far, down_far]), ([up_far, down_far], [up, down])]
@@ -768,15 +1186,15 @@
     unit_width = up.shape[1]
 
     def forward(layer, hidden):
-        normed = layer_norm(hidden, scales[layer, 0], scales[layer, 2]).astype(jnp.bfloat16)
+        normed = layer_norm(hidden, scales[layer][0], scales[layer][2]).astype(jnp.bfloat16)
         y, normed_all, q, kv, mixed = tensor_pass(
-            attention_forward_at, "attention_forward", 0, normed, *attention_weights[layer], segs,
+            attention_forward_at, 0, normed, *attention_weights[layer], segs,
             [head_width, keyvalue.shape[1], head_width],
         )
         after = hidden + y
-        normed_two = layer_norm(after, scales[layer, 1], scales[layer, 3]).astype(jnp.bfloat16)
+        normed_two = layer_norm(after, scales[layer][1], scales[layer][3]).astype(jnp.bfloat16)
         y, normed_two_all, up_rows, activated = tensor_pass(
-            ffn_forward_at, "ffn_forward", 1, normed_two, *ffn_weights[layer], [],
+            ffn_forward_at, 1, normed_two, *ffn_weights[layer], [],
             [unit_width, unit_width],
         )
         result = (after + y).astype(jnp.bfloat16)
@@ -788,71 +1206,101 @@
     def rows_of_all(grad):
         return grad.reshape(size, grad.shape[0] // size, grad.shape[1])
 
-    def backward(layer, grad_low, kept):
-        hidden, normed_all, q, kv, mixed, after, normed_two_all, up_rows, activated = kept
-        y, grad_low_all, grad_upper = tensor_pass(
-            ffn_backward_at, "ffn_backward", 2, grad_low, *ffn_weights[layer], [up_rows],
-            [unit_width],
-        )
-        up_grad = halves_summed(layer, rows_of_all(product(normed_two_all, grad_upper)))
-        down_grad = halves_summed(layer, product(activated, grad_low_all))
-        _, norm_back = jax.vjp(layer_norm, after, scales[layer, 1], scales[layer, 3])
-        grad_norm, gain_two, bias_two = norm_back(y)
-        grad_after = grad_low.astype(jnp.float32) + grad_norm
-        y, grad_branch_all, grad_query, grad_kv = tensor_pass(
-            attention_backward_at, "attention_backward", 3, grad_after.astype(jnp.bfloat16),
-            *attention_weights[layer], segs + [q, kv], [head_width, keyvalue.shape[1]],
-        )
-        query_grad = halves_summed(layer, rows_of_all(product(normed_all, grad_query)))
-        out_grad = halves_summed(layer, product(mixed, grad_branch_all))
+    def ffn_backward(layer, ident, grad_low, kept, sides):
+        _, _, _, _, _, after, normed_two_all, up_rows, activated = kept
+        y, grad_low_all, grad_upper, *arrived = tensor_pass(
+            ffn_backward_at, ident, grad_low, *ffn_weights[layer],
+            [up_rows], [unit_width], sides,
+        )
+        grads = [
+            rows_of_all(product(normed_two_all, grad_upper)),
+            product(activated, grad_low_all),
+        ]
+        _, norm_back = jax.vjp(layer_norm, after, scales[layer][1], scales[layer][3])
+        grad_norm, gain, bias = norm_back(y)
+        return grad_low.astype(jnp.float32) + grad_norm, grads, [gain, bias], arrived
+
+    def attention_backward(layer, ident, grad_after, grad_branch, kept, sides):
+        hidden, normed_all, q, kv, mixed, _, _, _, _ = kept
+        y, grad_branch_all, grad_query, grad_kv, *arrived = tensor_pass(
+            attention_backward_at, ident, grad_branch,
+            *attention_weights[layer], segs + [q, kv], [head_width, keyvalue.shape[1]], sides,
+        )
+        grads = [
+            rows_of_all(product(normed_all, grad_query)),
+            product(mixed, grad_branch_all),
+        ]
         keyvalue_grad = product(normed_all, grad_kv)
-        _, norm_back = jax.vjp(layer_norm, hidden, scales[layer, 0], scales[layer, 2])
-        grad_norm, gain_one, bias_one = norm_back(y)
-        grad_input = (grad_after + grad_norm).astype(jnp.bfloat16)
-        weight_grads = (query_grad, keyvalue_grad, out_grad, up_grad, down_grad)
-        return grad_input, weight_grads, jnp.stack([gain_one, gain_two, bias_one, bias_two])
-
-    first, kept_first = forward(0, hidden)
-    second, kept_second = forward(1, first.astype(jnp.float32))
-    grad_low = regroup(own_micro(cotangent))
-    grad_second, weights_second, scales_second = backward(1, grad_low, kept_second)
-    grad_first, weights_first, scales_first = backward(0, grad_second, kept_first)
+        _, norm_back = jax.vjp(layer_norm, hidden, scales[layer][0], scales[layer][2])
+        grad_norm, gain, bias = norm_back(y)
+        return (
+            (grad_after + grad_norm).astype(jnp.bfloat16), grads, keyvalue_grad, [gain, bias], arrived
+        )
+
+    def low(x):
+        return x.astype(jnp.bfloat16)
+
+    def ctx_sums(grads, arrived):
+        return [own_half(grad) + other for grad, other in zip(grads, arrived)]
 
     def both_rows(one, two):
         near = regroup(jnp.where(early, one, two))
         far = regroup_across(jnp.where(early, two, one))
         return jnp.stack([jnp.where(early, near, far), jnp.where(early, far, near)])[None, :, None]
 
-    query_grad, _, out_grad, up_grad, down_grad = [
-        jnp.where(early, one, two) for one, two in zip(weights_first, weights_second)
-    ]
-
-    def turned(grad):
-        grad = lax.all_to_all(grad, "dp", 0, 0)
-        return grad.transpose(1, 0, 2).reshape(grad.shape[1], size * grad.shape[2])
-
-    keyvalue_grad = lax.psum_scatter(
-        jnp.stack([weights_first[1], weights_second[1]]), "dp", scatter_dimension=1, tiled=True
-    )
-    keyvalue_grad = lax.psum(keyvalue_grad, ("section", "ctx"))
-    keyvalue_grad = lax.dynamic_index_in_dim(keyvalue_grad, section, 0, keepdims=False)
-    scale_grads = lax.psum_scatter(
-        jnp.stack([scales_first, scales_second]), "dp", scatter_dimension=2, tiled=True
-    )
-    scale_grads = lax.psum(scale_grads, ("section", "ctx"))
-    scale_grads = lax.dynamic_index_in_dim(scale_grads, section, 0, keepdims=True)
+    hold = lax.optimization_barrier
+    first, kept_first = forward(0, hidden)
+    second, kept_second = forward(1, first.astype(jnp.float32))
+    section_rows = both_rows(first, second)
+    grad_low = regroup(own_micro(cotangent))
+
+    def sides(axis, arrays):
+        return [(axis, array) for array in arrays]
+
+    grad_after, ffn_two, scales_two, _ = ffn_backward(1, 2, grad_low, kept_second, [])
+    branch, up_two, down_two = hold((low(grad_after), *ffn_two))
+    grad_second, attention_two, keyvalue_two, more, arrived = attention_backward(
+        1, 3, grad_after, branch, kept_second, sides("ctx", [up_two])
+    )
+    scales_two = more[:1] + scales_two[:1] + more[1:] + scales_two[1:]
+    (up_two,) = ctx_sums([up_two], arrived)
+    grad_after, ffn_one, scales_one, arrived = ffn_backward(
+        0, 6, grad_second, kept_first,
+        sides("section", [up_two]) + sides("ctx", [down_two] + attention_two),
+    )
+    up_two_far = arrived[0]
+    down_two, *attention_two = ctx_sums([down_two] + attention_two, arrived[1:])
+    branch, *both = hold((low(grad_after), *ffn_one, down_two, *attention_two))
+    ffn_one, rest_two = both[:2], both[2:]
+    grad_first, attention_one, keyvalue_one, more, arrived = attention_backward(
+        0, 7, grad_after, branch, kept_first,
+        sides("ctx", ffn_one) + sides("section", rest_two),
+    )
+    scales_one = more[:1] + scales_one[:1] + more[1:] + scales_one[1:]
+    ffn_moved, rest_far = arrived[:2], arrived[2:]
+
+    def small_of(keyvalue_grad, rows):
+        rows = low(jnp.stack(rows)).reshape(4, size, columns).transpose(1, 0, 2)
+        rows = jnp.pad(rows, ((0, 0), (0, 12), (0, 0)))
+        return jnp.concatenate([keyvalue_grad.reshape(size, columns, -1), rows], axis=1)
+
+    small = jnp.stack([small_of(keyvalue_one, scales_one), small_of(keyvalue_two, scales_two)])
+    up_grad, down_grad, query_grad, out_grad, small = collect(
+        ffn_one + attention_one, ffn_moved, [up_two] + rest_two, [up_two_far] + rest_far, small,
+    )
+    scale_grads = small[None, columns : columns + 4]
 
     def given(grad):
         return grad.astype(jnp.float32)[None]
 
     return (
-        both_rows(first, second),
+        section_rows,
         both_rows(grad_first, grad_second),
-        given(both_halves(turned(query_grad))),
-        given(keyvalue_grad),
-        given(both_halves(out_grad)),
-        given(both_halves(turned(up_grad))),
-        given(both_halves(down_grad)),
+        given(query_grad),
+        small[None, :columns],
+        given(out_grad),
+        given(up_grad),
+        given(down_grad),
         scale_grads[:, 0:2],
         scale_grads[:, 2:4],
     )
@@ -1004,7 +1452,6 @@
     micro = tokens.shape[0]
     width = tokens.shape[3]
     early = section_index == 0
-    late = section_index == 1
     segments = segment_ids[:, 0]
     own_tokens = tokens[:, 0].reshape(-1, width)
     own_cotangent = cotangent[:, 0].reshape(-1, width)
@@ -1114,5 +1561,8 @@
         P("section", None, "dp"),
         P("section", None, "dp"),
     )
-    step = spread_body if mesh.shape["dp"] == 8 else body
-    return jax.shard_map(step, mesh=mesh, in_specs=in_specs, out_specs=out_specs, check_vma=False)
+    spread = mesh.shape["dp"] == 8
+    return jax.shard_map(
+        spread_body if spread else body,
+        mesh=mesh, in_specs=in_specs, out_specs=out_specs, check_vma=False,
+    )

time: 1390 us -> 1200 us (0.86)
  waiting for transfers between devices: 195 us -> 3.42 us
  Pallas kernels: 889 us -> 1020 us
  blocking collectives: 67.7 us -> 0 us
  starting transfers between devices: 56.9 us -> 31.9 us
  other arithmetic: 86.4 us -> 62.3 us
  local copies, waits for them, and re-layouts: 31.9 us -> 16.5 us
    pallas_call x8 -> x9, Pallas kernels: 656 us -> 822 us  [the longest x8 672 us: tensor_pass(): call(x, *early_weights, *late_weights, *ins, *[array for _, array in sides])]
    ppermute x20 -> x0, waiting for transfers between devices: 149 us -> none  [the longest x8 80.6 us: halves_summed(): return mine + lax.ppermute(mine, 'section', [(1 - layer, layer)])]
    psum x1 -> x0, waiting for transfers between devices: 43.6 us -> none  [spread_body(): keyvalue_grad = lax.psum(keyvalue_grad, ('section', 'ctx'))]
    pallas_call x1, Pallas kernels: 233 us -> 195 us  [distribute(): pl.pallas_call(functools.partial(distribute_kernel, places), name='distri...]
    psum x1 -> x0, blocking collectives: 36.6 us -> none  [spread_body(): scale_grads = lax.psum(scale_grads, ('section', 'ctx'))]
    all_gather x2 -> x0, blocking collectives: 31.1 us -> none  [the longest x1 17.6 us: spread_body(): lax.all_gather(jnp.concatenate([ln_gains[0], ln_biases[0]], axis=0), ('se...]
    ppermute x20 -> x0, starting transfers between devices: 29.6 us -> none  [the longest x8 20.2 us: halves_summed(): return mine + lax.ppermute(mine, 'section', [(1 - layer, layer)])]
    ppermute x2, starting transfers between devices: 1.98 us -> 19.7 us  [regroup_across(): return lax.ppermute(x, ('section', 'ctx', 'dp'), across)]
  transfers between devices with their start and end apart: 31 -> 6, of which waited for: 8 -> 1; matrix products, arithmetic and copies ran while one was open for 9% -> 3% of each run, Pallas kernels for 58% -> 44%
where the time goes in v4:
time: 1200 us; the launch traced here: 1180 us
  Pallas kernels  1020 us (85%)
  other arithmetic  62.3 us (5%)
  matrix products  47.8 us (4%)
  starting transfers between devices  31.9 us (3%)
  local copies, waits for them, and re-layouts  16.5 us (1%)
    pallas_call x8, Pallas kernels, tensor_pass(): call(x, *early_weights, *late_weights, *ins, *[array for _, array in sides])  672 us
    pallas_call x1, Pallas kernels, distribute(): pl.pallas_call(functools.partial(distribute_kernel, places), name='distri...  195 us
    pallas_call x1, Pallas kernels, collect(): pl.pallas_call(functools.partial(collect_kernel, size // 2), name='collec...  150 us
    dot_general x10, matrix products, dense_left(): lax.dot_general(left, right, (((0,), (0,)), ((), ())), preferred_element_...  47.8 us
  transfers between devices with their start and end apart: 6, of which 1 were waited for; matrix products, arithmetic and copies ran while one was open for 3% of the time, Pallas kernels for 44%

profile of v4, /device:TPU:0, one launch (start us, length us, event | category | flops | bytes accessed | tf_op | source)
XLA Modules:
  0.0 1181.3 jit_solution(1940625129942920829)
XLA Ops:
  2.7 5.4 collective-permute-start.3
  10.0 5.4 collective-permute-start
  17.3 195.4 %distribute.1 = (bf16[2048,256]{1,0:T(8,128)(2,1)}, bf16[2048,256]{1,0:T(8,128)(2,1)}, bf16[256,256]{1,0:T(8,128)(2,1)}, bf16[2048,1024]{1,0:T(8,128)(2,1)}, bf1...) custom-call(bf16[256,2048]{1,0:T(8,128)(2,1)} %bitcast.166, ...), custom_call_target="tpu_custom_call" | custom-call | flops 149999992832 | bytes 20000000 | tf_op jit(solution)/shard_map/distribute/pallas_call | solution.py:752
  222.5 78.3 %shard_map.169 = (f32[128,2048]{1,0:T(8,128)}, bf16[4,2,128,2048]{3,2,1,0:T(8,128)(2,1)}, bf16[4,256,256]{2,1,0:T(8,128)(2,1)}, bf16[4,256,256]{2,1,0:T(8,128)(2,1)}, bf16[4,256,256]{2,1,0:T(8,128)(2,1)}) custom-call(bf16[128,2048]{1,0:T(8,128)(2,1)} %fusion.22.refs_0_, bf16[2048,256]{1,0:T(8,128)(2,1)} %get-tuple-element.77.refs_1_.refs_4_, ...), custom_call_target="tpu_custom_call" | custom-call | flops 60000002048 | bytes 20000000 | tf_op jit(solution)/shard_map/pallas_call | solution.py:517
  303.8 83.9 %shard_map.170 = (f32[128,2048]{1,0:T(8,128)}, bf16[4,2,128,2048]{3,2,1,0:T(8,128)(2,1)}, bf16[4,256,1024]{2,1,0:T(8,128)(2,1)}, bf16[4,256,1024]{2,1,0:T(8,128)(2,1)}) custom-call(bf16[128,2048]{1,0:T(8,128)(2,1)} %add_convert_fusion.5.refs_0_, bf16[2048,1024]{1,0:T(8,128)(2,1)} %get-tuple-element.83.refs_1_.refs_3_, bf16[1024,2048]{1,0:T(8,128)(2,1)} %bitcast.162, ...), custom_call_target="tpu_custom_call" | custom-call | flops 60000002048 | bytes 20000000 | tf_op jit(solution)/shard_map/pallas_call | solution.py:517
  390.6 78.4 %shard_map.171 = (f32[128,2048]{1,0:T(8,128)}, bf16[4,2,128,2048]{3,2,1,0:T(8,128)(2,1)}, bf16[4,256,256]{2,1,0:T(8,128)(2,1)}, bf16[4,256,256]{2,1,0:T(8,128)(2,1)}, bf16[4,256,256]{2,1,0:T(8,128)(2,1)}) custom-call(bf16[128,2048]{1,0:T(8,128)(2,1)} %fusion.19.refs_0_, bf16[2048,256]{1,0:T(8,128)(2,1)} %get-tuple-element.79.refs_4_.refs_1_, ...), custom_call_target="tpu_custom_call" | custom-call | flops 60000002048 | bytes 20000000 | tf_op jit(solution)/shard_map/pallas_call | solution.py:517
  471.8 83.8 %shard_map.172 = (f32[128,2048]{1,0:T(8,128)}, bf16[4,2,128,2048]{3,2,1,0:T(8,128)(2,1)}, bf16[4,256,1024]{2,1,0:T(8,128)(2,1)}, bf16[4,256,1024]{2,1,0:T(8,128)(2,1)}) custom-call(bf16[128,2048]{1,0:T(8,128)(2,1)} %add_convert_fusion.3.refs_0_, bf16[2048,1024]{1,0:T(8,128)(2,1)} %get-tuple-element.84.refs_3_.refs_1_, ...), custom_call_target="tpu_custom_call" | custom-call | flops 60000002048 | bytes 20000000 | tf_op jit(solution)/shard_map/pallas_call | solution.py:517
  555.6 84.6 %shard_map.173 = (f32[128,2048]{1,0:T(8,128)}, bf16[4,2,128,2048]{3,2,1,0:T(8,128)(2,1)}, bf16[4,256,1024]{2,1,0:T(8,128)(2,1)}) custom-call(bf16[128,2048]{1,0:T(8,128)(2,1)} %collective-permute-done.3.refs_0_, bf16[2048,1024]{1,0:T(8,128)(2,1)} %get-tuple-element.84.refs_3_.refs_1_, bf16[1024,2048]{1,0:T(8,128)(2,1)} %get-tuple-element.85.refs_4_.refs_2_, ...), custom_call_target="tpu_custom_call" | custom-call | flops 60000002048 | bytes 20000000 | tf_op jit(solution)/shard_map/pallas_call | solution.py:517
  644.7 9.6 convolution_convert_fusion.3
  654.3 6.2 convolution_convert_fusion.2.refs_7_
  662.6 80.9 %shard_map.174 = (f32[128,2048]{1,0:T(8,128)}, bf16[4,2,128,2048]{3,2,1,0:T(8,128)(2,1)}, bf16[4,256,256]{2,1,0:T(8,128)(2,1)}, bf16[4,256,256]{2,1,0:T(8,128)(2,1)}, bf16[8,128,1024]{2,1,0:T(8,128)(2,1)}) custom-call(bf16[128,2048]{1,0:T(8,128)(2,1)} %fusion.28.refs_0_, bf16[2048,256]{1,0:T(8,128)(2,1)} %get-tuple-element.79.refs_4_.refs_1_, ...), custom_call_target="tpu_custom_call" | custom-call | flops 60000002048 | bytes 20000000 | tf_op jit(solution)/shard_map/pallas_call | solution.py:517
  748.1 4.8 convolution_convert_fusion.9
  760.7 2.4 add_convert_fusion.1.refs_0_
  763.1 84.4 %shard_map.175 = (f32[128,2048]{1,0:T(8,128)}, bf16[4,2,128,2048]{3,2,1,0:T(8,128)(2,1)}, bf16[4,256,1024]{2,1,0:T(8,128)(2,1)}, bf16[8,128,1024]{2,1,0:T(8,128)...) custom-call(bf16[128,2048]{1,0:T(8,128)(2,1)} %add_convert_fusion.1.refs_0_, ...), custom_call_target="tpu_custom_call" | custom-call | flops 60000002048 | bytes 20000000 | tf_op jit(solution)/shard_map/pallas_call | solution.py:517
  853.8 4.8 dynamic-slice_add_fusion.refs_13_.down_late
  858.6 7.9 convolution_convert_fusion.1
  866.5 6.2 convolution_convert_fusion.refs_12_.down_full
  873.8 97.8 %shard_map.176 = (f32[128,2048]{1,0:T(8,128)}, bf16[4,2,128,2048]{3,2,1,0:T(8,128)(2,1)}, bf16[4,256,256]{2,1,0:T(8,128)(2,1)}, bf16[4,256,256]{2,1,0:T(8,128)(2...) custom-call(bf16[128,2048]{1,0:T(8,128)(2,1)} %fusion.29.refs_0_, ...), custom_call_target="tpu_custom_call" | custom-call | flops 60000002048 | bytes 20000000 | tf_op jit(solution)/shard_map/pallas_call | solution.py:517
  975.3 4.8 convolution_convert_fusion.7
  986.8 150.1 %collect.1 = (bf16[256,8192]{1,0:T(8,128)(2,1)}, bf16[1024,2048]{1,0:T(8,128)(2,1)}, bf16[256,2048]{1,0:T(8,128)(2,1)}, bf16[256,2048]{1,0:T(8,128)(2,1)}, f32[272,256]{1,0:T(8,128)}) custom-call(bf16[8,256,1024]{2,1,0:T(8,128)(2,1)} %bitcast.179, bf16[1024,2048]{1,0:T(8,128)(2,1)} %convolution_convert_fusion.refs_12_.down_full, ...), custom_call_target="tpu_custom_call" | custom-call | flops 120000004096 | bytes 20000000 | tf_op jit(solution)/shard_map/collect/pallas_call | solution.py:1097
  1140.6 19.6 %collective-permute-start.2 = (bf16[128,2048]{1,0:T(8,128)(2,1)S(1)}, bf16[128,2048]{1,0:T(8,128)(2,1)S(1)}, u32[]{:S(2)}, u32[]{:S(2)}) collective-permute-start(bf16[128,2048]{1,0:T(8,128)(2,1)S(1)} %get-tuple-element.186), channel_id=1, source_target_pairs={{0,16},{1,24},{2,18},{3,26},{4,20},{5,28},{6,22},{7,30},{8,17},{9,... | collective-permute-start | bytes 1572872 | tf_op jit(solution)/shard_map/ppermute | solution.py:1137
  1165.0 4.4 bitcast_convert_fusion.1
  1169.4 4.4 bitcast_convert_fusion
  1176.6 3.4 collective-permute-done.5
  (240 shorter events, 72.6 us)
Async XLA Ops:
  2.7 552.9 %collective-permute-start.3 = (bf16[128,2048]{1,0:T(8,128)(2,1)}, bf16[128,2048]{1,0:T(8,128)(2,1)}, u32[]{:S(2)}, u32[]{:S(2)}) collective-permute-start(bf16[128,2048]{1,0:T(8,128)(2,1)} %dynamic-slice_bitcast_fusion), channel_id=1, source_target_pairs={{0,0},{1,8},{2,2},{3,10},{4,4},{5,12},{6,6},{7,14},{8,1},{9,9},{10... | collective-permute-start | bytes 1572872 | tf_op jit(solution)/shard_map/ppermute | solution.py:1129
  10.0 207.7 %collective-permute-start = (bf16[128,2048]{1,0:T(8,128)(2,1)}, bf16[128,2048]{1,0:T(8,128)(2,1)}, u32[]{:S(2)}, u32[]{:S(2)}) collective-permute-start(bf16[128,2048]{1,0:T(8,128)(2,1)} %dynamic-slice_bitcast_fusion.1), channel_id=1, source_target_pairs={{0,0},{1,8},{2,2},{3,10},{4,4},{5,12},{6,6},{7,14},{8,1},{9,9},{10... | collective-permute-start | bytes 1572872 | tf_op jit(solution)/shard_map/ppermute | solution.py:1129
  216.0 173.4 %copy-start.28 = (f32[1,2,8,128]{3,1,2,0:T(2,128)}, f32[1,2,8,128]{3,1,2,0:T(2,128)S(1)}, u32[]{:S(2)}) copy-start(f32[1,2,8,128]{3,1,2,0:T(2,128)S(1)} %copy.43) | copy-start | bytes 24580
  216.0 84.8 %copy-start.26 = (f32[1,2,8,128]{3,1,2,0:T(2,128)}, f32[1,2,8,128]{3,1,2,0:T(2,128)S(1)}, u32[]{:S(2)}) copy-start(f32[1,2,8,128]{3,1,2,0:T(2,128)S(1)} %copy.39) | copy-start | bytes 24580
  216.1 86.7 %copy-start.30 = (f32[1,2,8,128]{3,1,2,0:T(2,128)}, f32[1,2,8,128]{3,1,2,0:T(2,128)S(1)}, u32[]{:S(2)}) copy-start(f32[1,2,8,128]{3,1,2,0:T(2,128)S(1)} %copy.41) | copy-start | bytes 24580
  302.4 85.2 %copy-start.2 = (f32[128,2048]{1,0:T(8,128)}, f32[128,2048]{1,0:T(8,128)S(1)}, u32[]{:S(2)}) copy-start(f32[128,2048]{1,0:T(8,128)S(1)} %get-tuple-element.182) | copy-start | bytes 3145732
  470.5 171.4 %copy-start.4 = (f32[128,2048]{1,0:T(8,128)}, f32[128,2048]{1,0:T(8,128)S(1)}, u32[]{:S(2)}) copy-start(f32[128,2048]{1,0:T(8,128)S(1)} %get-tuple-element.178) | copy-start | bytes 3145732
  763.1 84.5 %copy-start.25 = (bf16[256,2048]{1,0:T(8,128)(2,1)S(1)}, bf16[256,2048]{1,0:T(8,128)(2,1)}, u32[]{:S(2)}) copy-start(bf16[256,2048]{1,0:T(8,128)(2,1)} %convolution_convert_fusion.8.refs_9_) | copy-start | bytes 3145732
  763.1 86.5 %copy-start.24 = (bf16[2048,256]{1,0:T(8,128)(2,1)S(1)}, bf16[2048,256]{1,0:T(8,128)(2,1)}, u32[]{:S(2)}) copy-start(bf16[2048,256]{1,0:T(8,128)(2,1)} %convolution_convert_fusion.9) | copy-start | bytes 3145732
  763.1 88.5 %copy-start.3 = (f32[128,2048]{1,0:T(8,128)S(1)}, f32[128,2048]{1,0:T(8,128)}, u32[]{:S(2)}) copy-start(f32[128,2048]{1,0:T(8,128)} %copy-done.2) | copy-start | bytes 3145732
  763.1 88.5 %copy-start.31 = (f32[1,2,8,128]{3,1,2,0:T(2,128)S(1)}, f32[1,2,8,128]{3,1,2,0:T(2,128)}, u32[]{:S(2)}) copy-start(f32[1,2,8,128]{3,1,2,0:T(2,128)} %copy-done.30) | copy-start | bytes 24580
  763.1 88.5 %copy-start.43 = (f32[128]{0:T(128)S(1)}, f32[128]{0:T(128)}, u32[]{:S(2)}) copy-start(f32[128]{0:T(128)} %copy-done.42) | copy-start | bytes 1540
  763.1 88.5 %copy-start.49 = (f32[128]{0:T(128)S(1)}, f32[128]{0:T(128)}, u32[]{:S(2)}) copy-start(f32[128]{0:T(128)} %copy-done.48) | copy-start | bytes 1540
  873.8 97.9 %copy-start.27 = (f32[1,2,8,128]{3,1,2,0:T(2,128)S(1)}, f32[1,2,8,128]{3,1,2,0:T(2,128)}, u32[]{:S(2)}) copy-start(f32[1,2,8,128]{3,1,2,0:T(2,128)} %copy-done.26) | copy-start | bytes 24580
  873.8 97.9 %copy-start.39 = (f32[128]{0:T(128)S(1)}, f32[128]{0:T(128)}, u32[]{:S(2)}) copy-start(f32[128]{0:T(128)} %copy-done.38) | copy-start | bytes 1540
  873.8 99.6 %copy-start.55 = (f32[128]{0:T(128)S(1)}, f32[128]{0:T(128)}, u32[]{:S(2)}) copy-start(f32[128]{0:T(128)} %copy-done.54) | copy-start | bytes 1540
  873.8 99.6 %copy-start.45 = (f32[128]{0:T(128)S(1)}, f32[128]{0:T(128)}, u32[]{:S(2)}) copy-start(f32[128]{0:T(128)} %copy-done.44) | copy-start | bytes 1540
  986.8 152.7 %copy-start.5 = (f32[128,2048]{1,0:T(8,128)S(1)}, f32[128,2048]{1,0:T(8,128)}, u32[]{:S(2)}) copy-start(f32[128,2048]{1,0:T(8,128)} %copy-done.4) | copy-start | bytes 3145732
  986.8 152.7 %copy-start.8 = (bf16[128,2048]{1,0:T(8,128)(2,1)S(1)}, bf16[128,2048]{1,0:T(8,128)(2,1)}, u32[]{:S(2)}) copy-start(bf16[128,2048]{1,0:T(8,128)(2,1)} %copy-done.6) | copy-start | bytes 1572868
  986.8 152.7 %copy-start.23 = (f32[128,2048]{1,0:T(8,128)S(1)}, f32[128,2048]{1,0:T(8,128)}, u32[]{:S(2)}) copy-start(f32[128,2048]{1,0:T(8,128)} %get-tuple-element.88) | copy-start | bytes 3145732
  1139.8 35.7 %collective-permute-start.1 = (bf16[128,2048]{1,0:T(8,128)(2,1)S(1)}, bf16[128,2048]{1,0:T(8,128)(2,1)S(1)}, u32[]{:S(2)}, u32[]{:S(2)}) collective-permute-start(bf16[128,2048]{1,0:T(8,128)(2,1)S(1)} %get-tuple-element.185), channel_id=1, source_target_pairs={{0,0},{1,8},{2,2},{3,10},{4,4},{5,12},{6,6},{7,14},{8,1},{9,9},{10... | collective-permute-start | bytes 1572872 | tf_op jit(solution)/shard_map/ppermute | solution.py:1129
  1140.6 34.9 %collective-permute-start.2 = (bf16[128,2048]{1,0:T(8,128)(2,1)S(1)}, bf16[128,2048]{1,0:T(8,128)(2,1)S(1)}, u32[]{:S(2)}, u32[]{:S(2)}) collective-permute-start(bf16[128,2048]{1,0:T(8,128)(2,1)S(1)} %get-tuple-element.186), channel_id=1, source_target_pairs={{0,16},{1,24},{2,18},{3,26},{4,20},{5,28},{6,22},{7,30},{8,17},{9,... | collective-permute-start | bytes 1572872 | tf_op jit(solution)/shard_map/ppermute | solution.py:1137
  1162.7 17.2 %collective-permute-start.5 = (bf16[128,2048]{1,0:T(8,128)(2,1)S(1)}, bf16[128,2048]{1,0:T(8,128)(2,1)S(1)}, u32[]{:S(2)}, u32[]{:S(2)}) collective-permute-start(bf16[128,2048]{1,0:T(8,128)(2,1)S(1)} %broadcast_select_fusion), channel_id=1, source_target_pairs={{0,16},{1,24},{2,18},{3,26},{4,20},{5,28},{6,22},{7,30},{8,17},{9,... | collective-permute-start | bytes 1572872 | tf_op jit(solution)/shard_map/ppermute | solution.py:1137
  1162.8 17.2 %collective-permute-start.4 = (bf16[128,2048]{1,0:T(8,128)(2,1)S(1)}, bf16[128,2048]{1,0:T(8,128)(2,1)S(1)}, u32[]{:S(2)}, u32[]{:S(2)}) collective-permute-start(bf16[128,2048]{1,0:T(8,128)(2,1)S(1)} %get-tuple-element.171), channel_id=1, source_target_pairs={{0,0},{1,8},{2,2},{3,10},{4,4},{5,12},{6,6},{7,14},{8,1},{9,9},{10... | collective-permute-start | bytes 1572872 | tf_op jit(solution)/shard_map/ppermute | solution.py:1129
  (53 other events, 1414.5 us)

commit v5 on v4

--- a/solution.py
+++ b/solution.py
@@ -40,7 +40,7 @@
 
 
 MESH = pl.DeviceIdType.MESH
-PARTS = 2
+PARTS = 4
 
 
 def gelu(v):
@@ -207,16 +207,18 @@
     late_weights = take(n_weights)
     ins = take(n_ins)
     side_from = take(len(side_axes))
-    y_ref, gath = take(2)
-    outs = take(n_outs)
+    (y_ref,) = take(1)
+    given = take(1 + n_outs)
     side_to = take(len(side_axes))
+    kept = take(1 + n_outs)
+    gath, outs = kept[0], kept[1:]
     weights = take(n_weights)
     part, partner_out, partner_in, total, line_out, from_left, from_right = take(7)
     (
         weight_sem, gather_right, gather_left, gather_partner, gather_line_in, gather_partner_in,
         partner_send, partner_recv, right_send, right_recv, left_send, left_recv,
-        side_send, side_recv,
-    ) = take(14)
+        side_send, side_recv, given_sem,
+    ) = take(15)
 
     section = lax.axis_index("section")
     me = lax.axis_index("dp")
@@ -329,6 +331,12 @@
     at_end = (z == 0) | (z == last)
     low_half = z < places // 2
 
+    def give(block):
+        return [
+            pltpu.make_async_copy(kept[index].at[block], given[index].at[block], given_sem.at[index, block])
+            for index in range(1 + n_outs)
+        ]
+
     def step(i, carry):
         inner_block = jnp.where(i == 0, 1, jnp.where(i == 1, 0, i))
         low_block = jnp.where(z == 0, i, inner_block)
@@ -378,6 +386,9 @@
         sum_to_partner(block).wait_recv()
         total[block] = part[k] + partner_in[block].astype(jnp.float32)
 
+        for copy in give(block):
+            copy.start()
+
         @pl.when((z == 0) & (block > 0))
         def _():
             line_out[block] = total[block].astype(jnp.bfloat16)
@@ -434,6 +445,8 @@
     def drain(block, carry):
         to_partner(block, gath.at[block, k]).wait_send()
         sum_to_partner(block).wait_send()
+        for copy in give(block):
+            copy.wait()
         for index in range(PARTS):
 
             @pl.when((block <= z) & has_right)
@@ -482,8 +495,10 @@
         + [jax.ShapeDtypeStruct((places, 2 * rows, out), jnp.bfloat16) for out in out_widths]
         + [jax.ShapeDtypeStruct(shape, jnp.bfloat16) for shape in moved],
         in_specs=[vmem] + [hbm] * (2 * count) + [vmem] * len(ins) + [hbm] * len(axes),
-        out_specs=[vmem] * (2 + len(out_widths)) + [hbm] * len(axes),
-        scratch_shapes=[pltpu.VMEM(weight.shape, weight.dtype) for weight in early_weights]
+        out_specs=[vmem] + [hbm] * (1 + len(out_widths) + len(axes)),
+        scratch_shapes=[pltpu.VMEM((places, 2, rows, width), jnp.bfloat16)]
+        + [pltpu.VMEM((places, 2 * rows, out), jnp.bfloat16) for out in out_widths]
+        + [pltpu.VMEM(weight.shape, weight.dtype) for weight in early_weights]
         + [
             pltpu.VMEM((2, rows, width), jnp.float32),
             pltpu.VMEM((places, rows, width), jnp.bfloat16),
@@ -506,6 +521,7 @@
             dma((places, PARTS)),
             dma((max(len(axes), 1),)),
             dma((max(len(axes), 1),)),
+            dma((1 + len(out_widths), places)),
         ],
         cost_estimate=pl.CostEstimate(
             flops=60_000_000_000, bytes_accessed=20_000_000, transcendentals=0
@@ -540,19 +556,24 @@
     across = {"section": 1 - section}
     over = {"ctx": 1 - ctx}
 
+    def group(away, act):
+        if away == 0:
+            act(2 * z + 1 - k)
+            return
+
+        @pl.when(z + away <= last)
+        def _():
+            act(2 * (z + away) + k)
+            act(2 * (z + away) + 1 - k)
+
+        @pl.when(z - away >= 0)
+        def _():
+            act(2 * (z - away) + k)
+            act(2 * (z - away) + 1 - k)
+
     def peers(act):
-        act(2 * z + 1 - k)
-        for away in range(1, places):
-
-            @pl.when(z + away <= last)
-            def _():
-                act(2 * (z + away) + k)
-                act(2 * (z + away) + 1 - k)
-
-            @pl.when(z - away >= 0)
-            def _():
-                act(2 * (z - away) + k)
-                act(2 * (z - away) + 1 - k)
+        for away in range(places):
+            group(away, act)
 
     def remote(source, target, send, recv, device):
         return pltpu.make_async_remote_copy(
@@ -691,18 +712,24 @@
         up_copy(source, me, 0).wait_recv()
         block_across(3, source).start()
 
-    peers(pass_up)
-
     def over_block(kind):
-        def move(owner, carry):
+        def move(owner):
             block_across(kind, owner).wait_recv()
             block_over(kind, owner).start()
-            return carry
-
-        lax.fori_loop(0, 2 * places, move, 0)
-
-    for kind in range(len(kinds)):
-        over_block(kind)
+
+        return move
+
+    group(0, pass_up)
+    group(1, pass_up)
+    for kind in range(3):
+        over_block(kind)(me)
+        peers(over_block(kind))
+    over_block(3)(me)
+    for away in range(2, places):
+        group(away, pass_up)
+        group(away - 2, over_block(3))
+    group(places - 2, over_block(3))
+    group(places - 1, over_block(3))
 
     peers(lambda source: up_copy(source, me, 1).wait_recv())
 
@@ -792,19 +819,24 @@
     turned = [(up, up_out), (query, query_out)]
     half = up.shape[1]
 
+    def group(away, act):
+        if away == 0:
+            act(2 * z + 1 - k)
+            return
+
+        @pl.when(z + away <= last)
+        def _():
+            act(2 * (z + away) + k)
+            act(2 * (z + away) + 1 - k)
+
+        @pl.when(z - away >= 0)
+        def _():
+            act(2 * (z - away) + k)
+            act(2 * (z - away) + 1 - k)
+
     def peers(act):
-        act(2 * z + 1 - k)
-        for away in range(1, places):
-
-            @pl.when(z + away <= last)
-            def _():
-                act(2 * (z + away) + k)
-                act(2 * (z + away) + 1 - k)
-
-            @pl.when(z - away >= 0)
-            def _():
-                act(2 * (z - away) + k)
-                act(2 * (z - away) + 1 - k)
+        for away in range(places):
+            group(away, act)
 
     def remote(source, target, send, recv, device):
         return pltpu.make_async_remote_copy(
@@ -978,11 +1010,14 @@
 
         return act
 
-    peers(up_block)
+    for away in range(places):
+        group(away, up_block)
+        if away > 0:
+            group(away - 1, arrived(0))
     sum_up(me)
     peers(small_start)
     own_block(0).start()
-    peers(arrived(0))
+    group(last, arrived(0))
     own_block(0).wait()
     hand_over(0, me, ctx).start()
 

time: 1200 us -> 1160 us (0.967)
  Pallas kernels: 1020 us -> 1000 us
  starting transfers between devices: 31.9 us -> 14.3 us
    pallas_call x1, Pallas kernels: 195 us -> 166 us  [distribute(): pl.pallas_call(functools.partial(distribute_kernel, places), name='distri...]
    pallas_call x1, Pallas kernels: 150 us -> 178 us  [collect(): pl.pallas_call(functools.partial(collect_kernel, size // 2), name='collec...]
    ppermute x2, starting transfers between devices: 19.7 us -> 2.06 us  [regroup_across(): return lax.ppermute(x, ('section', 'ctx', 'dp'), across)]
    pallas_call x8, Pallas kernels: 672 us -> 657 us  [tensor_pass(): call(x, *early_weights, *late_weights, *ins, *[array for _, array in sides])]
  transfers between devices with their start and end apart: 6 -> 6, of which waited for: 1 -> 1; matrix products, arithmetic and copies ran while one was open for 3% -> 3% of each run, Pallas kernels for 44% -> 41%
where the time goes in v5:
time: 1160 us; the launch traced here: 1150 us
  Pallas kernels  1000 us (86%)
  other arithmetic  62.3 us (5%)
  matrix products  47.8 us (4%)
  local copies, waits for them, and re-layouts  16.5 us (1%)
  starting transfers between devices  14.3 us (1%)
    pallas_call x8, Pallas kernels, tensor_pass(): call(x, *early_weights, *late_weights, *ins, *[array for _, array in sides])  657 us
    pallas_call x1, Pallas kernels, collect(): pl.pallas_call(functools.partial(collect_kernel, size // 2), name='collec...  178 us
    pallas_call x1, Pallas kernels, distribute(): pl.pallas_call(functools.partial(distribute_kernel, places), name='distri...  166 us
    dot_general x10, matrix products, dense_left(): lax.dot_general(left, right, (((0,), (0,)), ((), ())), preferred_element_...  47.8 us
  transfers between devices with their start and end apart: 6, of which 1 were waited for; matrix products, arithmetic and copies ran while one was open for 3% of the time, Pallas kernels for 41%

profile of v5, /device:TPU:0, one launch (start us, length us, event | category | flops | bytes accessed | tf_op | source)
XLA Modules:
  0.0 1148.9 jit_solution(8744312452680025572)
XLA Ops:
  2.7 5.4 collective-permute-start.3
  10.0 5.4 collective-permute-start
  17.3 165.9 %distribute.1 = (bf16[2048,256]{1,0:T(8,128)(2,1)}, bf16[2048,256]{1,0:T(8,128)(2,1)}, bf16[256,256]{1,0:T(8,128)(2,1)}, bf16[2048,1024]{1,0:T(8,128)(2,1)}, bf1...) custom-call(bf16[256,2048]{1,0:T(8,128)(2,1)} %bitcast.166, ...), custom_call_target="tpu_custom_call" | custom-call | flops 149999992832 | bytes 20000000 | tf_op jit(solution)/shard_map/distribute/pallas_call | solution.py:779
  193.0 74.4 %shard_map.169 = (f32[128,2048]{1,0:T(8,128)}, bf16[4,2,128,2048]{3,2,1,0:T(8,128)(2,1)}, bf16[4,256,256]{2,1,0:T(8,128)(2,1)}, bf16[4,256,256]{2,1,0:T(8,128)(2,1)}, bf16[4,256,256]{2,1,0:T(8,128)(2,1)}) custom-call(bf16[128,2048]{1,0:T(8,128)(2,1)} %fusion.22.refs_0_, bf16[2048,256]{1,0:T(8,128)(2,1)} %get-tuple-element.77.refs_1_.refs_4_, ...), custom_call_target="tpu_custom_call" | custom-call | flops 60000002048 | bytes 20000000 | tf_op jit(solution)/shard_map/pallas_call | solution.py:533
  270.3 78.9 %shard_map.170 = (f32[128,2048]{1,0:T(8,128)}, bf16[4,2,128,2048]{3,2,1,0:T(8,128)(2,1)}, bf16[4,256,1024]{2,1,0:T(8,128)(2,1)}, bf16[4,256,1024]{2,1,0:T(8,128)(2,1)}) custom-call(bf16[128,2048]{1,0:T(8,128)(2,1)} %add_convert_fusion.5.refs_0_, bf16[2048,1024]{1,0:T(8,128)(2,1)} %get-tuple-element.83.refs_1_.refs_3_, bf16[1024,2048]{1,0:T(8,128)(2,1)} %bitcast.162, ...), custom_call_target="tpu_custom_call" | custom-call | flops 60000002048 | bytes 20000000 | tf_op jit(solution)/shard_map/pallas_call | solution.py:533
  352.2 73.5 %shard_map.171 = (f32[128,2048]{1,0:T(8,128)}, bf16[4,2,128,2048]{3,2,1,0:T(8,128)(2,1)}, bf16[4,256,256]{2,1,0:T(8,128)(2,1)}, bf16[4,256,256]{2,1,0:T(8,128)(2,1)}, bf16[4,256,256]{2,1,0:T(8,128)(2,1)}) custom-call(bf16[128,2048]{1,0:T(8,128)(2,1)} %fusion.19.refs_0_, bf16[2048,256]{1,0:T(8,128)(2,1)} %get-tuple-element.79.refs_4_.refs_1_, ...), custom_call_target="tpu_custom_call" | custom-call | flops 60000002048 | bytes 20000000 | tf_op jit(solution)/shard_map/pallas_call | solution.py:533
  428.5 77.1 %shard_map.172 = (f32[128,2048]{1,0:T(8,128)}, bf16[4,2,128,2048]{3,2,1,0:T(8,128)(2,1)}, bf16[4,256,1024]{2,1,0:T(8,128)(2,1)}, bf16[4,256,1024]{2,1,0:T(8,128)(2,1)}) custom-call(bf16[128,2048]{1,0:T(8,128)(2,1)} %add_convert_fusion.3.refs_0_, bf16[2048,1024]{1,0:T(8,128)(2,1)} %get-tuple-element.84.refs_3_.refs_1_, ...), custom_call_target="tpu_custom_call" | custom-call | flops 60000002048 | bytes 20000000 | tf_op jit(solution)/shard_map/pallas_call | solution.py:533
  505.6 80.1 %shard_map.173 = (f32[128,2048]{1,0:T(8,128)}, bf16[4,2,128,2048]{3,2,1,0:T(8,128)(2,1)}, bf16[4,256,1024]{2,1,0:T(8,128)(2,1)}) custom-call(bf16[128,2048]{1,0:T(8,128)(2,1)} %collective-permute-done.3.refs_0_, bf16[2048,1024]{1,0:T(8,128)(2,1)} %get-tuple-element.84.refs_3_.refs_1_, bf16[1024,2048]{1,0:T(8,128)(2,1)} %get-tuple-element.85.refs_4_.refs_2_, ...), custom_call_target="tpu_custom_call" | custom-call | flops 60000002048 | bytes 20000000 | tf_op jit(solution)/shard_map/pallas_call | solution.py:533
  590.3 9.6 convolution_convert_fusion.3
  599.8 6.2 convolution_convert_fusion.2.refs_7_
  608.1 77.7 %shard_map.174 = (f32[128,2048]{1,0:T(8,128)}, bf16[4,2,128,2048]{3,2,1,0:T(8,128)(2,1)}, bf16[4,256,256]{2,1,0:T(8,128)(2,1)}, bf16[4,256,256]{2,1,0:T(8,128)(2,1)}, bf16[8,128,1024]{2,1,0:T(8,128)(2,1)}) custom-call(bf16[128,2048]{1,0:T(8,128)(2,1)} %fusion.28.refs_0_, bf16[2048,256]{1,0:T(8,128)(2,1)} %get-tuple-element.79.refs_4_.refs_1_, ...), custom_call_target="tpu_custom_call" | custom-call | flops 60000002048 | bytes 20000000 | tf_op jit(solution)/shard_map/pallas_call | solution.py:533
  690.4 4.8 convolution_convert_fusion.9
  695.2 2.4 convolution_convert_fusion.4
  703.0 2.4 add_convert_fusion.1.refs_0_
  705.4 98.4 %shard_map.175 = (f32[128,2048]{1,0:T(8,128)}, bf16[4,2,128,2048]{3,2,1,0:T(8,128)(2,1)}, bf16[4,256,1024]{2,1,0:T(8,128)(2,1)}, bf16[8,128,1024]{2,1,0:T(8,128)...) custom-call(bf16[128,2048]{1,0:T(8,128)(2,1)} %add_convert_fusion.1.refs_0_, ...), custom_call_target="tpu_custom_call" | custom-call | flops 60000002048 | bytes 20000000 | tf_op jit(solution)/shard_map/pallas_call | solution.py:533
  810.1 4.8 dynamic-slice_add_fusion.refs_13_.down_late
  814.9 7.9 convolution_convert_fusion.1
  822.8 6.2 convolution_convert_fusion.refs_12_.down_full
  830.1 96.6 %shard_map.176 = (f32[128,2048]{1,0:T(8,128)}, bf16[4,2,128,2048]{3,2,1,0:T(8,128)(2,1)}, bf16[4,256,256]{2,1,0:T(8,128)(2,1)}, bf16[4,256,256]{2,1,0:T(8,128)(2...) custom-call(bf16[128,2048]{1,0:T(8,128)(2,1)} %fusion.29.refs_0_, ...), custom_call_target="tpu_custom_call" | custom-call | flops 60000002048 | bytes 20000000 | tf_op jit(solution)/shard_map/pallas_call | solution.py:533
  930.4 4.8 convolution_convert_fusion.7
  941.9 177.8 %collect.1 = (bf16[256,8192]{1,0:T(8,128)(2,1)}, bf16[1024,2048]{1,0:T(8,128)(2,1)}, bf16[256,2048]{1,0:T(8,128)(2,1)}, bf16[256,2048]{1,0:T(8,128)(2,1)}, f32[272,256]{1,0:T(8,128)}) custom-call(bf16[8,256,1024]{2,1,0:T(8,128)(2,1)} %bitcast.179, bf16[1024,2048]{1,0:T(8,128)(2,1)} %convolution_convert_fusion.refs_12_.down_full, ...), custom_call_target="tpu_custom_call" | custom-call | flops 120000004096 | bytes 20000000 | tf_op jit(solution)/shard_map/collect/pallas_call | solution.py:1132
  1130.2 4.4 bitcast_convert_fusion.1
  1134.6 4.4 bitcast_convert_fusion
  1141.8 5.9 collective-permute-done.5
  (240 shorter events, 72.2 us)
Async XLA Ops:
  2.7 502.9 %collective-permute-start.3 = (bf16[128,2048]{1,0:T(8,128)(2,1)}, bf16[128,2048]{1,0:T(8,128)(2,1)}, u32[]{:S(2)}, u32[]{:S(2)}) collective-permute-start(bf16[128,2048]{1,0:T(8,128)(2,1)} %dynamic-slice_bitcast_fusion), channel_id=1, source_target_pairs={{0,0},{1,8},{2,2},{3,10},{4,4},{5,12},{6,6},{7,14},{8,1},{9,9},{10... | collective-permute-start | bytes 1572872 | tf_op jit(solution)/shard_map/ppermute | solution.py:1164
  10.0 178.2 %collective-permute-start = (bf16[128,2048]{1,0:T(8,128)(2,1)}, bf16[128,2048]{1,0:T(8,128)(2,1)}, u32[]{:S(2)}, u32[]{:S(2)}) collective-permute-start(bf16[128,2048]{1,0:T(8,128)(2,1)} %dynamic-slice_bitcast_fusion.1), channel_id=1, source_target_pairs={{0,0},{1,8},{2,2},{3,10},{4,4},{5,12},{6,6},{7,14},{8,1},{9,9},{10... | collective-permute-start | bytes 1572872 | tf_op jit(solution)/shard_map/ppermute | solution.py:1164
  186.5 164.5 %copy-start.28 = (f32[1,2,8,128]{3,1,2,0:T(2,128)}, f32[1,2,8,128]{3,1,2,0:T(2,128)S(1)}, u32[]{:S(2)}) copy-start(f32[1,2,8,128]{3,1,2,0:T(2,128)S(1)} %copy.43) | copy-start | bytes 24580
  186.5 80.9 %copy-start.26 = (f32[1,2,8,128]{3,1,2,0:T(2,128)}, f32[1,2,8,128]{3,1,2,0:T(2,128)S(1)}, u32[]{:S(2)}) copy-start(f32[1,2,8,128]{3,1,2,0:T(2,128)S(1)} %copy.39) | copy-start | bytes 24580
  186.6 82.7 %copy-start.30 = (f32[1,2,8,128]{3,1,2,0:T(2,128)}, f32[1,2,8,128]{3,1,2,0:T(2,128)S(1)}, u32[]{:S(2)}) copy-start(f32[1,2,8,128]{3,1,2,0:T(2,128)S(1)} %copy.41) | copy-start | bytes 24580
  269.0 80.2 %copy-start.2 = (f32[128,2048]{1,0:T(8,128)}, f32[128,2048]{1,0:T(8,128)S(1)}, u32[]{:S(2)}) copy-start(f32[128,2048]{1,0:T(8,128)S(1)} %get-tuple-element.182) | copy-start | bytes 3145732
  427.2 160.2 %copy-start.4 = (f32[128,2048]{1,0:T(8,128)}, f32[128,2048]{1,0:T(8,128)S(1)}, u32[]{:S(2)}) copy-start(f32[128,2048]{1,0:T(8,128)S(1)} %get-tuple-element.178) | copy-start | bytes 3145732
  705.4 98.5 %copy-start.25 = (bf16[256,2048]{1,0:T(8,128)(2,1)S(1)}, bf16[256,2048]{1,0:T(8,128)(2,1)}, u32[]{:S(2)}) copy-start(bf16[256,2048]{1,0:T(8,128)(2,1)} %convolution_convert_fusion.8.refs_9_) | copy-start | bytes 3145732
  705.4 100.5 %copy-start.24 = (bf16[2048,256]{1,0:T(8,128)(2,1)S(1)}, bf16[2048,256]{1,0:T(8,128)(2,1)}, u32[]{:S(2)}) copy-start(bf16[2048,256]{1,0:T(8,128)(2,1)} %convolution_convert_fusion.9) | copy-start | bytes 3145732
  705.4 102.5 %copy-start.3 = (f32[128,2048]{1,0:T(8,128)S(1)}, f32[128,2048]{1,0:T(8,128)}, u32[]{:S(2)}) copy-start(f32[128,2048]{1,0:T(8,128)} %copy-done.2) | copy-start | bytes 3145732
  705.4 102.5 %copy-start.31 = (f32[1,2,8,128]{3,1,2,0:T(2,128)S(1)}, f32[1,2,8,128]{3,1,2,0:T(2,128)}, u32[]{:S(2)}) copy-start(f32[1,2,8,128]{3,1,2,0:T(2,128)} %copy-done.30) | copy-start | bytes 24580
  705.4 102.5 %copy-start.43 = (f32[128]{0:T(128)S(1)}, f32[128]{0:T(128)}, u32[]{:S(2)}) copy-start(f32[128]{0:T(128)} %copy-done.42) | copy-start | bytes 1540
  705.4 102.5 %copy-start.49 = (f32[128]{0:T(128)S(1)}, f32[128]{0:T(128)}, u32[]{:S(2)}) copy-start(f32[128]{0:T(128)} %copy-done.48) | copy-start | bytes 1540
  830.1 96.7 %copy-start.27 = (f32[1,2,8,128]{3,1,2,0:T(2,128)S(1)}, f32[1,2,8,128]{3,1,2,0:T(2,128)}, u32[]{:S(2)}) copy-start(f32[1,2,8,128]{3,1,2,0:T(2,128)} %copy-done.26) | copy-start | bytes 24580
  830.1 96.7 %copy-start.39 = (f32[128]{0:T(128)S(1)}, f32[128]{0:T(128)}, u32[]{:S(2)}) copy-start(f32[128]{0:T(128)} %copy-done.38) | copy-start | bytes 1540
  830.1 98.4 %copy-start.55 = (f32[128]{0:T(128)S(1)}, f32[128]{0:T(128)}, u32[]{:S(2)}) copy-start(f32[128]{0:T(128)} %copy-done.54) | copy-start | bytes 1540
  830.1 98.4 %copy-start.45 = (f32[128]{0:T(128)S(1)}, f32[128]{0:T(128)}, u32[]{:S(2)}) copy-start(f32[128]{0:T(128)} %copy-done.44) | copy-start | bytes 1540
  941.9 180.4 %copy-start.5 = (f32[128,2048]{1,0:T(8,128)S(1)}, f32[128,2048]{1,0:T(8,128)}, u32[]{:S(2)}) copy-start(f32[128,2048]{1,0:T(8,128)} %copy-done.4) | copy-start | bytes 3145732
  941.9 180.4 %copy-start.8 = (bf16[128,2048]{1,0:T(8,128)(2,1)S(1)}, bf16[128,2048]{1,0:T(8,128)(2,1)}, u32[]{:S(2)}) copy-start(bf16[128,2048]{1,0:T(8,128)(2,1)} %copy-done.6) | copy-start | bytes 1572868
  941.9 180.4 %copy-start.23 = (f32[128,2048]{1,0:T(8,128)S(1)}, f32[128,2048]{1,0:T(8,128)}, u32[]{:S(2)}) copy-start(f32[128,2048]{1,0:T(8,128)} %get-tuple-element.88) | copy-start | bytes 3145732
  1122.5 18.1 %collective-permute-start.1 = (bf16[128,2048]{1,0:T(8,128)(2,1)S(1)}, bf16[128,2048]{1,0:T(8,128)(2,1)S(1)}, u32[]{:S(2)}, u32[]{:S(2)}) collective-permute-start(bf16[128,2048]{1,0:T(8,128)(2,1)S(1)} %get-tuple-element.185), channel_id=1, source_target_pairs={{0,0},{1,8},{2,2},{3,10},{4,4},{5,12},{6,6},{7,14},{8,1},{9,9},{10... | collective-permute-start | bytes 1572872 | tf_op jit(solution)/shard_map/ppermute | solution.py:1164
  1123.3 17.3 %collective-permute-start.2 = (bf16[128,2048]{1,0:T(8,128)(2,1)S(1)}, bf16[128,2048]{1,0:T(8,128)(2,1)S(1)}, u32[]{:S(2)}, u32[]{:S(2)}) collective-permute-start(bf16[128,2048]{1,0:T(8,128)(2,1)S(1)} %get-tuple-element.186), channel_id=1, source_target_pairs={{0,16},{1,24},{2,18},{3,26},{4,20},{5,28},{6,22},{7,30},{8,17},{9,... | collective-permute-start | bytes 1572872 | tf_op jit(solution)/shard_map/ppermute | solution.py:1172
  1126.0 21.6 %collective-permute-start.5 = (bf16[128,2048]{1,0:T(8,128)(2,1)S(1)}, bf16[128,2048]{1,0:T(8,128)(2,1)S(1)}, u32[]{:S(2)}, u32[]{:S(2)}) collective-permute-start(bf16[128,2048]{1,0:T(8,128)(2,1)S(1)} %broadcast_select_fusion), channel_id=1, source_target_pairs={{0,16},{1,24},{2,18},{3,26},{4,20},{5,28},{6,22},{7,30},{8,17},{9,... | collective-permute-start | bytes 1572872 | tf_op jit(solution)/shard_map/ppermute | solution.py:1172
  1128.0 19.7 %collective-permute-start.4 = (bf16[128,2048]{1,0:T(8,128)(2,1)S(1)}, bf16[128,2048]{1,0:T(8,128)(2,1)S(1)}, u32[]{:S(2)}, u32[]{:S(2)}) collective-permute-start(bf16[128,2048]{1,0:T(8,128)(2,1)S(1)} %get-tuple-element.171), channel_id=1, source_target_pairs={{0,0},{1,8},{2,2},{3,10},{4,4},{5,12},{6,6},{7,14},{8,1},{9,9},{10... | collective-permute-start | bytes 1572872 | tf_op jit(solution)/shard_map/ppermute | solution.py:1164
  (53 other events, 1266.0 us)

commit v6 on v5

--- a/solution.py
+++ b/solution.py
@@ -189,6 +189,70 @@
     lax.fori_loop(0, w_query.shape[0] // size, back_tile, 0)
 
 
+class Rows:
+    def __init__(self, one, two, rows, near_send, near_recv, far_send, far_recv, local):
+        section, ctx, me = lax.axis_index("section"), lax.axis_index("ctx"), lax.axis_index("dp")
+        k = me % 2
+        self.early, self.stays = section == 0, k == ctx
+        self.one, self.two = one, two
+        place = {"ctx": k, "dp": me - k + ctx}
+        self.peers = (place, {**place, "section": 1 - section})
+
+        def near(source, at):
+            return pltpu.make_async_remote_copy(
+                source, rows.at[at], near_send, near_recv, device_id=place, device_id_type=MESH
+            )
+
+        def far(source, at):
+            return pltpu.make_async_remote_copy(
+                source, rows.at[at], far_send, far_recv,
+                device_id=self.peers[1], device_id_type=MESH,
+            )
+
+        self.near = lambda source: near(source, section)
+        self.far = lambda source: far(source, section)
+        self.far_in = far(two, 1 - section)
+        self.kept = lambda source: pltpu.make_async_copy(source, rows.at[section], local)
+        self.count = 1 + jnp.where(self.stays, 0, 1)
+
+    def greet(self, barrier):
+        pl.semaphore_signal(barrier, inc=1, device_id=self.peers[1], device_id_type=MESH)
+
+        @pl.when(jnp.logical_not(self.stays))
+        def _():
+            pl.semaphore_signal(barrier, inc=1, device_id=self.peers[0], device_id_type=MESH)
+
+    def start(self):
+        for cond, mine, other in (
+            (self.early, self.one, self.two),
+            (jnp.logical_not(self.early), self.two, self.one),
+        ):
+
+            @pl.when(cond)
+            def _():
+                self.far(other).start()
+
+            @pl.when(cond & self.stays)
+            def _():
+                self.kept(mine).start()
+
+            @pl.when(cond & jnp.logical_not(self.stays))
+            def _():
+                self.near(mine).start()
+
+    def wait(self):
+        self.far(self.two).wait_send()
+        self.far_in.wait_recv()
+
+        @pl.when(self.stays)
+        def _():
+            self.kept(self.one).wait()
+
+        @pl.when(jnp.logical_not(self.stays))
+        def _():
+            self.near(self.one).wait()
+
+
 def half_of(ref, which):
     half = ref.shape[-2] // 2
     at = pl.ds(pl.multiple_of(which * half, half), half)
@@ -199,7 +263,7 @@
     return shape[:-2] + (shape[-2] // 2, shape[-1])
 
 
-def pass_kernel(compute, n_weights, n_ins, n_outs, places, side_axes, *refs):
+def pass_kernel(compute, n_weights, n_ins, n_outs, places, side_axes, has_rows, *refs):
     refs = list(refs)
     take = lambda count: [refs.pop(0) for _ in range(count)]
     (x_ref,) = take(1)
@@ -207,9 +271,11 @@
     late_weights = take(n_weights)
     ins = take(n_ins)
     side_from = take(len(side_axes))
+    rows_from = take(2 * has_rows)
     (y_ref,) = take(1)
     given = take(1 + n_outs)
     side_to = take(len(side_axes))
+    rows_to = take(has_rows)
     kept = take(1 + n_outs)
     gath, outs = kept[0], kept[1:]
     weights = take(n_weights)
@@ -217,8 +283,8 @@
     (
         weight_sem, gather_right, gather_left, gather_partner, gather_line_in, gather_partner_in,
         partner_send, partner_recv, right_send, right_recv, left_send, left_recv,
-        side_send, side_recv, given_sem,
-    ) = take(15)
+        side_send, side_recv, given_sem, rows_sem,
+    ) = take(16)
 
     section = lax.axis_index("section")
     me = lax.axis_index("dp")
@@ -257,7 +323,11 @@
     far = {"ctx": 1 - lax.axis_index("ctx"), "section": 1 - section}
     for axis in sorted(set(side_axes)):
         pl.semaphore_signal(barrier, inc=1, device_id={axis: far[axis]}, device_id_type=MESH)
-    peers = 1 + len(set(side_axes)) + jnp.where(has_left, 1, 0) + jnp.where(has_right, 1, 0)
+    moved = [Rows(*rows_from, *rows_to, *[rows_sem.at[i] for i in range(5)])] if has_rows else []
+    for rows_back in moved:
+        rows_back.greet(barrier)
+    extra = sum([rows_back.count for rows_back in moved], len(set(side_axes)))
+    peers = 1 + extra + jnp.where(has_left, 1, 0) + jnp.where(has_right, 1, 0)
     pl.semaphore_wait(barrier, peers)
 
     sides = []
@@ -324,7 +394,7 @@
             to_left(z, index, x_ref.at[cut(index)]).start()
 
     to_partner(z, x_ref).start()
-    for copy in sides:
+    for copy in sides + moved:
         copy.start()
     gath[z, k] = x_ref[...]
 
@@ -468,11 +538,11 @@
         return carry
 
     lax.fori_loop(0, places, drain, 0)
-    for copy in sides:
+    for copy in sides + moved:
         copy.wait()
 
 
-def tensor_pass(compute, ident, x, early_weights, late_weights, ins, out_widths, sides=()):
+def tensor_pass(compute, ident, x, early_weights, late_weights, ins, out_widths, sides=(), back=()):
     rows, width = x.shape
     places = lax.axis_size("dp") // 2
     vmem = pl.BlockSpec(memory_space=pltpu.VMEM)
@@ -484,7 +554,7 @@
         half_shape(array.shape) if axis == "ctx" else array.shape for axis, array in sides
     ]
     kernel = functools.partial(
-        pass_kernel, compute, count, len(ins), len(out_widths), places, axes
+        pass_kernel, compute, count, len(ins), len(out_widths), places, axes, len(back) // 2
     )
     call = pl.pallas_call(
         kernel,
@@ -493,9 +563,10 @@
             jax.ShapeDtypeStruct((places, 2, rows, width), jnp.bfloat16),
         ]
         + [jax.ShapeDtypeStruct((places, 2 * rows, out), jnp.bfloat16) for out in out_widths]
-        + [jax.ShapeDtypeStruct(shape, jnp.bfloat16) for shape in moved],
-        in_specs=[vmem] + [hbm] * (2 * count) + [vmem] * len(ins) + [hbm] * len(axes),
-        out_specs=[vmem] + [hbm] * (1 + len(out_widths) + len(axes)),
+        + [jax.ShapeDtypeStruct(shape, jnp.bfloat16) for shape in moved]
+        + [jax.ShapeDtypeStruct((2, rows, width), jnp.bfloat16)] * (len(back) // 2),
+        in_specs=[vmem] + [hbm] * (2 * count) + [vmem] * len(ins) + [hbm] * len(axes) + [vmem] * len(back),
+        out_specs=[vmem] + [hbm] * (1 + len(out_widths) + len(axes) + len(back) // 2),
         scratch_shapes=[pltpu.VMEM((places, 2, rows, width), jnp.bfloat16)]
         + [pltpu.VMEM((places, 2 * rows, out), jnp.bfloat16) for out in out_widths]
         + [pltpu.VMEM(weight.shape, weight.dtype) for weight in early_weights]
@@ -522,6 +593,7 @@
             dma((max(len(axes), 1),)),
             dma((max(len(axes), 1),)),
             dma((1 + len(out_widths), places)),
+            dma((5,)),
         ],
         cost_estimate=pl.CostEstimate(
             flops=60_000_000_000, bytes_accessed=20_000_000, transcendentals=0
@@ -531,17 +603,17 @@
         ),
     )
     return call(
-        x, *early_weights, *late_weights, *ins, *[array for _, array in sides]
+        x, *early_weights, *late_weights, *ins, *[array for _, array in sides], *back
     )
 
 
 def distribute_kernel(
-    places, query, keyvalue, notes, out, up, down,
+    places, query, keyvalue, notes, out, up, down, tokens, cotangent,
     query_own, keyvalue_own, notes_own, up_own,
-    query_far, keyvalue_far, notes_far, out_far, up_far, down_far,
+    query_far, keyvalue_far, notes_far, out_far, up_far, down_far, tokens_out, cotangent_out,
     local_sem, query_send, query_recv, keyvalue_send, keyvalue_recv, notes_send, notes_recv,
     up_send, up_recv,
-    across_send, across_recv, over_send, over_recv,
+    across_send, across_recv, over_send, over_recv, rows_send, rows_recv,
 ):
     section = lax.axis_index("section")
     ctx = lax.axis_index("ctx")
@@ -618,7 +690,23 @@
     peers(greet)
     pl.semaphore_signal(barrier, inc=1, device_id=across, device_id_type=MESH)
     pl.semaphore_signal(barrier, inc=1, device_id=over, device_id_type=MESH)
-    pl.semaphore_wait(barrier, 2 * places + 1)
+    stays = k == ctx
+    place = {"ctx": k, "dp": 2 * z + ctx}
+    pairs = [(tokens.at[section, 0], tokens_out), (cotangent.at[section, 0], cotangent_out)]
+    rows_moves = [
+        remote(source, target, rows_send.at[i], rows_recv.at[i], place)
+        for i, (source, target) in enumerate(pairs)
+    ]
+    rows_kept = [
+        pltpu.make_async_copy(source, target, rows_send.at[2 + i])
+        for i, (source, target) in enumerate(pairs)
+    ]
+
+    @pl.when(jnp.logical_not(stays))
+    def _():
+        pl.semaphore_signal(barrier, inc=1, device_id=place, device_id_type=MESH)
+
+    pl.semaphore_wait(barrier, 2 * places + 1 + jnp.where(stays, 0, 1))
 
     local = [
         pltpu.make_async_copy(
@@ -731,6 +819,20 @@
     group(places - 2, over_block(3))
     group(places - 1, over_block(3))
 
+    @pl.when(stays)
+    def _():
+        for copy in rows_kept:
+            copy.start()
+        for copy in rows_kept:
+            copy.wait()
+
+    @pl.when(jnp.logical_not(stays))
+    def _():
+        for copy in rows_moves:
+            copy.start()
+        for copy in rows_moves:
+            copy.wait()
+
     peers(lambda source: up_copy(source, me, 1).wait_recv())
 
     def over_wait(slot_owner, carry):
@@ -762,9 +864,10 @@
     peers(sent)
 
 
-def distribute(query, keyvalue, notes, out, up, down):
+def distribute(query, keyvalue, notes, out, up, down, tokens, cotangent):
     size = lax.axis_size("dp")
     places = size // 2
+    vmem = pl.BlockSpec(memory_space=pltpu.VMEM)
     hbm = pl.BlockSpec(memory_space=pl.ANY)
     dma = pltpu.SemaphoreType.DMA
     rows = query.shape[0] * size
@@ -775,33 +878,35 @@
     ]
     turned = (rows, up.shape[1] // size)
     shapes = small + [turned] + small + [out.shape, turned, down.shape]
+    shapes += [tokens.shape[2:]] * 2
     slots = 1 + 5 * size
     return pl.pallas_call(
         functools.partial(distribute_kernel, places),
         name="distribute",
         out_shape=[jax.ShapeDtypeStruct(shape, jnp.bfloat16) for shape in shapes],
-        in_specs=[hbm] * 6,
+        in_specs=[vmem] * 3 + [hbm, vmem, hbm] + [vmem] * 2,
         out_specs=[hbm] * len(shapes),
         scratch_shapes=[dma((4,))]
         + [dma((size,))] * 6
         + [dma((size, 2))] * 2
-        + [dma((slots,))] * 4,
+        + [dma((slots,))] * 4
+        + [dma((4,)), dma((2,))],
         cost_estimate=pl.CostEstimate(
             flops=150_000_000_000, bytes_accessed=20_000_000, transcendentals=0
         ),
         compiler_params=pltpu.CompilerParams(collective_id=4, has_side_effects=True),
-    )(query, keyvalue, notes, out, up, down)
+    )(query, keyvalue, notes, out, up, down, tokens, cotangent)
 
 
 def collect_kernel(
     places, up_full, down_full, query_full, out_full, up_moved, down_moved,
-    up_late, down_late, query_late, out_late, up_far, down_far, query_far, out_far, small,
-    up_out, down_out, query_out, out_out, small_out,
+    up_late, down_late, query_late, out_late, up_far, down_far, query_far, out_far, small, grad_one, grad_two,
+    up_out, down_out, query_out, out_out, small_out, rows_out,
     small_in, small_sum, small_far, small_total, small_side,
     up, up_in, up_part, up_side, down, down_in, down_part, down_side,
     query, query_in, query_part, query_side, out, out_in, out_part, out_side,
     local_sem, side_send, side_recv, across_send, across_recv,
-    turn_send, turn_recv, over_send, over_recv, small_send, small_recv,
+    turn_send, turn_recv, over_send, over_recv, small_send, small_recv, rows_sem,
 ):
     section = lax.axis_index("section")
     ctx = lax.axis_index("ctx")
@@ -851,13 +956,15 @@
     peers(greet)
     pl.semaphore_signal(barrier, inc=1, device_id=across, device_id_type=MESH)
     pl.semaphore_signal(barrier, inc=1, device_id=over, device_id_type=MESH)
-    pl.semaphore_wait(barrier, size + 1)
+    rows_back = Rows(grad_one, grad_two, rows_out, *[rows_sem.at[i] for i in range(5)])
+    rows_back.greet(barrier)
+    pl.semaphore_wait(barrier, size + 1 + rows_back.count)
 
     side = [
         remote(half_of(query_full, 1 - ctx), query_side, side_send.at[0], side_recv.at[0], over),
         remote(half_of(out_full, 1 - ctx), out_side, side_send.at[1], side_recv.at[1], over),
     ]
-    for copy in side:
+    for copy in side + [rows_back]:
         copy.start()
 
     def small_turn(source, to, layer):
@@ -1086,6 +1193,7 @@
     small_over.wait_recv()
     small_out[...] = (small_total[...] + small_side[...]).astype(jnp.float32)
 
+    rows_back.wait()
     peers(small_sent)
     small_across.wait_send()
     small_over.wait_send()
@@ -1117,7 +1225,7 @@
         flat_over(index, 1 - ctx)[0].wait_recv()
 
 
-def collect(fulls, moved, late, far, small):
+def collect(fulls, moved, late, far, small, rows):
     size = lax.axis_size("dp")
     hbm = pl.BlockSpec(memory_space=pl.ANY)
     dma = pltpu.SemaphoreType.DMA
@@ -1133,9 +1241,10 @@
         functools.partial(collect_kernel, size // 2),
         name="collect",
         out_shape=[jax.ShapeDtypeStruct(shape, jnp.bfloat16) for shape in shapes]
-        + [jax.ShapeDtypeStruct(small.shape[2:], jnp.float32)],
-        in_specs=[hbm] * 15,
-        out_specs=[hbm] * 4 + [pl.BlockSpec(memory_space=pltpu.VMEM)],
+        + [jax.ShapeDtypeStruct(small.shape[2:], jnp.float32)]
+        + [jax.ShapeDtypeStruct((2,) + rows[0].shape, jnp.bfloat16)],
+        in_specs=[hbm] * 15 + [pl.BlockSpec(memory_space=pltpu.VMEM)] * 2,
+        out_specs=[hbm] * 4 + [pl.BlockSpec(memory_space=pltpu.VMEM), hbm],
         scratch_shapes=[vmem(small), vmem(small[:, 0])]
         + [vmem(small[0, 0])] * 3
         + [vmem(x) for x in late for _ in range(4)]
@@ -1143,33 +1252,13 @@
         + [dma((size + 7,))] * 2
         + [dma((2 * size,))] * 2
         + [dma((2 * size + 5,))] * 2
-        + [dma((2, size))] * 2,
+        + [dma((2, size))] * 2
+        + [dma((5,))],
         cost_estimate=pl.CostEstimate(
             flops=120_000_000_000, bytes_accessed=20_000_000, transcendentals=0
         ),
         compiler_params=pltpu.CompilerParams(collective_id=5, has_side_effects=True),
-    )(*fulls, *moved, *late, *far, small)
-
-
-def swapped(size):
-    pairs = []
-    for ctx in range(2):
-        for at in range(size):
-            z, k = at // 2, at % 2
-            pairs.append((ctx * size + at, k * size + 2 * z + ctx))
-    return pairs
-
-
-def regroup(x):
-    return lax.ppermute(x, ("ctx", "dp"), swapped(lax.axis_size("dp")))
-
-
-def regroup_across(x):
-    size = lax.axis_size("dp")
-    half = 2 * size
-    pairs = swapped(size)
-    across = [(a, b + half) for a, b in pairs] + [(a + half, b) for a, b in pairs]
-    return lax.ppermute(x, ("section", "ctx", "dp"), across)
+    )(*fulls, *moved, *late, *far, small, *rows)
 
 
 def own_half(grad):
@@ -1196,16 +1285,17 @@
     def own_micro(x):
         return lax.dynamic_index_in_dim(x, section, 0, keepdims=False)[0]
 
-    hidden = regroup(own_micro(tokens)).astype(jnp.float32)
     out, down = w_out[0], w_down[0]
     columns = ln_gains.shape[2]
     notes = jnp.concatenate(
         [ln_gains[0], ln_biases[0], own_micro(segment_ids).astype(jnp.bfloat16)[None]], axis=0
     )
     notes = jnp.pad(notes, ((0, 32 - notes.shape[0]), (0, 0)))
-    query, keyvalue, notes, up, query_far, keyvalue_far, notes_far, out_far, up_far, down_far = (
-        distribute(w_query[0], w_keyvalue[0], notes, out, w_up[0], down)
-    )
+    query, keyvalue, notes, up, query_far, keyvalue_far, notes_far, out_far, *rest = (
+        distribute(w_query[0], w_keyvalue[0], notes, out, w_up[0], down, tokens, cotangent)
+    )
+    up_far, down_far, hidden, grad_low = rest
+    hidden = hidden.astype(jnp.float32)
     notes = notes.reshape(size, 32, columns).transpose(1, 0, 2)
     near = notes[:4].reshape(4, width).astype(jnp.float32)
     far = notes_far.reshape(size, 32, columns).transpose(1, 0, 2)[:4].reshape(4, width)
@@ -1241,11 +1331,11 @@
     def rows_of_all(grad):
         return grad.reshape(size, grad.shape[0] // size, grad.shape[1])
 
-    def ffn_backward(layer, ident, grad_low, kept, sides):
+    def ffn_backward(layer, ident, grad_low, kept, sides, back=()):
         _, _, _, _, _, after, normed_two_all, up_rows, activated = kept
         y, grad_low_all, grad_upper, *arrived = tensor_pass(
             ffn_backward_at, ident, grad_low, *ffn_weights[layer],
-            [up_rows], [unit_width], sides,
+            [up_rows], [unit_width], sides, back,
         )
         grads = [
             rows_of_all(product(normed_two_all, grad_upper)),
@@ -1278,21 +1368,16 @@
     def ctx_sums(grads, arrived):
         return [own_half(grad) + other for grad, other in zip(grads, arrived)]
 
-    def both_rows(one, two):
-        near = regroup(jnp.where(early, one, two))
-        far = regroup_across(jnp.where(early, two, one))
-        return jnp.stack([jnp.where(early, near, far), jnp.where(early, far, near)])[None, :, None]
-
     hold = lax.optimization_barrier
     first, kept_first = forward(0, hidden)
     second, kept_second = forward(1, first.astype(jnp.float32))
-    section_rows = both_rows(first, second)
-    grad_low = regroup(own_micro(cotangent))
 
     def sides(axis, arrays):
         return [(axis, array) for array in arrays]
 
-    grad_after, ffn_two, scales_two, _ = ffn_backward(1, 2, grad_low, kept_second, [])
+    grad_after, ffn_two, scales_two, (section_rows,) = ffn_backward(
+        1, 2, grad_low, kept_second, [], [first, second]
+    )
     branch, up_two, down_two = hold((low(grad_after), *ffn_two))
     grad_second, attention_two, keyvalue_two, more, arrived = attention_backward(
         1, 3, grad_after, branch, kept_second, sides("ctx", [up_two])
@@ -1320,8 +1405,9 @@
         return jnp.concatenate([keyvalue_grad.reshape(size, columns, -1), rows], axis=1)
 
     small = jnp.stack([small_of(keyvalue_one, scales_one), small_of(keyvalue_two, scales_two)])
-    up_grad, down_grad, query_grad, out_grad, small = collect(
+    up_grad, down_grad, query_grad, out_grad, small, grad_rows = collect(
         ffn_one + attention_one, ffn_moved, [up_two] + rest_two, [up_two_far] + rest_far, small,
+        [grad_first, grad_second],
     )
     scale_grads = small[None, columns : columns + 4]
 
@@ -1329,8 +1415,8 @@
         return grad.astype(jnp.float32)[None]
 
     return (
-        section_rows,
-        both_rows(grad_first, grad_second),
+        section_rows[None, :, None],
+        grad_rows[None, :, None],
         given(query_grad),
         small[None, :columns],
         given(out_grad),

time: 1160 us -> 1150 us (level)
  Pallas kernels: 1000 us -> 1020 us
  starting transfers between devices: 14.3 us -> 0 us
    ppermute x6 -> x0, starting transfers between devices: 14.3 us -> none  [the longest x4 12.2 us: regroup(): return lax.ppermute(x, ('ctx', 'dp'), swapped(lax.axis_size('dp')))]
    pallas_call x8, Pallas kernels: 657 us -> 669 us  [tensor_pass(): call(x, *early_weights, *late_weights, *ins, *[array for _, array in side...]
  transfers between devices with their start and end apart: 6 -> 0, of which waited for: 1 -> 0; matrix products, arithmetic and copies ran while one was open for 3% -> 0% of each run, Pallas kernels for 41% -> 0%
where the time goes in v6:
time: 1150 us; the launch traced here: 1140 us
  Pallas kernels  1020 us (89%)
  other arithmetic  55.5 us (5%)
  matrix products  51.3 us (4%)
  local copies, waits for them, and re-layouts  12.3 us (1%)
    pallas_call x8, Pallas kernels, tensor_pass(): call(x, *early_weights, *late_weights, *ins, *[array for _, array in side...  669 us
    pallas_call x1, Pallas kernels, collect(): pl.pallas_call(functools.partial(collect_kernel, size // 2), name='collec...  185 us
    pallas_call x1, Pallas kernels, distribute(): pl.pallas_call(functools.partial(distribute_kernel, places), name='distri...  169 us
    dot_general x10, matrix products, dense_left(): lax.dot_general(left, right, (((0,), (0,)), ((), ())), preferred_element_...  51.3 us

profile of v6, /device:TPU:0, one launch (start us, length us, event | category | flops | bytes accessed | tf_op | source)
XLA Modules:
  0.0 1144.7 jit_solution(11250591898683500155)
XLA Ops:
  2.6 169.4 %distribute.1 = (bf16[2048,256]{1,0:T(8,128)(2,1)}, bf16[2048,256]{1,0:T(8,128)(2,1)}, bf16[256,256]{1,0:T(8,128)(2,1)}, bf16[2048,1024]{1,0:T(8,128)(2,1)}, bf1...) custom-call(bf16[256,2048]{1,0:T(8,128)(2,1)} %bitcast.154, ...), custom_call_target="tpu_custom_call" | custom-call | flops 149999992832 | bytes 20000000 | tf_op jit(solution)/shard_map/distribute/pallas_call | solution.py:883
  181.8 84.9 %shard_map.169 = (f32[128,2048]{1,0:T(8,128)}, bf16[4,2,128,2048]{3,2,1,0:T(8,128)(2,1)}, bf16[4,256,256]{2,1,0:T(8,128)(2,1)}, bf16[4,256,256]{2,1,0:T(8,128)(2,1)}, bf16[4,256,256]{2,1,0:T(8,128)(2,1)}) custom-call(bf16[128,2048]{1,0:T(8,128)(2,1)} %fusion.22.refs_0_, bf16[2048,256]{1,0:T(8,128)(2,1)} %get-tuple-element.86.refs_1_.refs_4_, ...), custom_call_target="tpu_custom_call" | custom-call | flops 60000002048 | bytes 20000000 | tf_op jit(solution)/shard_map/pallas_call | solution.py:605
  270.8 78.9 %shard_map.170 = (f32[128,2048]{1,0:T(8,128)}, bf16[4,2,128,2048]{3,2,1,0:T(8,128)(2,1)}, bf16[4,256,1024]{2,1,0:T(8,128)(2,1)}, bf16[4,256,1024]{2,1,0:T(8,128)(2,1)}) custom-call(bf16[128,2048]{1,0:T(8,128)(2,1)} %add_convert_fusion.5.refs_0_, bf16[2048,1024]{1,0:T(8,128)(2,1)} %get-tuple-element.82.refs_1_.refs_3_, bf16[1024,2048]{1,0:T(8,128)(2,1)} %bitcast.150, ...), custom_call_target="tpu_custom_call" | custom-call | flops 60000002048 | bytes 20000000 | tf_op jit(solution)/shard_map/pallas_call | solution.py:605
  353.1 73.7 %shard_map.171 = (f32[128,2048]{1,0:T(8,128)}, bf16[4,2,128,2048]{3,2,1,0:T(8,128)(2,1)}, bf16[4,256,256]{2,1,0:T(8,128)(2,1)}, bf16[4,256,256]{2,1,0:T(8,128)(2,1)}, bf16[4,256,256]{2,1,0:T(8,128)(2,1)}) custom-call(bf16[128,2048]{1,0:T(8,128)(2,1)} %fusion.19.refs_0_, bf16[2048,256]{1,0:T(8,128)(2,1)} %get-tuple-element.88.refs_4_.refs_1_, ...), custom_call_target="tpu_custom_call" | custom-call | flops 60000002048 | bytes 20000000 | tf_op jit(solution)/shard_map/pallas_call | solution.py:605
  429.5 77.2 %shard_map.172 = (f32[128,2048]{1,0:T(8,128)}, bf16[4,2,128,2048]{3,2,1,0:T(8,128)(2,1)}, bf16[4,256,1024]{2,1,0:T(8,128)(2,1)}, bf16[4,256,1024]{2,1,0:T(8,128)(2,1)}) custom-call(bf16[128,2048]{1,0:T(8,128)(2,1)} %add_convert_fusion.3.refs_0_, bf16[2048,1024]{1,0:T(8,128)(2,1)} %get-tuple-element.80.refs_3_.refs_1_, ...), custom_call_target="tpu_custom_call" | custom-call | flops 60000002048 | bytes 20000000 | tf_op jit(solution)/shard_map/pallas_call | solution.py:605
  508.9 98.9 %shard_map.173 = (f32[128,2048]{1,0:T(8,128)}, bf16[4,2,128,2048]{3,2,1,0:T(8,128)(2,1)}, bf16[4,256,1024]{2,1,0:T(8,128)(2,1)}, bf16[2,128,2048]{2,1,0:T(8,128)(2,1)}) custom-call(bf16[128,2048]{1,0:T(8,128)(2,1)} %get-tuple-element.79.refs_0_, bf16[2048,1024]{1,0:T(8,128)(2,1)} %get-tuple-element.80.refs_3_.refs_1_, ...), custom_call_target="tpu_custom_call" | custom-call | flops 60000002048 | bytes 20000000 | tf_op jit(solution)/shard_map/pallas_call | solution.py:605
  607.8 9.5 convolution_convert_fusion.3
  619.4 9.4 convolution_convert_fusion.2.refs_7_
  628.8 77.7 %shard_map.174 = (f32[128,2048]{1,0:T(8,128)}, bf16[4,2,128,2048]{3,2,1,0:T(8,128)(2,1)}, bf16[4,256,256]{2,1,0:T(8,128)(2,1)}, bf16[4,256,256]{2,1,0:T(8,128)(2,1)}, bf16[8,128,1024]{2,1,0:T(8,128)(2,1)}) custom-call(bf16[128,2048]{1,0:T(8,128)(2,1)} %fusion.28.refs_0_, bf16[2048,256]{1,0:T(8,128)(2,1)} %get-tuple-element.88.refs_4_.refs_1_, ...), custom_call_target="tpu_custom_call" | custom-call | flops 60000002048 | bytes 20000000 | tf_op jit(solution)/shard_map/pallas_call | solution.py:605
  706.5 4.7 dynamic-slice_add_fusion.1.refs_6_.up_late
  713.6 4.6 convolution_convert_fusion.8.refs_9_
  720.5 2.4 convolution_convert_fusion.4
  722.9 81.4 %shard_map.175 = (f32[128,2048]{1,0:T(8,128)}, bf16[4,2,128,2048]{3,2,1,0:T(8,128)(2,1)}, bf16[4,256,1024]{2,1,0:T(8,128)(2,1)}, bf16[8,128,1024]{2,1,0:T(8,128)...) custom-call(bf16[128,2048]{1,0:T(8,128)(2,1)} %add_convert_fusion.1.refs_0_.grad_two, ...), custom_call_target="tpu_custom_call" | custom-call | flops 60000002048 | bytes 20000000 | tf_op jit(solution)/shard_map/pallas_call | solution.py:605
  808.6 3.8 dynamic-slice_add_fusion.refs_13_.down_late
  812.4 6.2 convolution_convert_fusion.1
  818.7 6.2 convolution_convert_fusion.refs_12_.down_full
  828.1 96.5 %shard_map.176 = (f32[128,2048]{1,0:T(8,128)}, bf16[4,2,128,2048]{3,2,1,0:T(8,128)(2,1)}, bf16[4,256,256]{2,1,0:T(8,128)(2,1)}, bf16[4,256,256]{2,1,0:T(8,128)(2...) custom-call(bf16[128,2048]{1,0:T(8,128)(2,1)} %fusion.29.refs_0_, ...), custom_call_target="tpu_custom_call" | custom-call | flops 60000002048 | bytes 20000000 | tf_op jit(solution)/shard_map/pallas_call | solution.py:605
  924.7 4.5 convolution_convert_fusion.6.out_full
  931.6 4.7 convolution_convert_fusion.7
  939.3 185.3 %collect.1 = (bf16[256,8192]{1,0:T(8,128)(2,1)}, bf16[1024,2048]{1,0:T(8,128)(2,1)}, bf16[256,2048]{1,0:T(8,128)(2,1)}, bf16[256,2048]{1,0:T(8,128)(2,1)}, f32[2...) custom-call(bf16[8,256,1024]{2,1,0:T(8,128)(2,1)} %bitcast.167, ...), custom_call_target="tpu_custom_call" | custom-call | flops 120000004096 | bytes 20000000 | tf_op jit(solution)/shard_map/collect/pallas_call | solution.py:1240
  1127.9 2.8 bitcast_convert_fusion.3
  1130.7 2.8 bitcast_convert_fusion.2
  1133.5 4.4 bitcast_convert_fusion.1
  1137.9 4.4 bitcast_convert_fusion
  (195 shorter events, 48.7 us)
Async XLA Ops:
  176.5 90.2 %copy-start.27 = (f32[128]{0:T(128)}, f32[128]{0:T(128)S(1)}, u32[]{:S(2)}) copy-start(f32[128]{0:T(128)S(1)} %broadcast_multiply_fusion.3) | copy-start | bytes 1540
  177.8 88.9 %copy-start.41 = (f32[128]{0:T(128)}, f32[128]{0:T(128)S(1)}, u32[]{:S(2)}) copy-start(f32[128]{0:T(128)S(1)} %fusion.24) | copy-start | bytes 1540
  177.8 88.9 %copy-start.33 = (f32[128]{0:T(128)}, f32[128]{0:T(128)S(1)}, u32[]{:S(2)}) copy-start(f32[128]{0:T(128)S(1)} %fusion.37) | copy-start | bytes 1540
  178.4 173.0 %copy-start.21 = (f32[1,2,8,128]{3,1,2,0:T(2,128)}, f32[1,2,8,128]{3,1,2,0:T(2,128)S(1)}, u32[]{:S(2)}) copy-start(f32[1,2,8,128]{3,1,2,0:T(2,128)S(1)} %copy.43) | copy-start | bytes 24580
  178.5 90.6 %copy-start.23 = (f32[1,2,8,128]{3,1,2,0:T(2,128)}, f32[1,2,8,128]{3,1,2,0:T(2,128)S(1)}, u32[]{:S(2)}) copy-start(f32[1,2,8,128]{3,1,2,0:T(2,128)S(1)} %copy.41) | copy-start | bytes 24580
  181.7 85.0 %copy-start.2 = (bf16[128,2048]{1,0:T(8,128)(2,1)S(1)}, bf16[128,2048]{1,0:T(8,128)(2,1)}, u32[]{:S(2)}) copy-start(bf16[128,2048]{1,0:T(8,128)(2,1)} %get-tuple-element.83) | copy-start | bytes 1572868
  268.2 81.5 %copy-start = (f32[128,2048]{1,0:T(8,128)}, f32[128,2048]{1,0:T(8,128)S(1)}, u32[]{:S(2)}) copy-start(f32[128,2048]{1,0:T(8,128)S(1)} %get-tuple-element.188) | copy-start | bytes 3145732
  351.1 75.7 %copy-start.4 = (bf16[128,2048]{1,0:T(8,128)(2,1)}, bf16[128,2048]{1,0:T(8,128)(2,1)S(1)}, u32[]{:S(2)}) copy-start(bf16[128,2048]{1,0:T(8,128)(2,1)S(1)} %get-tuple-element.186.refs_6_) | copy-start | bytes 1572868
  351.1 75.7 %copy-start.29 = (f32[128]{0:T(128)}, f32[128]{0:T(128)S(1)}, u32[]{:S(2)}) copy-start(f32[128]{0:T(128)S(1)} %broadcast_multiply_fusion.1) | copy-start | bytes 1540
  351.9 74.9 %copy-start.35 = (f32[128]{0:T(128)}, f32[128]{0:T(128)S(1)}, u32[]{:S(2)}) copy-start(f32[128]{0:T(128)S(1)} %fusion.39) | copy-start | bytes 1540
  353.1 75.4 %copy-start.25 = (f32[1,2,8,128]{3,1,2,0:T(2,128)S(1)}, f32[1,2,8,128]{3,1,2,0:T(2,128)}, u32[]{:S(2)}) copy-start(f32[1,2,8,128]{3,1,2,0:T(2,128)} %copy.45) | copy-start | bytes 24580
  353.1 75.4 %copy-start.26 = (f32[1,2,8,128]{3,1,2,0:T(2,128)S(1)}, f32[1,2,8,128]{3,1,2,0:T(2,128)}, u32[]{:S(2)}) copy-start(f32[1,2,8,128]{3,1,2,0:T(2,128)} %copy.46) | copy-start | bytes 24580
  607.8 9.5 copy-start.12
  722.9 81.4 %copy-start.18 = (bf16[256,2048]{1,0:T(8,128)(2,1)S(1)}, bf16[256,2048]{1,0:T(8,128)(2,1)}, u32[]{:S(2)}) copy-start(bf16[256,2048]{1,0:T(8,128)(2,1)} %convolution_convert_fusion.8.refs_9_) | copy-start | bytes 3145732
  722.9 83.6 %copy-start.17 = (bf16[2048,256]{1,0:T(8,128)(2,1)S(1)}, bf16[2048,256]{1,0:T(8,128)(2,1)}, u32[]{:S(2)}) copy-start(bf16[2048,256]{1,0:T(8,128)(2,1)} %convolution_convert_fusion.9) | copy-start | bytes 3145732
  812.4 6.2 copy-start.49
  818.6 6.3 copy-start.1
  818.6 6.3 copy-start.11
  818.7 6.3 copy-start.24
  818.7 6.3 copy-start.32
  818.7 6.3 copy-start.38
  818.7 6.7 copy-start.40
  828.1 96.5 %copy-start.51 = (bf16[4,256,256]{2,1,0:T(8,128)(2,1)S(1)}, bf16[4,256,256]{2,1,0:T(8,128)(2,1)}, u32[]{:S(2)}) copy-start(bf16[4,256,256]{2,1,0:T(8,128)(2,1)} %get-tuple-element.132) | copy-start | bytes 1572868
  1124.6 8.9 copy-start.10
  (33 other events, 128.0 us)
